TPU v7x, 256 devices: a whole 4x4x8 slice. The times are simulated.
256 devices in a mesh: expert: 64 (over z, x, core), pair: 4 (over y).
Axes of the slice: x: 4, y: 4, z: 8, core: 2. Of those that a mesh axis runs over, the one named last changes fastest.
Arguments:
- tokens: bfloat16 [98304, 2048], P(('expert', 'pair')), may hold values from -6 to 6
- token_ids: int32 [98304], P(('expert', 'pair')), may hold values from 0 to 8191
- table: int32 [8192], replicated, may hold values from 0 to 127
- w_in: bfloat16 [128, 2048, 2048], P('expert', None, 'pair'), may hold values from -0.125 to 0.125
- w_out: bfloat16 [128, 2048, 2048], P('expert', 'pair'), may hold values from -0.125 to 0.125
Outputs:
- mixed: bfloat16 [98304, 2048], P(('expert', 'pair'))
All inputs are finite; a program needn't handle non-finite values.
Results may differ from a plain program's by a relative error of at most 0.0085.
Values may be sent and summed in bfloat16 or wider, within the bound.
No kernel may reach another device: no remote copies, remote signals or barrier semaphores. Data moves between devices by JAX's collectives and lax.ppermute only.
A program may use at most 192 MiB of HBM per device.

v0:
```python
import jax
import jax.numpy as jnp
from jax import lax
from jax.sharding import PartitionSpec as P


def on_device(tokens, token_ids, table, w_in, w_out):
    groups = lax.axis_size("expert")
    exp_local = w_in.shape[0]
    experts = groups * exp_local
    tok_rows, width = tokens.shape
    slots = max(2, 2 * tok_rows // experts)
    quarter = w_out.shape[1]
    chosen = jnp.take(table, token_ids, axis=0)
    expert_hot = (chosen[:, None] == jnp.arange(experts, dtype=jnp.int32)[None, :]).astype(
        jnp.int32
    )
    earlier = jnp.cumsum(expert_hot, axis=0) - expert_hot
    rank_tok = jnp.sum(earlier * expert_hot, axis=1)
    kept = rank_tok < slots
    column = (chosen // exp_local * slots + rank_tok) * exp_local + chosen % exp_local
    placer = (
        (column[:, None] == jnp.arange(experts * slots, dtype=jnp.int32)[None, :]) & kept[:, None]
    ).astype(jnp.bfloat16)
    packed = jnp.einsum("ts,td->sd", placer, tokens, preferred_element_type=jnp.float32).astype(
        jnp.bfloat16
    )
    packed = packed.reshape(groups * slots, exp_local, width)
    arrived = lax.all_to_all(packed, "expert", split_axis=0, concat_axis=0, tiled=True)
    rows = arrived.shape[0]
    hidden = jax.nn.relu(
        jnp.einsum(
            "red,edh->reh",
            arrived,
            lax.all_gather(w_in, "pair", axis=2, tiled=True),
            preferred_element_type=jnp.float32,
        )
    ).astype(jnp.bfloat16)
    total = jnp.zeros((rows, exp_local, width), jnp.float32)
    piece = lax.all_gather(w_out, "pair", axis=1, tiled=True)
    for index in range(piece.shape[1] // quarter):
        cols = lax.dynamic_slice_in_dim(hidden, index * quarter, quarter, 2)
        part = jnp.einsum(
            "reh,ehd->red",
            cols,
            piece[:, index * quarter : (index + 1) * quarter],
            preferred_element_type=jnp.float32,
        ).astype(jnp.bfloat16)
        total = total + lax.optimization_barrier(part).astype(jnp.float32)
    result = total.astype(jnp.bfloat16)
    returned = lax.all_to_all(result, "expert", split_axis=0, concat_axis=0, tiled=True)
    flat = returned.reshape(experts * slots, width)
    return jnp.dot(placer, flat, preferred_element_type=jnp.float32).astype(jnp.bfloat16)


def solution(mesh):
    in_specs = (
        P(("expert", "pair"), None),
        P(("expert", "pair")),
        P(),
        P("expert", None, "pair"),
        P("expert", "pair", None),
    )
    out_specs = P(("expert", "pair"), None)
    return jax.shard_map(
        on_device, mesh=mesh, in_specs=in_specs, out_specs=out_specs, check_vma=False
    )
```

profile of v0, /device:TPU:1, one launch (start us, length us, event | category | flops | bytes accessed | tf_op | source)
XLA Modules:
  0.0 449.1 jit_solution(8437720418810895938)
XLA Ops:
  6.5 0.0 copy-start
  6.5 0.0 copy-start.3
  6.5 0.0 all-gather.3.cloned.1.call-start
  6.5 0.7 all-gather.3.cloned.1.call-update
  7.3 0.0 copy-start.2
  7.3 0.0 all-gather.5.cloned.1.call-start
  7.3 0.7 all-gather.5.cloned.1.call-update
  8.0 0.0 copy-done.3
  8.1 0.0 copy-done.2
  8.1 2.5 gather_fusion
  10.6 0.1 copy.11
  10.7 0.2 fusion.47
  11.0 0.1 broadcast_add_fusion
  11.1 0.2 fusion.50
  11.3 0.0 copy-done
  11.3 3.6 convolution_convert_fusion
  14.9 4.6 %reshape.67 = bf16[384,2,2048]{2,1,0:T(2,128)(2,1)S(1)} reshape(bf16[768,2048]{1,0:T(8,128)(2,1)} %convolution_convert_fusion) | data formatting | bytes 6291456 | tf_op jit(solution)/shard_map/reshape | solution.py:28
  19.5 86.0 %all_to_all.10 = bf16[384,2,2048]{2,1,0:T(2,128)(2,1)} all-to-all(bf16[384,2,2048]{2,1,0:T(2,128)(2,1)S(1)} %reshape.67), channel_id=1, replica_groups=mesh['expert'=64,'pair'=4] {'expert'}, dimensions={0} | all-to-all | bytes 6291456 | tf_op jit(solution)/shard_map/all_to_all | solution.py:29
  105.5 63.8 %all-gather.3.cloned.1.call-done = bf16[2,2048,2048]{2,1,0:T(8,128)(2,1)} async-done(((bf16[2,2048,512]{2,1,0:T(8,128)(2,1)}), bf16[2,2048,2048]{2,1,0:T(8,128)(2,1)}) %all-gather.3.cloned.1.call-update) | async-done | bytes 16777232 | tf_op jit(solution)/shard_map/all_gather | solution.py:35
  169.4 14.0 %fusion.33 = bf16[384,2,2048]{2,0,1:T(8,128)(2,1)S(1)} fusion(bf16[2,2048,2048]{2,1,0:T(8,128)(2,1)} %all-gather.3.cloned.1.call-done, bf16[384,2,2048]{2,1,0:T(2,128)(2,1)} %all_to_all.10), kind=kOutput, calls=%fused_computation.21 | convolution fusion | flops 6445596672 | bytes 23068672 | tf_op jit(solution)/shard_map/red,edh->reh/dot_general | solution.py:32
  183.4 145.5 %all-gather.5.cloned.1.call-done = bf16[2,2048,2048]{2,1,0:T(8,128)(2,1)} async-done(((bf16[2,512,2048]{2,1,0:T(8,128)(2,1)}), bf16[2,2048,2048]{2,1,0:T(8,128)(2,1)}) %all-gather.5.cloned.1.call-update) | async-done | bytes 16777232 | tf_op jit(solution)/shard_map/all_gather | solution.py:40
  328.9 4.1 fusion.30
  333.1 4.7 %fusion.27 = bf16[384,2,2048]{2,0,1:T(8,128)(2,1)S(1)} fusion(bf16[2,2048,2048]{2,1,0:T(8,128)(2,1)} %all-gather.5.cloned.1.call-done, bf16[384,2,2048]{2,0,1:T(8,128)(2,1)S(1)} %fusion.33), kind=kOutput, calls=%fused_computation.19 | convolution fusion | flops 1612185600 | bytes 8126464 | tf_op jit(solution)/shard_map/reh,ehd->red/dot_general | solution.py:43
  337.8 0.0 copy-done.4
  337.8 1.8 fusion.24
  339.7 1.8 fusion.21
  341.5 3.2 add_convert_fusion
  344.7 3.5 copy.14
  348.2 83.8 %all_to_all.11 = bf16[384,2,2048]{2,1,0:T(2,128)(2,1)} all-to-all(bf16[384,2,2048]{2,1,0:T(2,128)(2,1)S(1)} %copy.14), channel_id=1, replica_groups=mesh['expert'=64,'pair'=4] {'expert'}, dimensions={0} | all-to-all | bytes 6291456 | tf_op jit(solution)/shard_map/all_to_all | solution.py:51
  432.0 5.8 %reshape.68 = bf16[768,2048]{1,0:T(8,128)(2,1)} reshape(bf16[384,2,2048]{2,1,0:T(2,128)(2,1)} %all_to_all.11) | data formatting | bytes 6291456 | tf_op jit(solution)/shard_map/reshape | solution.py:52
  437.8 4.5 convolution_convert_fusion.1
  442.3 0.0 copy-done.1
  (10 shorter events, 0.1 us)
Async XLA Ops:
  6.5 4.8 %copy-start = (bf16[384,2048]{1,0:T(8,128)(2,1)S(1)}, bf16[384,2048]{1,0:T(8,128)(2,1)}, u32[]{:S(2)}) copy-start(bf16[384,2048]{1,0:T(8,128)(2,1)} %param.5) | copy-start | bytes 4718596
  6.5 1.5 copy-start.3
  6.5 162.8 %all-gather.3.cloned.1.call-start = ((), (), s32[]{:S(2)}) async-start(), calls=%async_computation.2 | async-start | bytes 20971520 | tf_op jit(solution)/shard_map/all_gather | solution.py:35
  7.3 0.8 copy-start.2
  7.3 321.7 %all-gather.5.cloned.1.call-start = ((), (), s32[]{:S(2)}) async-start(), calls=%async_computation.3 | async-start | bytes 20971520 | tf_op jit(solution)/shard_map/all_gather | solution.py:40
  328.9 8.9 %copy-start.4 = (bf16[2,2048,2048]{2,1,0:T(8,128)(2,1)S(1)}, bf16[2,2048,2048]{2,1,0:T(8,128)(2,1)}, u32[]{:S(2)}) copy-start(bf16[2,2048,2048]{2,1,0:T(8,128)(2,1)} %all-gather.5.cloned.1.call-done) | copy-start | bytes 50331652
  432.0 10.3 %copy-start.1 = (bf16[384,2048]{1,0:T(8,128)(2,1)S(1)}, bf16[384,2048]{1,0:T(8,128)(2,1)}, u32[]{:S(2)}) copy-start(bf16[384,2048]{1,0:T(8,128)(2,1)} %param.5) | copy-start | bytes 4718596
Sparse Core Ops, SparseCore 0:
  9.1 160.1 all-gather.2
  171.2 157.6 all-gather.4
where the time goes:
time: 450 us; the launch traced here: 449 us
  waiting for transfers between devices  211 us (47%)
  blocking collectives  170 us (38%)
  matrix products  34.6 us (8%)
  local copies, waits for them, and re-layouts  16.5 us (4%)
  between operations  13.6 us (3%)
    all_gather x1, waiting for transfers between devices, on_device(): piece = lax.all_gather(w_out, 'pair', axis=1, tiled=True)  146 us
    all_to_all x1, blocking collectives, on_device(): lax.all_to_all(packed, 'expert', split_axis=0, concat_axis=0, tiled=True)  86 us
    all_to_all x1, blocking collectives, on_device(): lax.all_to_all(result, 'expert', split_axis=0, concat_axis=0, tiled=True)  83.8 us
    all_gather x1, waiting for transfers between devices, on_device(): lax.all_gather(w_in, 'pair', axis=2, tiled=True)  63.8 us
    dot_general x1, matrix products, on_device(): jnp.einsum('red,edh->reh', arrived, lax.all_gather(w_in, 'pair', axis=2,...  14 us
    dot_general x4, matrix products, on_device(): jnp.einsum('reh,ehd->red', cols, piece[:, index * quarter:(index + 1) * q...  12.5 us
  transfers between devices with their start and end apart: 2, of which 2 were waited for; matrix products, arithmetic and copies ran while one was open for 6% of the time, Pallas kernels for 0%

commit v1 on v0

v1 whole, which is shorter than its diff:
```python
import jax
import jax.numpy as jnp
from jax import lax
from jax.sharding import Mesh, PartitionSpec as P

BF = jnp.bfloat16
F32 = jnp.float32


def weight_route():
    rounds = []
    for p in range(4):
        pairs = []
        for c in range(2):
            for y in range(4):
                bits = y ^ p
                h, k = bits >> 1, bits & 1
                pairs.append((c * 4 + y, h * 4 + 2 * c + k))
        rounds.append(pairs)
    return rounds


def on_device(tokens, token_ids, table, w_in, w_out):
    experts = lax.axis_size("g") * lax.axis_size("y")
    tok_rows, width = tokens.shape
    slots = 2 * tok_rows // experts
    quarter = w_out.shape[1]
    half = quarter // 2
    y = lax.axis_index("y")
    own_in, own_out = [], []
    blocks = []
    for p in range(4):
        bits = y ^ p
        h, k = bits >> 1, bits & 1
        blocks.append((
            lax.dynamic_slice(w_in, (k, 0, h * half), (1, width, half))[0],
            lax.dynamic_slice(w_out, (k, h * half, 0), (1, half, width))[0],
        ))
    route = weight_route()
    for p in range(4):
        own_in.append(lax.ppermute(blocks[p][0], ("c", "y"), route[p]))
    for p in range(4):
        own_out.append(lax.ppermute(blocks[p][1], ("c", "y"), route[p]))
    swap = [(0, 1), (1, 0)]
    other_in = [lax.ppermute(b, "c", swap) for b in own_in]
    other_out = [lax.ppermute(b, "c", swap) for b in own_out]
    full_in = jnp.concatenate(own_in + other_in, axis=1)
    full_out = jnp.concatenate(own_out + other_out, axis=0)

    chosen = jnp.take(table, token_ids, axis=0)
    expert_hot = (chosen[:, None] == jnp.arange(experts, dtype=jnp.int32)[None, :]).astype(jnp.int32)
    earlier = jnp.cumsum(expert_hot, axis=0) - expert_hot
    rank_tok = jnp.sum(earlier * expert_hot, axis=1)
    kept = rank_tok < slots
    column = chosen * slots + rank_tok
    placer = (
        (column[:, None] == jnp.arange(experts * slots, dtype=jnp.int32)[None, :]) & kept[:, None]
    ).astype(BF)
    packed = jnp.einsum("ts,td->sd", placer, tokens, preferred_element_type=F32).astype(BF)
    packed = packed.reshape(experts * slots // 2, 2, width)
    arrived = lax.all_to_all(packed, ("g", "y"), split_axis=0, concat_axis=0, tiled=True)
    arrived = arrived.reshape(experts * slots, width)
    hidden = jax.nn.relu(jnp.dot(arrived, full_in, preferred_element_type=F32)).astype(BF)
    result = jnp.dot(hidden, full_out, preferred_element_type=F32).astype(BF)
    result = result.reshape(experts * slots // 2, 2, width)
    returned = lax.all_to_all(result, ("g", "y"), split_axis=0, concat_axis=0, tiled=True)
    flat = returned.reshape(experts * slots, width)
    return jnp.dot(placer, flat, preferred_element_type=F32).astype(BF)


def solution(mesh):
    groups, pair = mesh.shape["expert"], mesh.shape["pair"]
    fine = Mesh(mesh.devices.reshape(groups // 2, 2, pair), ("g", "c", "y"))
    rows = ("g", "c", "y")
    in_specs = (
        P(rows, None),
        P(rows),
        P(),
        P(("g", "c"), None, "y"),
        P(("g", "c"), "y", None),
    )
    return jax.shard_map(
        on_device, mesh=fine, in_specs=in_specs, out_specs=P(rows, None), check_vma=False
    )
```

time: 450 us -> 290 us (0.64)
  waiting for transfers between devices: 211 us -> 98.5 us
  blocking collectives: 170 us -> 82.7 us
  starting transfers between devices: 0.04 us -> 41.2 us
  local copies, waits for them, and re-layouts: 16.5 us -> 36 us
  between operations: 13.6 us -> 0.28 us
  matrix products: 34.6 us -> 27.2 us
    all_gather x2 -> x0, waiting for transfers between devices: 209 us -> none  [the longest x1 146 us: on_device(): piece = lax.all_gather(w_out, 'pair', axis=1, tiled=True)]
    ppermute x0 -> x16, waiting for transfers between devices: none -> 98.5 us  [the longest x4 51.4 us: on_device(): own_in.append(lax.ppermute(blocks[p][0], ('c', 'y'), route[p]))]
    all_to_all x2 -> x1, blocking collectives: 170 us -> 82.7 us  [on_device(): lax.all_to_all(result, ('g', 'y'), split_axis=0, concat_axis=0, tiled=True)]
    ppermute x0 -> x16, starting transfers between devices: none -> 24.8 us  [the longest x4 8.32 us: on_device(): own_in.append(lax.ppermute(blocks[p][0], ('c', 'y'), route[p]))]
    all_to_all x0 -> x1, starting transfers between devices: none -> 16.3 us  [on_device(): lax.all_to_all(packed, ('g', 'y'), split_axis=0, concat_axis=0, tiled=True)]
    unnamed x10 -> x22, local copies, waits for them, and re-layouts: 0.02 us -> 9.27 us
    reshape x1 -> x3, local copies, waits for them, and re-layouts: 4.59 us -> 13 us  [the longest x1 6.02 us: on_device(): packed = packed.reshape(experts * slots // 2, 2, width)]
    dot_general x7 -> x4, matrix products: 34.6 us -> 27.2 us  [the longest x1 10 us: on_device(): jnp.dot(arrived, full_in, preferred_element_type=F32)]
  transfers between devices with their start and end apart: 2 -> 17, of which waited for: 2 -> 7; matrix products, arithmetic and copies ran while one was open for 6% -> 5% of each run, Pallas kernels for 0% -> 0%
where the time goes in v1:
time: 290 us; the launch traced here: 288 us
  waiting for transfers between devices  98.5 us (34%)
  blocking collectives  82.7 us (29%)
  starting transfers between devices  41.2 us (14%)
  local copies, waits for them, and re-layouts  36 us (12%)
  matrix products  27.2 us (9%)
    all_to_all x1, blocking collectives, on_device(): lax.all_to_all(result, ('g', 'y'), split_axis=0, concat_axis=0, tiled=True)  82.7 us
    ppermute x4, waiting for transfers between devices, on_device(): own_in.append(lax.ppermute(blocks[p][0], ('c', 'y'), route[p]))  51.4 us
    ppermute x4, waiting for transfers between devices, on_device(): own_out.append(lax.ppermute(blocks[p][1], ('c', 'y'), route[p]))  46.8 us
    all_to_all x1, starting transfers between devices, on_device(): lax.all_to_all(packed, ('g', 'y'), split_axis=0, concat_axis=0, tiled=True)  16.3 us
    dot_general x1, matrix products, on_device(): jnp.dot(arrived, full_in, preferred_element_type=F32)  10 us
    unnamed x22, local copies, waits for them, and re-layouts  9.27 us
    dot_general x1, matrix products, on_device(): result = jnp.dot(hidden, full_out, preferred_element_type=F32).astype(BF)  9.12 us
    ppermute x4, starting transfers between devices, on_device(): own_in.append(lax.ppermute(blocks[p][0], ('c', 'y'), route[p]))  8.32 us
  transfers between devices with their start and end apart: 17, of which 7 were waited for; matrix products, arithmetic and copies ran while one was open for 5% of the time, Pallas kernels for 0%

profile of v1, /device:TPU:1, one launch (start us, length us, event | category | flops | bytes accessed | tf_op | source)
XLA Modules:
  0.0 287.9 jit_solution(4290998969786285967)
XLA Ops:
  0.8 3.4 %gather_fusion = s32[384]{0:T(512)S(1)} fusion(s32[8192]{0:T(1024)} %param.7, s32[1024]{0:T(1024)S(1)} %pad_clamp_fusion), kind=kCustom, calls=%fused_computation | custom fusion | bytes 4608 | tf_op jit(solution)/shard_map/jit(_take)/gather | solution.py:50
  5.7 3.6 %convolution_convert_fusion.1 = bf16[768,2048]{1,0:T(8,128)(2,1)} fusion(bf16[384,2048]{1,0:T(8,128)(2,1)S(1)} %copy-done, s32[384]{0:T(512)S(1)} %multiply_add_fusion, pred[384]{0:T(512)(128)(4,1)S(1)} %broadcast_compare_fusion), kind=kOutput, calls=%fused_computation.3 | convolution fusion | flops 1210122240 | bytes 4720512 | tf_op jit(solution)/shard_map/ts,td->sd/dot_general | solution.py:59
  9.2 6.0 %reshape.45 = bf16[384,2,2048]{2,1,0:T(2,128)(2,1)} reshape(bf16[768,2048]{1,0:T(8,128)(2,1)} %convolution_convert_fusion.1) | data formatting | bytes 6291456 | tf_op jit(solution)/shard_map/reshape | solution.py:60
  15.3 16.3 %all-to-all-start = ((bf16[384,2,2048]{2,1,0:T(2,128)(2,1)}), bf16[384,2,2048]{2,1,0:T(2,128)(2,1)S(1)}, u32[]{:S(2)}, u32[]{:S(2)}) async-start(bf16[384,2,2048]{2,1,0:T(2,128)(2,1)} %reshape.45), calls=%async_computation | async-start | bytes 6291456 | tf_op jit(solution)/shard_map/all_to_all | solution.py:61
  31.6 2.6 dynamic-slice_bitcast_fusion.4
  34.2 5.1 %collective-permute-start = (bf16[2048,256]{1,0:T(8,128)(2,1)S(1)}, bf16[2048,256]{1,0:T(8,128)(2,1)S(1)}, u32[]{:S(2)}, u32[]{:S(2)}) collective-permute-start(bf16[2048,256]{1,0:T(8,128)(2,1)S(1)} %get-tuple-element.11), channel_id=1, source_target_pairs={{0,0},{1,1},{2,4},{3,5},{4,2},{5,3},{6,6},{7,7},{8,8},{9,9},{10,12... | collective-permute-start | bytes 3145736 | tf_op jit(solution)/shard_map/ppermute | solution.py:41
  40.0 2.0 collective-permute-start.8
  41.9 3.0 %collective-permute-start.1 = (bf16[2048,256]{1,0:T(8,128)(2,1)S(1)}, bf16[2048,256]{1,0:T(8,128)(2,1)S(1)}, u32[]{:S(2)}, u32[]{:S(2)}) collective-permute-start(bf16[2048,256]{1,0:T(8,128)(2,1)S(1)} %get-tuple-element.10), channel_id=1, source_target_pairs={{0,1},{1,0},{2,5},{3,4},{4,3},{5,2},{6,7},{7,6},{8,9},{9,8},{10,13... | collective-permute-start | bytes 3145736 | tf_op jit(solution)/shard_map/ppermute | solution.py:41
  45.1 35.6 %collective-permute-done = bf16[2048,256]{1,0:T(8,128)(2,1)S(1)} collective-permute-done((bf16[2048,256]{1,0:T(8,128)(2,1)S(1)}, bf16[2048,256]{1,0:T(8,128)(2,1)S(1)}, u32[]{:S(2)}, u32[]{:S(2)}) %collective-permute-start) | collective-permute-done | bytes 1048608 | tf_op jit(solution)/shard_map/ppermute | solution.py:41
  80.8 3.7 %collective-permute-start.9 = (bf16[256,2048]{1,0:T(8,128)(2,1)S(1)}, bf16[256,2048]{1,0:T(8,128)(2,1)S(1)}, u32[]{:S(2)}, u32[]{:S(2)}) collective-permute-start(bf16[256,2048]{1,0:T(8,128)(2,1)S(1)} %get-tuple-element.6), channel_id=1, source_target_pairs={{0,1},{1,0},{2,5},{3,4},{4,3},{5,2},{6,7},{7,6},{8,9},{9,8},{10,13... | collective-permute-start | bytes 3145736 | tf_op jit(solution)/shard_map/ppermute | solution.py:43
  84.6 29.2 %collective-permute-done.8 = bf16[256,2048]{1,0:T(8,128)(2,1)S(1)} collective-permute-done((bf16[256,2048]{1,0:T(8,128)(2,1)S(1)}, bf16[256,2048]{1,0:T(8,128)(2,1)S(1)}, u32[]{:S(2)}, u32[]{:S(2)}) %collective-permute-start.8) | collective-permute-done | bytes 1048608 | tf_op jit(solution)/shard_map/ppermute | solution.py:43
  113.8 1.1 constant_dynamic-update-slice_fusion.15
  114.9 2.7 collective-permute-start.11
  117.7 15.8 %collective-permute-done.2 = bf16[2048,256]{1,0:T(8,128)(2,1)S(1)} collective-permute-done((bf16[2048,256]{1,0:T(8,128)(2,1)S(1)}, bf16[2048,256]{1,0:T(8,128)(2,1)S(1)}, u32[]{:S(2)}, u32[]{:S(2)}) %collective-permute-start.2) | collective-permute-done | bytes 1048608 | tf_op jit(solution)/shard_map/ppermute | solution.py:41
  133.5 3.5 %collective-permute-start.4 = (bf16[2048,256]{1,0:T(8,128)(2,1)S(1)}, bf16[2048,256]{1,0:T(8,128)(2,1)S(1)}, u32[]{:S(2)}, u32[]{:S(2)}) collective-permute-start(bf16[2048,256]{1,0:T(8,128)(2,1)S(1)} %collective-permute-done), channel_id=1, source_target_pairs={{0,4},{4,0},{1,5},{5,1},{2,6},{6,2},{3,7},{7,3},{8,12},{12,8},{9,1... | collective-permute-start | bytes 3145736 | tf_op jit(solution)/shard_map/ppermute | solution.py:45
  137.4 1.6 collective-permute-done.9
  139.0 1.0 constant_dynamic-update-slice_fusion.14
  140.0 15.9 %collective-permute-done.10 = bf16[256,2048]{1,0:T(8,128)(2,1)S(1)} collective-permute-done((bf16[256,2048]{1,0:T(8,128)(2,1)S(1)}, bf16[256,2048]{1,0:T(8,128)(2,1)S(1)}, u32[]{:S(2)}, u32[]{:S(2)}) %collective-permute-start.10) | collective-permute-done | bytes 1048608 | tf_op jit(solution)/shard_map/ppermute | solution.py:43
  156.0 3.5 %collective-permute-start.7 = (bf16[2048,256]{1,0:T(8,128)(2,1)S(1)}, bf16[2048,256]{1,0:T(8,128)(2,1)S(1)}, u32[]{:S(2)}, u32[]{:S(2)}) collective-permute-start(bf16[2048,256]{1,0:T(8,128)(2,1)S(1)} %collective-permute-done.3), channel_id=1, source_target_pairs={{0,4},{4,0},{1,5},{5,1},{2,6},{6,2},{3,7},{7,3},{8,12},{12,8},{9,1... | collective-permute-start | bytes 3145736 | tf_op jit(solution)/shard_map/ppermute | solution.py:45
  159.4 1.0 constant_dynamic-update-slice_fusion.13
  160.6 1.1 constant_dynamic-update-slice_fusion.12
  163.4 1.2 constant_dynamic-update-slice_fusion.11
  164.7 1.6 constant_dynamic-update-slice_fusion.10
  166.3 1.2 constant_dynamic-update-slice_fusion.9
  167.7 1.0 constant_dynamic-update-slice_fusion.8
  168.8 3.2 %reshape.46 = bf16[768,2048]{1,0:T(8,128)(2,1)} reshape(bf16[384,2,2048]{2,1,0:T(2,128)(2,1)S(1)} %all-to-all-done) | data formatting | bytes 6291456 | tf_op jit(solution)/shard_map/reshape | solution.py:62
  172.0 10.0 %maximum_convert_fusion = bf16[768,2048]{1,0:T(8,128)(2,1)S(1)} fusion(bf16[768,2048]{1,0:T(8,128)(2,1)} %reshape.46, bf16[2048,2048]{1,0:T(8,128)(2,1)} %copy-done.3), kind=kOutput, calls=%fused_computation.1 | convolution fusion | flops 6445596672 | bytes 14680064 | tf_op jit(solution)/shard_map/dot_general | solution.py:63
  182.0 9.1 %convolution_convert_fusion = bf16[768,2048]{1,0:T(8,128)(2,1)S(1)} fusion(bf16[768,2048]{1,0:T(8,128)(2,1)S(1)} %maximum_convert_fusion, bf16[2048,2048]{1,0:T(8,128)(2,1)} %constant_dynamic-update-slice_fusion.8), kind=kOutput, calls=%fused_computation.2 | convolution fusion | flops 6444023808 | bytes 14680064 | tf_op jit(solution)/shard_map/dot_general | solution.py:64
  191.2 3.8 %reshape.47 = bf16[384,2,2048]{2,1,0:T(2,128)(2,1)} reshape(bf16[768,2048]{1,0:T(8,128)(2,1)S(1)} %convolution_convert_fusion) | data formatting | bytes 6291456 | tf_op jit(solution)/shard_map/reshape | solution.py:65
  195.0 82.7 %all_to_all.10 = bf16[384,2,2048]{2,1,0:T(2,128)(2,1)} all-to-all(bf16[384,2,2048]{2,1,0:T(2,128)(2,1)} %reshape.47), channel_id=1, replica_groups=mesh['g'=32,'c'=2,'y'=4] {'g','y'}, dimensions={0} | all-to-all | bytes 6291456 | tf_op jit(solution)/shard_map/all_to_all | solution.py:66
  277.7 5.7 %reshape.48 = bf16[768,2048]{1,0:T(8,128)(2,1)} reshape(bf16[384,2,2048]{2,1,0:T(2,128)(2,1)} %all_to_all.10) | data formatting | bytes 6291456 | tf_op jit(solution)/shard_map/reshape | solution.py:67
  283.4 4.5 %convolution_convert_fusion.2 = bf16[384,2048]{1,0:T(8,128)(2,1)} fusion(bf16[768,2048]{1,0:T(8,128)(2,1)} %reshape.48, s32[384]{0:T(512)S(1)} %multiply_add_fusion, pred[384]{0:T(512)(128)(4,1)S(1)} %broadcast_compare_fusion), kind=kOutput, calls=%fused_computation.4 | convolution fusion | flops 1209335808 | bytes 4720512 | tf_op jit(solution)/shard_map/dot_general | solution.py:68
  (50 shorter events, 5.7 us)
Async XLA Ops:
  0.0 5.6 %copy-start = (bf16[384,2048]{1,0:T(8,128)(2,1)S(1)}, bf16[384,2048]{1,0:T(8,128)(2,1)}, u32[]{:S(2)}) copy-start(bf16[384,2048]{1,0:T(8,128)(2,1)} %param.5) | copy-start | bytes 4718596
  15.3 153.5 %all-to-all-start = ((bf16[384,2,2048]{2,1,0:T(2,128)(2,1)}), bf16[384,2,2048]{2,1,0:T(2,128)(2,1)S(1)}, u32[]{:S(2)}, u32[]{:S(2)}) async-start(bf16[384,2,2048]{2,1,0:T(2,128)(2,1)} %reshape.45), calls=%async_computation | async-start | bytes 6291456 | tf_op jit(solution)/shard_map/all_to_all | solution.py:61
  31.6 7.7 %copy-start.2 = (bf16[2,512,2048]{2,1,0:T(8,128)(2,1)S(1)}, bf16[2,512,2048]{2,1,0:T(8,128)(2,1)}, u32[]{:S(2)}) copy-start(bf16[2,512,2048]{2,1,0:T(8,128)(2,1)} %param.9) | copy-start | bytes 12582916
  34.2 46.5 %collective-permute-start = (bf16[2048,256]{1,0:T(8,128)(2,1)S(1)}, bf16[2048,256]{1,0:T(8,128)(2,1)S(1)}, u32[]{:S(2)}, u32[]{:S(2)}) collective-permute-start(bf16[2048,256]{1,0:T(8,128)(2,1)S(1)} %get-tuple-element.11), channel_id=1, source_target_pairs={{0,0},{1,1},{2,4},{3,5},{4,2},{5,3},{6,6},{7,7},{8,8},{9,9},{10,12... | collective-permute-start | bytes 3145736 | tf_op jit(solution)/shard_map/ppermute | solution.py:41
  40.0 73.8 %collective-permute-start.8 = (bf16[256,2048]{1,0:T(8,128)(2,1)S(1)}, bf16[256,2048]{1,0:T(8,128)(2,1)S(1)}, u32[]{:S(2)}, u32[]{:S(2)}) collective-permute-start(bf16[256,2048]{1,0:T(8,128)(2,1)S(1)} %get-tuple-element.7), channel_id=1, source_target_pairs={{0,0},{1,1},{2,4},{3,5},{4,2},{5,3},{6,6},{7,7},{8,8},{9,9},{10,12... | collective-permute-start | bytes 3145736 | tf_op jit(solution)/shard_map/ppermute | solution.py:43
  41.9 73.0 %collective-permute-start.1 = (bf16[2048,256]{1,0:T(8,128)(2,1)S(1)}, bf16[2048,256]{1,0:T(8,128)(2,1)S(1)}, u32[]{:S(2)}, u32[]{:S(2)}) collective-permute-start(bf16[2048,256]{1,0:T(8,128)(2,1)S(1)} %get-tuple-element.10), channel_id=1, source_target_pairs={{0,1},{1,0},{2,5},{3,4},{4,3},{5,2},{6,7},{7,6},{8,9},{9,8},{10,13... | collective-permute-start | bytes 3145736 | tf_op jit(solution)/shard_map/ppermute | solution.py:41
  44.9 88.6 %collective-permute-start.2 = (bf16[2048,256]{1,0:T(8,128)(2,1)S(1)}, bf16[2048,256]{1,0:T(8,128)(2,1)S(1)}, u32[]{:S(2)}, u32[]{:S(2)}) collective-permute-start(bf16[2048,256]{1,0:T(8,128)(2,1)S(1)} %get-tuple-element.12), channel_id=1, source_target_pairs={{0,4},{1,5},{2,0},{3,1},{4,6},{5,7},{6,2},{7,3},{8,12},{9,13},{10,... | collective-permute-start | bytes 3145736 | tf_op jit(solution)/shard_map/ppermute | solution.py:41
  44.9 92.2 %collective-permute-start.3 = (bf16[2048,256]{1,0:T(8,128)(2,1)S(1)}, bf16[2048,256]{1,0:T(8,128)(2,1)S(1)}, u32[]{:S(2)}, u32[]{:S(2)}) collective-permute-start(bf16[2048,256]{1,0:T(8,128)(2,1)S(1)} %get-tuple-element.9), channel_id=1, source_target_pairs={{0,5},{1,4},{2,1},{3,0},{4,7},{5,6},{6,3},{7,2},{8,13},{9,12},{10,... | collective-permute-start | bytes 3145736 | tf_op jit(solution)/shard_map/ppermute | solution.py:41
  80.8 58.2 %collective-permute-start.9 = (bf16[256,2048]{1,0:T(8,128)(2,1)S(1)}, bf16[256,2048]{1,0:T(8,128)(2,1)S(1)}, u32[]{:S(2)}, u32[]{:S(2)}) collective-permute-start(bf16[256,2048]{1,0:T(8,128)(2,1)S(1)} %get-tuple-element.6), channel_id=1, source_target_pairs={{0,1},{1,0},{2,5},{3,4},{4,3},{5,2},{6,7},{7,6},{8,9},{9,8},{10,13... | collective-permute-start | bytes 3145736 | tf_op jit(solution)/shard_map/ppermute | solution.py:43
  113.8 42.2 %collective-permute-start.10 = (bf16[256,2048]{1,0:T(8,128)(2,1)S(1)}, bf16[256,2048]{1,0:T(8,128)(2,1)S(1)}, u32[]{:S(2)}, u32[]{:S(2)}) collective-permute-start(bf16[256,2048]{1,0:T(8,128)(2,1)S(1)} %get-tuple-element.8), channel_id=1, source_target_pairs={{0,4},{1,5},{2,0},{3,1},{4,6},{5,7},{6,2},{7,3},{8,12},{9,13},{10,... | collective-permute-start | bytes 3145736 | tf_op jit(solution)/shard_map/ppermute | solution.py:43
  114.9 45.5 %collective-permute-start.11 = (bf16[256,2048]{1,0:T(8,128)(2,1)S(1)}, bf16[256,2048]{1,0:T(8,128)(2,1)S(1)}, u32[]{:S(2)}, u32[]{:S(2)}) collective-permute-start(bf16[256,2048]{1,0:T(8,128)(2,1)S(1)} %get-tuple-element.5), channel_id=1, source_target_pairs={{0,5},{1,4},{2,1},{3,0},{4,7},{5,6},{6,3},{7,2},{8,13},{9,12},{10,... | collective-permute-start | bytes 3145736 | tf_op jit(solution)/shard_map/ppermute | solution.py:43
  133.5 28.2 %collective-permute-start.4 = (bf16[2048,256]{1,0:T(8,128)(2,1)S(1)}, bf16[2048,256]{1,0:T(8,128)(2,1)S(1)}, u32[]{:S(2)}, u32[]{:S(2)}) collective-permute-start(bf16[2048,256]{1,0:T(8,128)(2,1)S(1)} %collective-permute-done), channel_id=1, source_target_pairs={{0,4},{4,0},{1,5},{5,1},{2,6},{6,2},{3,7},{7,3},{8,12},{12,8},{9,1... | collective-permute-start | bytes 3145736 | tf_op jit(solution)/shard_map/ppermute | solution.py:45
  137.1 25.1 %collective-permute-start.5 = (bf16[2048,256]{1,0:T(8,128)(2,1)S(1)}, bf16[2048,256]{1,0:T(8,128)(2,1)S(1)}, u32[]{:S(2)}, u32[]{:S(2)}) collective-permute-start(bf16[2048,256]{1,0:T(8,128)(2,1)S(1)} %collective-permute-done.1), channel_id=1, source_target_pairs={{0,4},{4,0},{1,5},{5,1},{2,6},{6,2},{3,7},{7,3},{8,12},{12,8},{9,1... | collective-permute-start | bytes 3145736 | tf_op jit(solution)/shard_map/ppermute | solution.py:45
  139.0 23.6 %collective-permute-start.6 = (bf16[2048,256]{1,0:T(8,128)(2,1)S(1)}, bf16[2048,256]{1,0:T(8,128)(2,1)S(1)}, u32[]{:S(2)}, u32[]{:S(2)}) collective-permute-start(bf16[2048,256]{1,0:T(8,128)(2,1)S(1)} %collective-permute-done.2), channel_id=1, source_target_pairs={{0,4},{4,0},{1,5},{5,1},{2,6},{6,2},{3,7},{7,3},{8,12},{12,8},{9,1... | collective-permute-start | bytes 3145736 | tf_op jit(solution)/shard_map/ppermute | solution.py:45
  156.0 7.2 %collective-permute-start.7 = (bf16[2048,256]{1,0:T(8,128)(2,1)S(1)}, bf16[2048,256]{1,0:T(8,128)(2,1)S(1)}, u32[]{:S(2)}, u32[]{:S(2)}) collective-permute-start(bf16[2048,256]{1,0:T(8,128)(2,1)S(1)} %collective-permute-done.3), channel_id=1, source_target_pairs={{0,4},{4,0},{1,5},{5,1},{2,6},{6,2},{3,7},{7,3},{8,12},{12,8},{9,1... | collective-permute-start | bytes 3145736 | tf_op jit(solution)/shard_map/ppermute | solution.py:45
  160.5 2.9 %collective-permute-start.12 = (bf16[256,2048]{1,0:T(8,128)(2,1)S(1)}, bf16[256,2048]{1,0:T(8,128)(2,1)S(1)}, u32[]{:S(2)}, u32[]{:S(2)}) collective-permute-start(bf16[256,2048]{1,0:T(8,128)(2,1)S(1)} %collective-permute-done.8), channel_id=1, source_target_pairs={{0,4},{4,0},{1,5},{5,1},{2,6},{6,2},{3,7},{7,3},{8,12},{12,8},{9,1... | collective-permute-start | bytes 3145736 | tf_op jit(solution)/shard_map/ppermute | solution.py:46
  161.7 3.0 %collective-permute-start.13 = (bf16[256,2048]{1,0:T(8,128)(2,1)S(1)}, bf16[256,2048]{1,0:T(8,128)(2,1)S(1)}, u32[]{:S(2)}, u32[]{:S(2)}) collective-permute-start(bf16[256,2048]{1,0:T(8,128)(2,1)S(1)} %collective-permute-done.9), channel_id=1, source_target_pairs={{0,4},{4,0},{1,5},{5,1},{2,6},{6,2},{3,7},{7,3},{8,12},{12,8},{9,1... | collective-permute-start | bytes 3145736 | tf_op jit(solution)/shard_map/ppermute | solution.py:46
  162.2 4.1 %collective-permute-start.14 = (bf16[256,2048]{1,0:T(8,128)(2,1)S(1)}, bf16[256,2048]{1,0:T(8,128)(2,1)S(1)}, u32[]{:S(2)}, u32[]{:S(2)}) collective-permute-start(bf16[256,2048]{1,0:T(8,128)(2,1)S(1)} %collective-permute-done.10), channel_id=1, source_target_pairs={{0,4},{4,0},{1,5},{5,1},{2,6},{6,2},{3,7},{7,3},{8,12},{12,8},{9,1... | collective-permute-start | bytes 3145736 | tf_op jit(solution)/shard_map/ppermute | solution.py:46
  162.6 5.1 %collective-permute-start.15 = (bf16[256,2048]{1,0:T(8,128)(2,1)S(1)}, bf16[256,2048]{1,0:T(8,128)(2,1)S(1)}, u32[]{:S(2)}, u32[]{:S(2)}) collective-permute-start(bf16[256,2048]{1,0:T(8,128)(2,1)S(1)} %collective-permute-done.11), channel_id=1, source_target_pairs={{0,4},{4,0},{1,5},{5,1},{2,6},{6,2},{3,7},{7,3},{8,12},{12,8},{9,1... | collective-permute-start | bytes 3145736 | tf_op jit(solution)/shard_map/ppermute | solution.py:46
  163.3 4.4 %copy-start.3 = (bf16[2048,2048]{1,0:T(8,128)(2,1)}, bf16[2048,2048]{1,0:T(8,128)(2,1)S(1)}, u32[]{:S(2)}) copy-start(bf16[2048,2048]{1,0:T(8,128)(2,1)S(1)} %constant_dynamic-update-slice_fusion) | copy-start | bytes 25165828
  195.0 92.9 %copy-start.1 = (bf16[384,2048]{1,0:T(8,128)(2,1)S(1)}, bf16[384,2048]{1,0:T(8,128)(2,1)}, u32[]{:S(2)}) copy-start(bf16[384,2048]{1,0:T(8,128)(2,1)} %param.5) | copy-start | bytes 4718596

commit v2 on v1

v2 whole, which is shorter than its diff:
```python
import functools

import jax
import jax.numpy as jnp
from jax import lax
from jax.experimental import pallas as pl
from jax.experimental.pallas import tpu as pltpu
from jax.sharding import Mesh, PartitionSpec as P

BF = jnp.bfloat16
F32 = jnp.float32
CUTS = (0, 1536, 2048)


def weight_route():
    rounds = []
    for p in range(4):
        pairs = []
        for c in range(2):
            for y in range(4):
                bits = y ^ p
                h, k = bits >> 1, bits & 1
                pairs.append((c * 4 + y, h * 4 + 2 * c + k))
        rounds.append(pairs)
    return rounds


def pack_kernel(slots, ids_ref, table_ref, tok_ref, packed_ref, place_ref):
    rows, lanes = table_ref.shape
    tok = ids_ref.shape[1]
    pairs = packed_ref.shape[0]
    experts = 2 * pairs // slots
    ids = ids_ref[...]
    low = lax.rem(ids, lanes)
    high = lax.div(ids, lanes)
    low_hot = (lax.broadcasted_iota(jnp.int32, (lanes, tok), 0) == low).astype(F32).astype(BF)
    picked = jnp.dot(table_ref[...].astype(F32).astype(BF), low_hot, preferred_element_type=F32)
    high_hot = lax.broadcasted_iota(jnp.int32, (rows, tok), 0) == high
    chosen = jnp.sum(jnp.where(high_hot, picked, 0.0), axis=0, keepdims=True)
    hot = lax.broadcasted_iota(jnp.int32, (experts, tok), 0).astype(F32) == chosen
    before = (
        lax.broadcasted_iota(jnp.int32, (tok, tok), 0) < lax.broadcasted_iota(jnp.int32, (tok, tok), 1)
    ).astype(F32).astype(BF)
    earlier = jnp.dot(hot.astype(F32).astype(BF), before, preferred_element_type=F32)
    rank = jnp.sum(jnp.where(hot, earlier, 0.0), axis=0, keepdims=True)
    place = jnp.where(rank < slots, chosen * slots + rank, -1.0).astype(jnp.int32)
    place_ref[...] = place
    block = 128

    def step(i, _):
        at = lax.broadcasted_iota(jnp.int32, (block, tok), 0) + i * block
        onehot = (at == place).astype(F32).astype(BF)
        out = jnp.dot(onehot, tok_ref[...], preferred_element_type=F32).astype(BF)
        packed_ref[pl.ds(pl.multiple_of(i * (block // 2), block // 2), block // 2)] = out.reshape(block // 2, 2, out.shape[1])
        return 0

    lax.fori_loop(0, 2 * pairs // block, step, 0)


def pack(token_ids, table, tokens, experts, slots):
    tok, width = tokens.shape
    return pl.pallas_call(
        functools.partial(pack_kernel, slots),
        out_shape=(
            jax.ShapeDtypeStruct((experts * slots // 2, 2, width), BF),
            jax.ShapeDtypeStruct((1, tok), jnp.int32),
        ),
        cost_estimate=pl.CostEstimate(flops=2 * experts * slots * tok * width, bytes_accessed=6 * 1024 * 1024, transcendentals=0),
        compiler_params=pltpu.CompilerParams(vmem_limit_bytes=12 * 1024 * 1024),
        name="pack",
    )(token_ids.reshape(1, tok), table.reshape(-1, 128), tokens)


def flatten_rows(src_ref, dst_ref):
    pairs, _, width = src_ref.shape
    block = 16

    def step(i, _):
        part = src_ref[pl.ds(pl.multiple_of(i * block, block), block)]
        dst_ref[pl.ds(pl.multiple_of(i * 2 * block, 2 * block), 2 * block), :] = part.reshape(2 * block, width)
        return 0

    lax.fori_loop(0, pairs // block, step, 0)


def up_kernel(x_ref, own_ref, other_ref, hidden_ref, rows_ref):
    j = pl.program_id(0)

    @pl.when(j == 0)
    def _():
        flatten_rows(x_ref, rows_ref)

    def run(w_ref):
        out = jnp.dot(rows_ref[...], w_ref[...], preferred_element_type=F32)
        hidden_ref[...] = jnp.maximum(out, 0.0).astype(BF)

    half = pl.num_programs(0) // 2

    @pl.when(j < half)
    def _():
        run(own_ref)

    @pl.when(j >= half)
    def _():
        run(other_ref)


def up(arrived, own, other):
    pairs, _, width = arrived.shape
    units = own.shape[1]
    block = 256
    half = units // block
    return pl.pallas_call(
        up_kernel,
        grid=(2 * half,),
        in_specs=[
            pl.BlockSpec(memory_space=pltpu.VMEM),
            pl.BlockSpec((width, block), lambda j: (0, jnp.minimum(j, half - 1))),
            pl.BlockSpec((width, block), lambda j: (0, jnp.maximum(j - half, 0))),
        ],
        out_specs=pl.BlockSpec((2 * pairs, block), lambda j: (0, j)),
        out_shape=jax.ShapeDtypeStruct((2 * pairs, 2 * units), BF),
        scratch_shapes=[pltpu.VMEM((2 * pairs, width), BF)],
        cost_estimate=pl.CostEstimate(flops=8 * pairs * units * width, bytes_accessed=16 * 1024 * 1024, transcendentals=0),
        compiler_params=pltpu.CompilerParams(vmem_limit_bytes=24 * 1024 * 1024),
        name="up",
    )(arrived, own, other)


def down_kernel(n, hidden_ref, *refs):
    pieces, out_ref, w_ref = refs[:n], refs[-2], refs[-1]
    depth = pieces[0].shape[0]
    for p in range(n):
        w_ref[p * depth:(p + 1) * depth, :] = pieces[p][...]
    out = jnp.dot(hidden_ref[...], w_ref[...], preferred_element_type=F32).astype(BF)
    out_ref[...] = out.reshape(out_ref.shape)


def down(hidden, pieces, start, width, base):
    rows, units = hidden.shape
    depth, cols = pieces[0].shape
    n = len(pieces)
    block = 512
    first = start // block
    specs = [pl.BlockSpec(memory_space=pltpu.VMEM)]
    specs += [pl.BlockSpec((depth, block), lambda j: (0, j)) for _ in range(n)]
    args = [hidden, *pieces]
    aliases = {}
    if base is not None:
        aliases = {len(args): 0}
        args.append(base)
        specs.append(pl.BlockSpec(memory_space=pl.ANY))
    return pl.pallas_call(
        functools.partial(down_kernel, n),
        grid=(cols // block,),
        in_specs=specs,
        out_specs=pl.BlockSpec((rows // 2, 2, block), lambda j: (0, 0, j + first)),
        out_shape=jax.ShapeDtypeStruct((rows // 2, 2, width), BF),
        scratch_shapes=[pltpu.VMEM((units, block), BF)],
        input_output_aliases=aliases,
        cost_estimate=pl.CostEstimate(
            flops=2 * rows * units * cols, bytes_accessed=2 * rows * (units + cols) + 2 * units * cols, transcendentals=0
        ),
        compiler_params=pltpu.CompilerParams(vmem_limit_bytes=20 * 1024 * 1024),
        name="down",
    )(*args)


def mix_kernel(place_ref, back_ref, out_ref, rows_ref, hot_ref):
    @pl.when(pl.program_id(0) == 0)
    def _():
        at = lax.broadcasted_iota(jnp.int32, hot_ref.shape, 0)
        hot_ref[...] = (at == place_ref[...]).astype(F32).astype(BF)

    flatten_rows(back_ref, rows_ref)
    out_ref[...] = lax.dot_general(
        hot_ref[...], rows_ref[...], (((0,), (0,)), ((), ())), preferred_element_type=F32
    ).astype(BF)


def mix(place, returned, block=512):
    pairs, _, cols = returned.shape
    tok = place.shape[1]
    return pl.pallas_call(
        mix_kernel,
        grid=(cols // block,),
        in_specs=[
            pl.BlockSpec((1, tok), lambda j: (0, 0)),
            pl.BlockSpec((pairs, 2, block), lambda j: (0, 0, j)),
        ],
        out_specs=pl.BlockSpec((tok, block), lambda j: (0, j)),
        out_shape=jax.ShapeDtypeStruct((tok, cols), BF),
        scratch_shapes=[pltpu.VMEM((2 * pairs, block), BF), pltpu.VMEM((2 * pairs, tok), BF)],
        cost_estimate=pl.CostEstimate(flops=4 * tok * pairs * cols, bytes_accessed=4 * pairs * cols + 2 * tok * cols, transcendentals=0),
        compiler_params=pltpu.CompilerParams(vmem_limit_bytes=16 * 1024 * 1024),
        name="mix",
    )(place, returned)


def on_device(tokens, token_ids, table, w_in, w_out):
    experts = lax.axis_size("g") * lax.axis_size("y")
    tok_rows, width = tokens.shape
    slots = 2 * tok_rows // experts
    half = w_out.shape[1] // 2
    y = lax.axis_index("y")
    route = weight_route()
    swap = [(0, 1), (1, 0)]
    own_in = []
    for p in range(4):
        h, k = (y ^ p) >> 1, (y ^ p) & 1
        block = lax.dynamic_slice(w_in, (k, 0, h * half), (1, width, half))[0]
        own_in.append(lax.ppermute(block, ("c", "y"), route[p]))
    own_in = jnp.concatenate(own_in, axis=1)
    other_in = lax.ppermute(own_in, "c", swap)
    pieces = []
    for low, high in zip(CUTS[:-1], CUTS[1:]):
        own = []
        for p in range(4):
            h, k = (y ^ p) >> 1, (y ^ p) & 1
            block = lax.dynamic_slice(w_out, (k, h * half, low), (1, half, high - low))[0]
            own.append(lax.ppermute(block, ("c", "y"), route[p]))
        pieces.append(own + [lax.ppermute(o, "c", swap) for o in own])

    packed, place = pack(token_ids, table, tokens, experts, slots)
    arrived = lax.all_to_all(packed, ("g", "y"), split_axis=0, concat_axis=0, tiled=True)
    hidden = up(arrived, own_in, other_in)
    result = None
    for j, low in enumerate(CUTS[:-1]):
        result = down(hidden, pieces[j], low, width, result)
    returned = lax.all_to_all(result, ("g", "y"), split_axis=0, concat_axis=0, tiled=True)
    return mix(place, returned)


def solution(mesh):
    groups, pair = mesh.shape["expert"], mesh.shape["pair"]
    fine = Mesh(mesh.devices.reshape(groups // 2, 2, pair), ("g", "c", "y"))
    rows = ("g", "c", "y")
    in_specs = (
        P(rows, None),
        P(rows),
        P(),
        P(("g", "c"), None, "y"),
        P(("g", "c"), "y", None),
    )
    return jax.shard_map(on_device, mesh=fine, in_specs=in_specs, out_specs=P(rows, None), check_vma=False)
```

time: 290 us -> 275 us (0.948)
  Pallas kernels: 0 us -> 27.6 us
  matrix products: 27.2 us -> 0 us
  local copies, waits for them, and re-layouts: 36 us -> 15.6 us
  starting transfers between devices: 41.2 us -> 49.4 us
  waiting for transfers between devices: 98.5 us -> 95 us
    pallas_call x0 -> x5, Pallas kernels: none -> 27.6 us  [the longest x2 10.3 us: down(): pl.pallas_call(functools.partial(down_kernel, n), grid=(cols // block,),...]
    dot_general x4 -> x0, matrix products: 27.2 us -> none  [the longest x1 10 us: on_device(): jnp.dot(arrived, full_in, preferred_element_type=F32)]
    reshape x4 -> x1, local copies, waits for them, and re-layouts: 18.7 us -> 0.01 us  [pack(): token_ids.reshape(1, tok)]
    ppermute x16 -> x21, starting transfers between devices: 24.8 us -> 29.8 us  [the longest x8 13.2 us: on_device(): own.append(lax.ppermute(block, ('c', 'y'), route[p]))]
    ppermute x16 -> x21, waiting for transfers between devices: 98.5 us -> 95 us  [the longest x4 63.2 us: on_device(): own_in.append(lax.ppermute(block, ('c', 'y'), route[p]))]
    gather x1 -> x0, local copies, waits for them, and re-layouts: 3.44 us -> none  [on_device(): chosen = jnp.take(table, token_ids, axis=0)]
    all_to_all x1, starting transfers between devices: 16.3 us -> 19.6 us  [on_device(): lax.all_to_all(packed, ('g', 'y'), split_axis=0, concat_axis=0, tiled=True)]
    unnamed x22 -> x29, local copies, waits for them, and re-layouts: 9.27 us -> 9.84 us
  transfers between devices with their start and end apart: 17 -> 22, of which waited for: 7 -> 9; matrix products, arithmetic and copies ran while one was open for 5% -> 1% of each run, Pallas kernels for 0% -> 8%
where the time goes in v2:
time: 275 us; the launch traced here: 273 us
  waiting for transfers between devices  95 us (35%)
  blocking collectives  85.2 us (31%)
  starting transfers between devices  49.4 us (18%)
  Pallas kernels  27.6 us (10%)
  local copies, waits for them, and re-layouts  15.6 us (6%)
    all_to_all x1, blocking collectives, on_device(): lax.all_to_all(result, ('g', 'y'), split_axis=0, concat_axis=0, tiled=True)  85.2 us
    ppermute x4, waiting for transfers between devices, on_device(): own_in.append(lax.ppermute(block, ('c', 'y'), route[p]))  63.2 us
    ppermute x8, waiting for transfers between devices, on_device(): own.append(lax.ppermute(block, ('c', 'y'), route[p]))  31.8 us
    all_to_all x1, starting transfers between devices, on_device(): lax.all_to_all(packed, ('g', 'y'), split_axis=0, concat_axis=0, tiled=True)  19.6 us
    ppermute x8, starting transfers between devices, on_device(): own.append(lax.ppermute(block, ('c', 'y'), route[p]))  13.2 us
    pallas_call x2, Pallas kernels, down(): pl.pallas_call(functools.partial(down_kernel, n), grid=(cols // block,),...  10.3 us
    pallas_call x1, Pallas kernels, up(): pl.pallas_call(up_kernel, grid=(2 * half,), in_specs=[pl.BlockSpec(memory...  10 us
    unnamed x29, local copies, waits for them, and re-layouts  9.84 us
  transfers between devices with their start and end apart: 22, of which 9 were waited for; matrix products, arithmetic and copies ran while one was open for 1% of the time, Pallas kernels for 8%

profile of v2, /device:TPU:1, one launch (start us, length us, event | category | flops | bytes accessed | tf_op | source)
XLA Modules:
  0.0 273.1 jit_solution(18397844209956784943)
XLA Ops:
  0.0 4.4 %dynamic-slice_bitcast_fusion = (bf16[2048,256]{1,0:T(8,128)(2,1)}, bf16[2048,256]{1,0:T(8,128)(2,1)}, bf16[2048,256]{1,0:T(8,128)(2,1)}, bf16[2048,256]{1,0:T(8,128)(2,1)}) fusion(bf16[2,2048,512]{2,1,0:T(8,128)(2,1)} %param.8, s32[]{:T(128)S(6)} %select_n.22, s32[]{:T(128)S(6)} %select_n.23, s32[]{:T(128)S(6)} %select_n.18, s32[]{:T(128)S(6)} %select_n.19, ...), kind=kLoop, calls=%fused_computation | loop fusion | bytes 8388640 | tf_op jit(solution)/shard_map/squeeze | solution.py:211
  4.4 6.2 %collective-permute-start = (bf16[2048,256]{1,0:T(8,128)(2,1)}, bf16[2048,256]{1,0:T(8,128)(2,1)}, u32[]{:S(2)}, u32[]{:S(2)}) collective-permute-start(bf16[2048,256]{1,0:T(8,128)(2,1)} %get-tuple-element.19), channel_id=1, source_target_pairs={{0,0},{1,1},{2,4},{3,5},{4,2},{5,3},{6,6},{7,7},{8,8},{9,9},{10,12... | collective-permute-start | bytes 3145736 | tf_op jit(solution)/shard_map/ppermute | solution.py:212
  10.6 3.1 %pack.1 = (bf16[384,2,2048]{2,1,0:T(2,128)(2,1)S(1)}, s32[1,384]{1,0:T(1,128)S(1)}) custom-call(s32[1,384]{1,0:T(1,128)S(1)} %reshape.6.ids_ref, s32[64,128]{1,0:T(8,128)S(1)} %bitcast.25, bf16[384,2048]{1,0:T(8,128)(2,1)S(1)} %copy-done.9), custom_call_target="tpu_custom_call" | custom-call | flops 1207959552 | bytes 6291456 | tf_op jit(solution)/shard_map/pack/pallas_call | solution.py:62
  13.8 1.6 copy-done
  15.4 19.6 %all-to-all-start = ((bf16[384,2,2048]{2,1,0:T(2,128)(2,1)}), bf16[384,2,2048]{2,1,0:T(2,128)(2,1)S(1)}, u32[]{:S(2)}, u32[]{:S(2)}) async-start(bf16[384,2,2048]{2,1,0:T(2,128)(2,1)} %copy-done), calls=%async_computation | async-start | bytes 6291456 | tf_op jit(solution)/shard_map/all_to_all | solution.py:225
  35.0 1.4 collective-permute-start.1
  36.4 1.7 collective-permute-start.2
  38.2 1.5 constant_dynamic-update-slice_fusion.3
  39.7 39.9 %collective-permute-done.1 = bf16[2048,256]{1,0:T(8,128)(2,1)S(1)} collective-permute-done((bf16[2048,256]{1,0:T(8,128)(2,1)}, bf16[2048,256]{1,0:T(8,128)(2,1)S(1)}, u32[]{:S(2)}, u32[]{:S(2)}) %collective-permute-start.1) | collective-permute-done | bytes 1048608 | tf_op jit(solution)/shard_map/ppermute | solution.py:212
  79.7 4.0 %collective-permute-done.2 = bf16[2048,256]{1,0:T(8,128)(2,1)S(1)} collective-permute-done((bf16[2048,256]{1,0:T(8,128)(2,1)}, bf16[2048,256]{1,0:T(8,128)(2,1)S(1)}, u32[]{:S(2)}, u32[]{:S(2)}) %collective-permute-start.2) | collective-permute-done | bytes 1048608 | tf_op jit(solution)/shard_map/ppermute | solution.py:212
  83.9 19.2 %collective-permute-done.3 = bf16[2048,256]{1,0:T(8,128)(2,1)S(1)} collective-permute-done((bf16[2048,256]{1,0:T(8,128)(2,1)}, bf16[2048,256]{1,0:T(8,128)(2,1)S(1)}, u32[]{:S(2)}, u32[]{:S(2)}) %collective-permute-start.3) | collective-permute-done | bytes 1048608 | tf_op jit(solution)/shard_map/ppermute | solution.py:212
  103.3 1.2 collective-permute-start.4
  105.4 2.6 collective-permute-start.5
  108.0 2.1 collective-permute-start.6
  110.5 2.6 collective-permute-start.13
  113.1 1.6 collective-permute-done.5.refs_0_
  114.7 3.2 %collective-permute-start.14 = (bf16[256,1536]{1,0:T(8,128)(2,1)S(1)}, bf16[256,1536]{1,0:T(8,128)(2,1)}, u32[]{:S(2)}, u32[]{:S(2)}) collective-permute-start(bf16[256,1536]{1,0:T(8,128)(2,1)S(1)} %get-tuple-element.10), channel_id=1, source_target_pairs={{0,1},{1,0},{2,5},{3,4},{4,3},{5,2},{6,7},{7,6},{8,9},{9,8},{10,13... | collective-permute-start | bytes 2359304 | tf_op jit(solution)/shard_map/ppermute | solution.py:221
  117.9 2.8 %collective-permute-done.6.refs_1_ = bf16[256,512]{1,0:T(8,128)(2,1)S(1)} collective-permute-done((bf16[256,512]{1,0:T(8,128)(2,1)S(1)}, bf16[256,512]{1,0:T(8,128)(2,1)S(1)}, u32[]{:S(2)}, u32[]{:S(2)}) %collective-permute-start.6) | collective-permute-done | bytes 262176 | tf_op jit(solution)/shard_map/ppermute | solution.py:221
  120.7 1.6 collective-permute-start.16
  122.3 14.4 %collective-permute-done.13.refs_0_ = bf16[256,1536]{1,0:T(8,128)(2,1)} collective-permute-done((bf16[256,1536]{1,0:T(8,128)(2,1)S(1)}, bf16[256,1536]{1,0:T(8,128)(2,1)}, u32[]{:S(2)}, u32[]{:S(2)}) %collective-permute-start.13) | collective-permute-done | bytes 786464 | tf_op jit(solution)/shard_map/ppermute | solution.py:221
  136.8 1.1 collective-permute-done.14.refs_1_
  137.9 11.3 %collective-permute-done.15.refs_2_ = bf16[256,1536]{1,0:T(8,128)(2,1)} collective-permute-done((bf16[256,1536]{1,0:T(8,128)(2,1)S(1)}, bf16[256,1536]{1,0:T(8,128)(2,1)}, u32[]{:S(2)}, u32[]{:S(2)}) %collective-permute-start.15) | collective-permute-done | bytes 786464 | tf_op jit(solution)/shard_map/ppermute | solution.py:221
  149.2 2.8 %collective-permute-start.19 = (bf16[256,1536]{1,0:T(8,128)(2,1)}, bf16[256,1536]{1,0:T(8,128)(2,1)}, u32[]{:S(2)}, u32[]{:S(2)}) collective-permute-start(bf16[256,1536]{1,0:T(8,128)(2,1)} %collective-permute-done.15.refs_2_), channel_id=1, source_target_pairs={{0,4},{4,0},{1,5},{5,1},{2,6},{6,2},{3,7},{7,3},{8,12},{12,8},{9,1... | collective-permute-start | bytes 2359304 | tf_op jit(solution)/shard_map/ppermute | solution.py:222
  152.5 2.2 collective-permute-start.20
  154.8 2.0 copy-done.7
  157.8 2.2 copy-done.6
  160.0 2.2 copy-done.8
  162.2 10.0 %up.1.hidden_ref = bf16[768,2048]{1,0:T(8,128)(2,1)S(1)} custom-call(bf16[384,2,2048]{2,1,0:T(2,128)(2,1)S(1)} %all-to-all-done.x_ref, bf16[2048,1024]{1,0:T(8,128)(2,1)S(1)} %copy-done.6, bf16[2048,1024]{1,0:T(8,128)(2,1)S(1)} %copy-done.8), custom_call_target="tpu_custom_call" | custom-call | flops 6442450944 | bytes 16777216 | tf_op jit(solution)/shard_map/up/pallas_call | solution.py:113
  173.4 7.4 %down.2.refs_8_ = bf16[384,2,2048]{2,1,0:T(2,128)(2,1)S(1)} custom-call(bf16[768,2048]{1,0:T(8,128)(2,1)S(1)} %up.1.hidden_ref, bf16[256,1536]{1,0:T(8,128)(2,1)} %collective-permute-done.13.refs_0_, bf16[256,1536]{1,0:T(8,128)(2,1)} %collective-permute-done.14.refs_1_, bf16[256,1536]{1,0:T(8,128)(2,1)} %collective-permute-done.15.refs_2_, ...), custom_call_target="tpu_custom_call" | custom-call | flops 4831838208 | bytes 11796480 | tf_op jit(solution)/shard_map/down/pallas_call | solution.py:153
  180.8 2.9 %down.3 = bf16[384,2,2048]{2,1,0:T(2,128)(2,1)S(1)} custom-call(bf16[768,2048]{1,0:T(8,128)(2,1)S(1)} %up.1.hidden_ref, bf16[256,512]{1,0:T(8,128)(2,1)S(1)} %collective-permute-done.5.refs_0_, bf16[256,512]{1,0:T(8,128)(2,1)S(1)} %copy-done.2, bf16[256,512]{1,0:T(8,128)(2,1)S(1)} %copy-done.4, ...), custom_call_target="tpu_custom_call", output_to_operand_aliasing={{}: (9, {})} | custom-call | flops 1610612736 | bytes 6029312 | tf_op jit(solution)/shard_map/down/pallas_call | solution.py:153
  183.7 85.2 %all_to_all.10.back_ref = bf16[384,2,2048]{2,1,0:T(2,128)(2,1)S(1)} all-to-all(bf16[384,2,2048]{2,1,0:T(2,128)(2,1)S(1)} %down.3), channel_id=1, replica_groups=mesh['g'=32,'c'=2,'y'=4] {'g','y'}, dimensions={0} | all-to-all | bytes 6291456 | tf_op jit(solution)/shard_map/all_to_all | solution.py:230
  268.9 4.2 %mix.1 = bf16[384,2048]{1,0:T(8,128)(2,1)} custom-call(s32[1,384]{1,0:T(1,128)S(1)} %get-tuple-element.7.place_ref, bf16[384,2,2048]{2,1,0:T(2,128)(2,1)S(1)} %all_to_all.10.back_ref), custom_call_target="tpu_custom_call" | custom-call | flops 1207959552 | bytes 4718592 | tf_op jit(solution)/shard_map/mix/pallas_call | solution.py:184
  (52 shorter events, 4.4 us)
Async XLA Ops:
  0.0 10.6 %copy-start.12 = (s32[384]{0:T(512)S(1)}, s32[384]{0:T(512)}, u32[]{:S(2)}) copy-start(s32[384]{0:T(512)} %param.6) | copy-start | bytes 4612
  0.0 10.6 %copy-start.9 = (bf16[384,2048]{1,0:T(8,128)(2,1)S(1)}, bf16[384,2048]{1,0:T(8,128)(2,1)}, u32[]{:S(2)}) copy-start(bf16[384,2048]{1,0:T(8,128)(2,1)} %tok_ref.1) | copy-start | bytes 4718596
  0.0 10.6 %copy-start.10 = (s32[8192]{0:T(1024)S(1)}, s32[8192]{0:T(1024)}, u32[]{:S(2)}) copy-start(s32[8192]{0:T(1024)} %param.7) | copy-start | bytes 98308
  4.4 33.8 %collective-permute-start = (bf16[2048,256]{1,0:T(8,128)(2,1)}, bf16[2048,256]{1,0:T(8,128)(2,1)}, u32[]{:S(2)}, u32[]{:S(2)}) collective-permute-start(bf16[2048,256]{1,0:T(8,128)(2,1)} %get-tuple-element.19), channel_id=1, source_target_pairs={{0,0},{1,1},{2,4},{3,5},{4,2},{5,3},{6,6},{7,7},{8,8},{9,9},{10,12... | collective-permute-start | bytes 3145736 | tf_op jit(solution)/shard_map/ppermute | solution.py:212
  15.4 142.4 %all-to-all-start = ((bf16[384,2,2048]{2,1,0:T(2,128)(2,1)}), bf16[384,2,2048]{2,1,0:T(2,128)(2,1)S(1)}, u32[]{:S(2)}, u32[]{:S(2)}) async-start(bf16[384,2,2048]{2,1,0:T(2,128)(2,1)} %copy-done), calls=%async_computation | async-start | bytes 6291456 | tf_op jit(solution)/shard_map/all_to_all | solution.py:225
  35.0 44.6 %collective-permute-start.1 = (bf16[2048,256]{1,0:T(8,128)(2,1)}, bf16[2048,256]{1,0:T(8,128)(2,1)S(1)}, u32[]{:S(2)}, u32[]{:S(2)}) collective-permute-start(bf16[2048,256]{1,0:T(8,128)(2,1)} %get-tuple-element.18), channel_id=1, source_target_pairs={{0,1},{1,0},{2,5},{3,4},{4,3},{5,2},{6,7},{7,6},{8,9},{9,8},{10,13... | collective-permute-start | bytes 3145736 | tf_op jit(solution)/shard_map/ppermute | solution.py:212
  36.4 47.4 %collective-permute-start.2 = (bf16[2048,256]{1,0:T(8,128)(2,1)}, bf16[2048,256]{1,0:T(8,128)(2,1)S(1)}, u32[]{:S(2)}, u32[]{:S(2)}) collective-permute-start(bf16[2048,256]{1,0:T(8,128)(2,1)} %get-tuple-element.20), channel_id=1, source_target_pairs={{0,4},{1,5},{2,0},{3,1},{4,6},{5,7},{6,2},{7,3},{8,12},{9,13},{10,... | collective-permute-start | bytes 3145736 | tf_op jit(solution)/shard_map/ppermute | solution.py:212
  38.1 66.4 %copy-start.11 = (bf16[2,512,2048]{2,1,0:T(8,128)(2,1)S(1)}, bf16[2,512,2048]{2,1,0:T(8,128)(2,1)}, u32[]{:S(2)}) copy-start(bf16[2,512,2048]{2,1,0:T(8,128)(2,1)} %param.9) | copy-start | bytes 12582916
  38.1 65.1 %collective-permute-start.3 = (bf16[2048,256]{1,0:T(8,128)(2,1)}, bf16[2048,256]{1,0:T(8,128)(2,1)S(1)}, u32[]{:S(2)}, u32[]{:S(2)}) collective-permute-start(bf16[2048,256]{1,0:T(8,128)(2,1)} %get-tuple-element.17), channel_id=1, source_target_pairs={{0,5},{1,4},{2,1},{3,0},{4,7},{5,6},{6,3},{7,2},{8,13},{9,12},{10,... | collective-permute-start | bytes 3145736 | tf_op jit(solution)/shard_map/ppermute | solution.py:212
  103.3 7.2 %copy-start.5 = (bf16[2048,1024]{1,0:T(8,128)(2,1)}, bf16[2048,1024]{1,0:T(8,128)(2,1)S(1)}, u32[]{:S(2)}) copy-start(bf16[2048,1024]{1,0:T(8,128)(2,1)S(1)} %constant_dynamic-update-slice_fusion.own_ref) | copy-start | bytes 12582916
  103.3 51.5 %collective-permute-start.4 = (bf16[2048,1024]{1,0:T(8,128)(2,1)S(1)}, bf16[2048,1024]{1,0:T(8,128)(2,1)S(1)}, u32[]{:S(2)}, u32[]{:S(2)}) collective-permute-start(bf16[2048,1024]{1,0:T(8,128)(2,1)S(1)} %constant_dynamic-update-slice_fusion.own_ref), channel_id=1, source_target_pairs={{0,4},{4,0},{1,5},{5,1},{2,6},{6,2},{3,7},{7,3},{8,12},{12,8},{9,1... | collective-permute-start | bytes 12582920 | tf_op jit(solution)/shard_map/ppermute | solution.py:214
  105.4 9.4 %collective-permute-start.5 = (bf16[256,512]{1,0:T(8,128)(2,1)S(1)}, bf16[256,512]{1,0:T(8,128)(2,1)S(1)}, u32[]{:S(2)}, u32[]{:S(2)}) collective-permute-start(bf16[256,512]{1,0:T(8,128)(2,1)S(1)} %get-tuple-element.16), channel_id=1, source_target_pairs={{0,0},{1,1},{2,4},{3,5},{4,2},{5,3},{6,6},{7,7},{8,8},{9,9},{10,12... | collective-permute-start | bytes 786440 | tf_op jit(solution)/shard_map/ppermute | solution.py:221
  108.0 12.7 %collective-permute-start.6 = (bf16[256,512]{1,0:T(8,128)(2,1)S(1)}, bf16[256,512]{1,0:T(8,128)(2,1)S(1)}, u32[]{:S(2)}, u32[]{:S(2)}) collective-permute-start(bf16[256,512]{1,0:T(8,128)(2,1)S(1)} %get-tuple-element.15), channel_id=1, source_target_pairs={{0,1},{1,0},{2,5},{3,4},{4,3},{5,2},{6,7},{7,6},{8,9},{9,8},{10,13... | collective-permute-start | bytes 786440 | tf_op jit(solution)/shard_map/ppermute | solution.py:221
  110.1 10.6 %collective-permute-start.7 = (bf16[256,512]{1,0:T(8,128)(2,1)S(1)}, bf16[256,512]{1,0:T(8,128)(2,1)S(1)}, u32[]{:S(2)}, u32[]{:S(2)}) collective-permute-start(bf16[256,512]{1,0:T(8,128)(2,1)S(1)} %get-tuple-element.14), channel_id=1, source_target_pairs={{0,4},{1,5},{2,0},{3,1},{4,6},{5,7},{6,2},{7,3},{8,12},{9,13},{10,... | collective-permute-start | bytes 786440 | tf_op jit(solution)/shard_map/ppermute | solution.py:221
  110.5 26.3 %collective-permute-start.13 = (bf16[256,1536]{1,0:T(8,128)(2,1)S(1)}, bf16[256,1536]{1,0:T(8,128)(2,1)}, u32[]{:S(2)}, u32[]{:S(2)}) collective-permute-start(bf16[256,1536]{1,0:T(8,128)(2,1)S(1)} %get-tuple-element.11), channel_id=1, source_target_pairs={{0,0},{1,1},{2,4},{3,5},{4,2},{5,3},{6,6},{7,7},{8,8},{9,9},{10,12... | collective-permute-start | bytes 2359304 | tf_op jit(solution)/shard_map/ppermute | solution.py:221
  114.7 23.2 %collective-permute-start.14 = (bf16[256,1536]{1,0:T(8,128)(2,1)S(1)}, bf16[256,1536]{1,0:T(8,128)(2,1)}, u32[]{:S(2)}, u32[]{:S(2)}) collective-permute-start(bf16[256,1536]{1,0:T(8,128)(2,1)S(1)} %get-tuple-element.10), channel_id=1, source_target_pairs={{0,1},{1,0},{2,5},{3,4},{4,3},{5,2},{6,7},{7,6},{8,9},{9,8},{10,13... | collective-permute-start | bytes 2359304 | tf_op jit(solution)/shard_map/ppermute | solution.py:221
  120.7 36.1 %copy-start.1 = (bf16[256,512]{1,0:T(8,128)(2,1)}, bf16[256,512]{1,0:T(8,128)(2,1)S(1)}, u32[]{:S(2)}) copy-start(bf16[256,512]{1,0:T(8,128)(2,1)S(1)} %collective-permute-done.6.refs_1_) | copy-start | bytes 786436
  120.7 28.5 %collective-permute-start.15 = (bf16[256,1536]{1,0:T(8,128)(2,1)S(1)}, bf16[256,1536]{1,0:T(8,128)(2,1)}, u32[]{:S(2)}, u32[]{:S(2)}) collective-permute-start(bf16[256,1536]{1,0:T(8,128)(2,1)S(1)} %get-tuple-element.12), channel_id=1, source_target_pairs={{0,4},{1,5},{2,0},{3,1},{4,6},{5,7},{6,2},{7,3},{8,12},{9,13},{10,... | collective-permute-start | bytes 2359304 | tf_op jit(solution)/shard_map/ppermute | solution.py:221
  120.7 36.1 %copy-start.3 = (bf16[256,512]{1,0:T(8,128)(2,1)}, bf16[256,512]{1,0:T(8,128)(2,1)S(1)}, u32[]{:S(2)}) copy-start(bf16[256,512]{1,0:T(8,128)(2,1)S(1)} %collective-permute-done.7.refs_2_) | copy-start | bytes 786436
  120.7 31.8 %collective-permute-start.16 = (bf16[256,1536]{1,0:T(8,128)(2,1)S(1)}, bf16[256,1536]{1,0:T(8,128)(2,1)}, u32[]{:S(2)}, u32[]{:S(2)}) collective-permute-start(bf16[256,1536]{1,0:T(8,128)(2,1)S(1)} %get-tuple-element.9), channel_id=1, source_target_pairs={{0,5},{1,4},{2,1},{3,0},{4,7},{5,6},{6,3},{7,2},{8,13},{9,12},{10,... | collective-permute-start | bytes 2359304 | tf_op jit(solution)/shard_map/ppermute | solution.py:221
  136.8 35.5 %collective-permute-start.17 = (bf16[256,1536]{1,0:T(8,128)(2,1)}, bf16[256,1536]{1,0:T(8,128)(2,1)}, u32[]{:S(2)}, u32[]{:S(2)}) collective-permute-start(bf16[256,1536]{1,0:T(8,128)(2,1)} %collective-permute-done.13.refs_0_), channel_id=1, source_target_pairs={{0,4},{4,0},{1,5},{5,1},{2,6},{6,2},{3,7},{7,3},{8,12},{12,8},{9,1... | collective-permute-start | bytes 2359304 | tf_op jit(solution)/shard_map/ppermute | solution.py:222
  137.9 34.9 %collective-permute-start.18 = (bf16[256,1536]{1,0:T(8,128)(2,1)}, bf16[256,1536]{1,0:T(8,128)(2,1)}, u32[]{:S(2)}, u32[]{:S(2)}) collective-permute-start(bf16[256,1536]{1,0:T(8,128)(2,1)} %collective-permute-done.14.refs_1_), channel_id=1, source_target_pairs={{0,4},{4,0},{1,5},{5,1},{2,6},{6,2},{3,7},{7,3},{8,12},{12,8},{9,1... | collective-permute-start | bytes 2359304 | tf_op jit(solution)/shard_map/ppermute | solution.py:222
  149.2 23.8 %collective-permute-start.19 = (bf16[256,1536]{1,0:T(8,128)(2,1)}, bf16[256,1536]{1,0:T(8,128)(2,1)}, u32[]{:S(2)}, u32[]{:S(2)}) collective-permute-start(bf16[256,1536]{1,0:T(8,128)(2,1)} %collective-permute-done.15.refs_2_), channel_id=1, source_target_pairs={{0,4},{4,0},{1,5},{5,1},{2,6},{6,2},{3,7},{7,3},{8,12},{12,8},{9,1... | collective-permute-start | bytes 2359304 | tf_op jit(solution)/shard_map/ppermute | solution.py:222
  152.5 20.8 %collective-permute-start.20 = (bf16[256,1536]{1,0:T(8,128)(2,1)}, bf16[256,1536]{1,0:T(8,128)(2,1)}, u32[]{:S(2)}, u32[]{:S(2)}) collective-permute-start(bf16[256,1536]{1,0:T(8,128)(2,1)} %collective-permute-done.16.refs_3_), channel_id=1, source_target_pairs={{0,4},{4,0},{1,5},{5,1},{2,6},{6,2},{3,7},{7,3},{8,12},{12,8},{9,1... | collective-permute-start | bytes 2359304 | tf_op jit(solution)/shard_map/ppermute | solution.py:222
  156.8 15.4 %collective-permute-start.8 = (bf16[256,512]{1,0:T(8,128)(2,1)}, bf16[256,512]{1,0:T(8,128)(2,1)}, u32[]{:S(2)}, u32[]{:S(2)}) collective-permute-start(bf16[256,512]{1,0:T(8,128)(2,1)} %get-tuple-element.13), channel_id=1, source_target_pairs={{0,5},{1,4},{2,1},{3,0},{4,7},{5,6},{6,3},{7,2},{8,13},{9,12},{10,... | collective-permute-start | bytes 786440 | tf_op jit(solution)/shard_map/ppermute | solution.py:221
  157.8 2.2 copy-start.6
  162.2 10.2 %copy-start.2 = (bf16[256,512]{1,0:T(8,128)(2,1)S(1)}, bf16[256,512]{1,0:T(8,128)(2,1)}, u32[]{:S(2)}) copy-start(bf16[256,512]{1,0:T(8,128)(2,1)} %copy-done.1) | copy-start | bytes 786436
  162.2 10.7 %copy-start.4 = (bf16[256,512]{1,0:T(8,128)(2,1)S(1)}, bf16[256,512]{1,0:T(8,128)(2,1)}, u32[]{:S(2)}) copy-start(bf16[256,512]{1,0:T(8,128)(2,1)} %copy-done.3) | copy-start | bytes 786436
  172.2 8.5 %collective-permute-start.9 = (bf16[256,512]{1,0:T(8,128)(2,1)S(1)}, bf16[256,512]{1,0:T(8,128)(2,1)S(1)}, u32[]{:S(2)}, u32[]{:S(2)}) collective-permute-start(bf16[256,512]{1,0:T(8,128)(2,1)S(1)} %collective-permute-done.5.refs_0_), channel_id=1, source_target_pairs={{0,4},{4,0},{1,5},{5,1},{2,6},{6,2},{3,7},{7,3},{8,12},{12,8},{9,1... | collective-permute-start | bytes 786440 | tf_op jit(solution)/shard_map/ppermute | solution.py:222
  172.4 8.4 %collective-permute-start.10 = (bf16[256,512]{1,0:T(8,128)(2,1)S(1)}, bf16[256,512]{1,0:T(8,128)(2,1)S(1)}, u32[]{:S(2)}, u32[]{:S(2)}) collective-permute-start(bf16[256,512]{1,0:T(8,128)(2,1)S(1)} %copy-done.2), channel_id=1, source_target_pairs={{0,4},{4,0},{1,5},{5,1},{2,6},{6,2},{3,7},{7,3},{8,12},{12,8},{9,1... | collective-permute-start | bytes 786440 | tf_op jit(solution)/shard_map/ppermute | solution.py:222
  172.8 8.0 %collective-permute-start.11 = (bf16[256,512]{1,0:T(8,128)(2,1)S(1)}, bf16[256,512]{1,0:T(8,128)(2,1)S(1)}, u32[]{:S(2)}, u32[]{:S(2)}) collective-permute-start(bf16[256,512]{1,0:T(8,128)(2,1)S(1)} %copy-done.4), channel_id=1, source_target_pairs={{0,4},{4,0},{1,5},{5,1},{2,6},{6,2},{3,7},{7,3},{8,12},{12,8},{9,1... | collective-permute-start | bytes 786440 | tf_op jit(solution)/shard_map/ppermute | solution.py:222
  173.0 7.8 %collective-permute-start.12 = (bf16[256,512]{1,0:T(8,128)(2,1)}, bf16[256,512]{1,0:T(8,128)(2,1)S(1)}, u32[]{:S(2)}, u32[]{:S(2)}) collective-permute-start(bf16[256,512]{1,0:T(8,128)(2,1)} %collective-permute-done.8.refs_3_), channel_id=1, source_target_pairs={{0,4},{4,0},{1,5},{5,1},{2,6},{6,2},{3,7},{7,3},{8,12},{12,8},{9,1... | collective-permute-start | bytes 786440 | tf_op jit(solution)/shard_map/ppermute | solution.py:222
  (3 other events, 5.9 us)

commit v3 on v2

v3 whole, which is shorter than its diff:
```python
import functools

import jax
import jax.numpy as jnp
from jax import lax
from jax.experimental import pallas as pl
from jax.experimental.pallas import tpu as pltpu
from jax.sharding import Mesh, PartitionSpec as P

BF = jnp.bfloat16
F32 = jnp.float32
CUTS = (0, 512, 2048)
PACK_VMEM = 59 * 1024 * 1024
UP_VMEM = 57 * 1024 * 1024


def weight_route():
    rounds = []
    for p in range(4):
        pairs = []
        for c in range(2):
            for y in range(4):
                bits = y ^ p
                h, k = bits >> 1, bits & 1
                pairs.append((c * 4 + y, h * 4 + 2 * c + k))
        rounds.append(pairs)
    return rounds


def pack_kernel(slots, ids_ref, table_ref, tok_ref, packed_ref, place_ref):
    i = pl.program_id(0)
    pairs, _, width = packed_ref.shape
    block = 2 * pairs
    tok = ids_ref.shape[1]

    @pl.when(i == 0)
    def _():
        rows, lanes = table_ref.shape
        experts = pl.num_programs(0) * block // slots
        ids = ids_ref[...]
        low = lax.rem(ids, lanes)
        high = lax.div(ids, lanes)
        low_hot = (lax.broadcasted_iota(jnp.int32, (lanes, tok), 0) == low).astype(F32).astype(BF)
        picked = jnp.dot(table_ref[...].astype(F32).astype(BF), low_hot, preferred_element_type=F32)
        high_hot = lax.broadcasted_iota(jnp.int32, (rows, tok), 0) == high
        chosen = jnp.sum(jnp.where(high_hot, picked, 0.0), axis=0, keepdims=True)
        hot = lax.broadcasted_iota(jnp.int32, (experts, tok), 0).astype(F32) == chosen
        before = (
            lax.broadcasted_iota(jnp.int32, (tok, tok), 0) < lax.broadcasted_iota(jnp.int32, (tok, tok), 1)
        ).astype(F32).astype(BF)
        earlier = jnp.dot(hot.astype(F32).astype(BF), before, preferred_element_type=F32)
        rank = jnp.sum(jnp.where(hot, earlier, 0.0), axis=0, keepdims=True)
        place_ref[...] = jnp.where(rank < slots, chosen * slots + rank, -1.0).astype(jnp.int32)

    at = lax.broadcasted_iota(jnp.int32, (block, tok), 0) + i * block
    onehot = (at == place_ref[...]).astype(F32).astype(BF)
    out = jnp.dot(onehot, tok_ref[...], preferred_element_type=F32).astype(BF)
    packed_ref[...] = out.reshape(pairs, 2, width)


def pack(token_ids, table, tokens, experts, slots):
    tok, width = tokens.shape
    block = 64
    pairs = experts * slots // 2
    return pl.pallas_call(
        functools.partial(pack_kernel, slots),
        grid=(pairs // block,),
        in_specs=[pl.BlockSpec(memory_space=pltpu.VMEM)] * 3,
        out_specs=(
            pl.BlockSpec((block, 2, width), lambda i: (i, 0, 0)),
            pl.BlockSpec((1, tok), lambda i: (0, 0)),
        ),
        out_shape=(
            jax.ShapeDtypeStruct((pairs, 2, width), BF),
            jax.ShapeDtypeStruct((1, tok), jnp.int32),
        ),
        cost_estimate=pl.CostEstimate(flops=4 * pairs * tok * width, bytes_accessed=6 * 1024 * 1024, transcendentals=0),
        compiler_params=pltpu.CompilerParams(vmem_limit_bytes=PACK_VMEM),
        name="pack",
    )(token_ids.reshape(1, tok), table.reshape(-1, 128), tokens)


def flatten_rows(src_ref, dst_ref):
    pairs, _, width = src_ref.shape
    block = 16

    def step(i, _):
        part = src_ref[pl.ds(pl.multiple_of(i * block, block), block)]
        dst_ref[pl.ds(pl.multiple_of(i * 2 * block, 2 * block), 2 * block), :] = part.reshape(2 * block, width)
        return 0

    lax.fori_loop(0, pairs // block, step, 0)


def up_kernel(x_ref, own_ref, other_ref, hidden_ref, rows_ref):
    j = pl.program_id(0)

    @pl.when(j == 0)
    def _():
        flatten_rows(x_ref, rows_ref)

    def run(w_ref):
        out = jnp.dot(rows_ref[...], w_ref[...], preferred_element_type=F32)
        hidden_ref[...] = jnp.maximum(out, 0.0).astype(BF)

    half = pl.num_programs(0) // 2

    @pl.when(j < half)
    def _():
        run(own_ref)

    @pl.when(j >= half)
    def _():
        run(other_ref)


def up(arrived, own, other):
    pairs, _, width = arrived.shape
    units = own.shape[1]
    block = 256
    half = units // block
    return pl.pallas_call(
        up_kernel,
        grid=(2 * half,),
        in_specs=[
            pl.BlockSpec(memory_space=pltpu.VMEM),
            pl.BlockSpec((width, block), lambda j: (0, jnp.minimum(j, half - 1))),
            pl.BlockSpec((width, block), lambda j: (0, jnp.maximum(j - half, 0))),
        ],
        out_specs=pl.BlockSpec((2 * pairs, block), lambda j: (0, j)),
        out_shape=jax.ShapeDtypeStruct((2 * pairs, 2 * units), BF),
        scratch_shapes=[pltpu.VMEM((2 * pairs, width), BF)],
        cost_estimate=pl.CostEstimate(flops=8 * pairs * units * width, bytes_accessed=16 * 1024 * 1024, transcendentals=0),
        compiler_params=pltpu.CompilerParams(vmem_limit_bytes=UP_VMEM),
        name="up",
    )(arrived, own, other)


def down_kernel(n, hidden_ref, *refs):
    pieces, out_ref, w_ref = refs[:n], refs[-2], refs[-1]
    depth = pieces[0].shape[0]
    for p in range(n):
        w_ref[p * depth:(p + 1) * depth, :] = pieces[p][...]
    out = jnp.dot(hidden_ref[...], w_ref[...], preferred_element_type=F32).astype(BF)
    out_ref[...] = out.reshape(out_ref.shape)


def down(hidden, pieces):
    rows, units = hidden.shape
    depth, cols = pieces[0].shape
    n = len(pieces)
    block = 512
    return pl.pallas_call(
        functools.partial(down_kernel, n),
        grid=(cols // block,),
        in_specs=[pl.BlockSpec(memory_space=pltpu.VMEM)] + [pl.BlockSpec((depth, block), lambda j: (0, j)) for _ in range(n)],
        out_specs=pl.BlockSpec((rows // 2, 2, block), lambda j: (0, 0, j)),
        out_shape=jax.ShapeDtypeStruct((rows // 2, 2, cols), BF),
        scratch_shapes=[pltpu.VMEM((units, block), BF)],
        cost_estimate=pl.CostEstimate(
            flops=2 * rows * units * cols, bytes_accessed=2 * rows * (units + cols) + 2 * units * cols, transcendentals=0
        ),
        compiler_params=pltpu.CompilerParams(vmem_limit_bytes=20 * 1024 * 1024),
        name="down",
    )(hidden, *pieces)


def hot_kernel(place_ref, hot_ref):
    at = lax.broadcasted_iota(jnp.int32, hot_ref.shape, 0)
    hot_ref[...] = (at == place_ref[...]).astype(F32).astype(BF)


def hots(place, rows):
    tok = place.shape[1]
    return pl.pallas_call(
        hot_kernel,
        out_shape=jax.ShapeDtypeStruct((rows, tok), BF),
        compiler_params=pltpu.CompilerParams(vmem_limit_bytes=8 * 1024 * 1024),
        name="hots",
    )(place)


def mix_kernel(hot_ref, back_ref, *refs):
    out_ref, rows_ref = refs[-2:]
    flatten_rows(back_ref, rows_ref)
    out_ref[...] = lax.dot_general(
        hot_ref[...], rows_ref[...], (((0,), (0,)), ((), ())), preferred_element_type=F32
    ).astype(BF)


def mix(hot, returned, start, width, base):
    pairs, _, cols = returned.shape
    tok = hot.shape[1]
    block = 512
    first = start // block
    specs = [
        pl.BlockSpec(memory_space=pltpu.VMEM),
        pl.BlockSpec((pairs, 2, block), lambda j: (0, 0, j)),
    ]
    args, aliases = [hot, returned], {}
    if base is not None:
        aliases = {2: 0}
        args.append(base)
        specs.append(pl.BlockSpec(memory_space=pl.ANY))
    return pl.pallas_call(
        mix_kernel,
        grid=(cols // block,),
        in_specs=specs,
        out_specs=pl.BlockSpec((tok, block), lambda j: (0, j + first)),
        out_shape=jax.ShapeDtypeStruct((tok, width), BF),
        scratch_shapes=[pltpu.VMEM((2 * pairs, block), BF)],
        input_output_aliases=aliases,
        cost_estimate=pl.CostEstimate(flops=4 * tok * pairs * cols, bytes_accessed=4 * pairs * cols + 2 * tok * cols, transcendentals=0),
        compiler_params=pltpu.CompilerParams(vmem_limit_bytes=16 * 1024 * 1024),
        name="mix",
    )(*args)


def on_device(tokens, token_ids, table, w_in, w_out):
    experts = lax.axis_size("g") * lax.axis_size("y")
    tok_rows, width = tokens.shape
    slots = 2 * tok_rows // experts
    half = w_out.shape[1] // 2
    y = lax.axis_index("y")
    route = weight_route()
    swap = [(0, 1), (1, 0)]
    own_in = []
    for p in range(4):
        h, k = (y ^ p) >> 1, (y ^ p) & 1
        block = lax.dynamic_slice(w_in, (k, 0, h * half), (1, width, half))[0]
        own_in.append(lax.ppermute(block, ("c", "y"), route[p]))
    other_in = [lax.ppermute(o, "c", swap) for o in own_in]
    own_in = jnp.concatenate(own_in, axis=1)
    other_in = jnp.concatenate(other_in, axis=1)
    pieces = []
    for low, high in zip(CUTS[:-1], CUTS[1:]):
        own = []
        for p in range(4):
            h, k = (y ^ p) >> 1, (y ^ p) & 1
            block = lax.dynamic_slice(w_out, (k, h * half, low), (1, half, high - low))[0]
            own.append(lax.ppermute(block, ("c", "y"), route[p]))
        pieces.append(own + [lax.ppermute(o, "c", swap) for o in own])

    packed, place = pack(token_ids, table, tokens, experts, slots)
    arrived = lax.all_to_all(packed, ("g", "y"), split_axis=0, concat_axis=0, tiled=True)
    hidden = up(arrived, own_in, other_in)
    returned = []
    for j in range(len(CUTS) - 1):
        result = down(hidden, pieces[j])
        returned.append(lax.all_to_all(result, ("g", "y"), split_axis=0, concat_axis=0, tiled=True))
    hot = hots(place, experts * slots)
    mixed = None
    for j, low in enumerate(CUTS[:-1]):
        mixed = mix(hot, returned[j], low, width, mixed)
    return mixed


def solution(mesh):
    groups, pair = mesh.shape["expert"], mesh.shape["pair"]
    fine = Mesh(mesh.devices.reshape(groups // 2, 2, pair), ("g", "c", "y"))
    rows = ("g", "c", "y")
    in_specs = (
        P(rows, None),
        P(rows),
        P(),
        P(("g", "c"), None, "y"),
        P(("g", "c"), "y", None),
    )
    return jax.shard_map(on_device, mesh=fine, in_specs=in_specs, out_specs=P(rows, None), check_vma=False)
```

time: 275 us -> 281 us (1.022); the launches traced: 273 us -> 276 us
  blocking collectives: 85.2 us -> 0 us
  waiting for transfers between devices: 95 us -> 143 us
  starting transfers between devices: 49.4 us -> 76.4 us
  Pallas kernels: 27.6 us -> 34 us
  other arithmetic: 0 us -> 4.58 us
    all_to_all x1 -> x0, blocking collectives: 85.2 us -> none  [on_device(): lax.all_to_all(result, ('g', 'y'), split_axis=0, concat_axis=0, tiled=True)]
    all_to_all x0 -> x2, waiting for transfers between devices: none -> 59.5 us  [on_device(): lax.all_to_all(result, ('g', 'y'), split_axis=0, concat_axis=0, tiled=True)]
    all_to_all x0 -> x2, starting transfers between devices: none -> 22.7 us  [on_device(): lax.all_to_all(result, ('g', 'y'), split_axis=0, concat_axis=0, tiled=True)]
    ppermute x8, waiting for transfers between devices: 31.8 us -> 10.7 us  [on_device(): own.append(lax.ppermute(block, ('c', 'y'), route[p]))]
    ppermute x4, waiting for transfers between devices: 63.2 us -> 68.3 us  [on_device(): own_in.append(lax.ppermute(block, ('c', 'y'), route[p]))]
    ppermute x8, waiting for transfers between devices: 0.02 us -> 4.88 us  [on_device(): pieces.append(own + [lax.ppermute(o, 'c', swap) for o in own])]
    pallas_call x2 -> x4, Pallas kernels: 7.33 us -> 12.1 us  [the longest x1 6.11 us: pack(): pl.pallas_call(functools.partial(pack_kernel, slots), grid=(pairs // bloc...]
    concatenate x0 -> x2, other arithmetic: none -> 4.58 us  [the longest x1 2.31 us: on_device(): other_in = jnp.concatenate(other_in, axis=1)]
  transfers between devices with their start and end apart: 22 -> 27, of which waited for: 9 -> 12; matrix products, arithmetic and copies ran while one was open for 1% -> 3% of each run, Pallas kernels for 8% -> 9%
where the time goes in v3:
time: 281 us; the launch traced here: 276 us
  waiting for transfers between devices  143 us (51%)
  starting transfers between devices  76.4 us (27%)
  Pallas kernels  34 us (12%)
  local copies, waits for them, and re-layouts  17.2 us (6%)
  other arithmetic  4.58 us (2%)
    ppermute x4, waiting for transfers between devices, on_device(): own_in.append(lax.ppermute(block, ('c', 'y'), route[p]))  68.3 us
    all_to_all x2, waiting for transfers between devices, on_device(): lax.all_to_all(result, ('g', 'y'), split_axis=0, concat_axis=0, tiled=True)  59.5 us
    all_to_all x2, starting transfers between devices, on_device(): lax.all_to_all(result, ('g', 'y'), split_axis=0, concat_axis=0, tiled=True)  22.7 us
    ppermute x8, starting transfers between devices, on_device(): own.append(lax.ppermute(block, ('c', 'y'), route[p]))  17.4 us
    all_to_all x1, starting transfers between devices, on_device(): lax.all_to_all(packed, ('g', 'y'), split_axis=0, concat_axis=0, tiled=True)  16.8 us
    pallas_call x1, Pallas kernels, up(): pl.pallas_call(up_kernel, grid=(2 * half,), in_specs=[pl.BlockSpec(memory...  13.1 us
    unnamed x40, local copies, waits for them, and re-layouts  11.6 us
    ppermute x8, waiting for transfers between devices, on_device(): own.append(lax.ppermute(block, ('c', 'y'), route[p]))  10.7 us
  transfers between devices with their start and end apart: 27, of which 12 were waited for; matrix products, arithmetic and copies ran while one was open for 3% of the time, Pallas kernels for 9%

profile of v3, /device:TPU:1, one launch (start us, length us, event | category | flops | bytes accessed | tf_op | source)
XLA Modules:
  0.0 275.9 jit_solution(18150896353222954463)
XLA Ops:
  1.2 6.1 %pack.1 = (bf16[384,2,2048]{2,1,0:T(2,128)(2,1)}, s32[1,384]{1,0:T(1,128)}) custom-call(s32[1,384]{1,0:T(1,128)} %reshape.6.ids_ref, s32[64,128]{1,0:T(8,128)} %bitcast.25, bf16[384,2048]{1,0:T(8,128)(2,1)} %tok_ref.1), custom_call_target="tpu_custom_call" | custom-call | flops 1207959552 | bytes 6291456 | tf_op jit(solution)/shard_map/pack/pallas_call | solution.py:65
  7.4 16.8 %all-to-all-start = ((bf16[384,2,2048]{2,1,0:T(2,128)(2,1)}), bf16[384,2,2048]{2,1,0:T(2,128)(2,1)}, u32[]{:S(2)}, u32[]{:S(2)}) async-start(bf16[384,2,2048]{2,1,0:T(2,128)(2,1)} %get-tuple-element.8), calls=%async_computation | async-start | bytes 6291456 | tf_op jit(solution)/shard_map/all_to_all | solution.py:245
  24.2 2.6 dynamic-slice_bitcast_fusion.3
  26.8 5.0 %collective-permute-start = (bf16[2048,256]{1,0:T(8,128)(2,1)S(1)}, bf16[2048,256]{1,0:T(8,128)(2,1)S(1)}, u32[]{:S(2)}, u32[]{:S(2)}) collective-permute-start(bf16[2048,256]{1,0:T(8,128)(2,1)S(1)} %get-tuple-element.17), channel_id=1, source_target_pairs={{0,0},{1,1},{2,4},{3,5},{4,2},{5,3},{6,6},{7,7},{8,8},{9,9},{10,12... | collective-permute-start | bytes 3145736 | tf_op jit(solution)/shard_map/ppermute | solution.py:231
  32.1 3.0 %collective-permute-start.3 = (bf16[2048,256]{1,0:T(8,128)(2,1)S(1)}, bf16[2048,256]{1,0:T(8,128)(2,1)S(1)}, u32[]{:S(2)}, u32[]{:S(2)}) collective-permute-start(bf16[2048,256]{1,0:T(8,128)(2,1)S(1)} %get-tuple-element.19), channel_id=1, source_target_pairs={{0,5},{1,4},{2,1},{3,0},{4,7},{5,6},{6,3},{7,2},{8,13},{9,12},{10,... | collective-permute-start | bytes 3145736 | tf_op jit(solution)/shard_map/ppermute | solution.py:231
  35.0 38.1 %collective-permute-done = bf16[2048,256]{1,0:T(8,128)(2,1)S(1)} collective-permute-done((bf16[2048,256]{1,0:T(8,128)(2,1)S(1)}, bf16[2048,256]{1,0:T(8,128)(2,1)S(1)}, u32[]{:S(2)}, u32[]{:S(2)}) %collective-permute-start) | collective-permute-done | bytes 1048608 | tf_op jit(solution)/shard_map/ppermute | solution.py:231
  73.2 2.8 %collective-permute-done.1 = bf16[2048,256]{1,0:T(8,128)(2,1)S(1)} collective-permute-done((bf16[2048,256]{1,0:T(8,128)(2,1)S(1)}, bf16[2048,256]{1,0:T(8,128)(2,1)S(1)}, u32[]{:S(2)}, u32[]{:S(2)}) %collective-permute-start.1) | collective-permute-done | bytes 1048608 | tf_op jit(solution)/shard_map/ppermute | solution.py:231
  76.0 27.4 %collective-permute-done.2 = bf16[2048,256]{1,0:T(8,128)(2,1)S(1)} collective-permute-done((bf16[2048,256]{1,0:T(8,128)(2,1)S(1)}, bf16[2048,256]{1,0:T(8,128)(2,1)S(1)}, u32[]{:S(2)}, u32[]{:S(2)}) %collective-permute-start.2) | collective-permute-done | bytes 1048608 | tf_op jit(solution)/shard_map/ppermute | solution.py:231
  103.4 3.3 %collective-permute-start.6 = (bf16[2048,256]{1,0:T(8,128)(2,1)S(1)}, bf16[2048,256]{1,0:T(8,128)(2,1)S(1)}, u32[]{:S(2)}, u32[]{:S(2)}) collective-permute-start(bf16[2048,256]{1,0:T(8,128)(2,1)S(1)} %collective-permute-done.2), channel_id=1, source_target_pairs={{0,4},{4,0},{1,5},{5,1},{2,6},{6,2},{3,7},{7,3},{8,12},{12,8},{9,1... | collective-permute-start | bytes 3145736 | tf_op jit(solution)/shard_map/ppermute | solution.py:232
  107.5 2.2 collective-permute-start.16
  109.6 7.2 %collective-permute-done.16.refs_0_ = bf16[256,512]{1,0:T(8,128)(2,1)S(1)} collective-permute-done((bf16[256,512]{1,0:T(8,128)(2,1)S(1)}, bf16[256,512]{1,0:T(8,128)(2,1)S(1)}, u32[]{:S(2)}, u32[]{:S(2)}) %collective-permute-start.16) | collective-permute-done | bytes 262176 | tf_op jit(solution)/shard_map/ppermute | solution.py:241
  116.8 2.9 %collective-permute-start.17 = (bf16[256,512]{1,0:T(8,128)(2,1)S(1)}, bf16[256,512]{1,0:T(8,128)(2,1)S(1)}, u32[]{:S(2)}, u32[]{:S(2)}) collective-permute-start(bf16[256,512]{1,0:T(8,128)(2,1)S(1)} %get-tuple-element.10), channel_id=1, source_target_pairs={{0,1},{1,0},{2,5},{3,4},{4,3},{5,2},{6,7},{7,6},{8,9},{9,8},{10,13... | collective-permute-start | bytes 786440 | tf_op jit(solution)/shard_map/ppermute | solution.py:241
  119.7 1.7 dynamic-slice_bitcast_fusion.4
  121.4 2.4 collective-permute-done.17.refs_1_
  123.8 2.3 pad_maximum_fusion.own_ref
  127.2 2.1 collective-permute-start.19
  129.2 7.2 %collective-permute-start.8 = (bf16[256,1536]{1,0:T(8,128)(2,1)}, bf16[256,1536]{1,0:T(8,128)(2,1)}, u32[]{:S(2)}, u32[]{:S(2)}) collective-permute-start(bf16[256,1536]{1,0:T(8,128)(2,1)} %get-tuple-element.16), channel_id=1, source_target_pairs={{0,0},{1,1},{2,4},{3,5},{4,2},{5,3},{6,6},{7,7},{8,8},{9,9},{10,12... | collective-permute-start | bytes 2359304 | tf_op jit(solution)/shard_map/ppermute | solution.py:241
  137.8 2.3 pad_maximum_fusion.1.other_ref
  140.3 2.8 collective-permute-start.10
  143.3 4.5 %collective-permute-start.23 = (bf16[256,512]{1,0:T(8,128)(2,1)S(1)}, bf16[256,512]{1,0:T(8,128)(2,1)S(1)}, u32[]{:S(2)}, u32[]{:S(2)}) collective-permute-start(bf16[256,512]{1,0:T(8,128)(2,1)S(1)} %collective-permute-done.19.refs_3_), channel_id=1, source_target_pairs={{0,4},{4,0},{1,5},{5,1},{2,6},{6,2},{3,7},{7,3},{8,12},{12,8},{9,1... | collective-permute-start | bytes 786440 | tf_op jit(solution)/shard_map/ppermute | solution.py:242
  147.9 13.1 %up.1.hidden_ref = bf16[768,2048]{1,0:T(8,128)(2,1)} custom-call(bf16[384,2,2048]{2,1,0:T(2,128)(2,1)} %all-to-all-done.x_ref, bf16[2048,1024]{1,0:T(8,128)(2,1)} %pad_maximum_fusion.own_ref, bf16[2048,1024]{1,0:T(8,128)(2,1)} %pad_maximum_fusion.1.other_ref), custom_call_target="tpu_custom_call" | custom-call | flops 6442450944 | bytes 16777216 | tf_op jit(solution)/shard_map/up/pallas_call | solution.py:122
  161.7 1.9 copy-done
  170.2 1.8 down.3
  172.9 15.5 %all-to-all-start.2 = ((bf16[384,2,512]{2,1,0:T(2,128)(2,1)}), bf16[384,2,512]{2,1,0:T(2,128)(2,1)}, u32[]{:S(2)}, u32[]{:S(2)}) async-start(bf16[384,2,512]{2,1,0:T(2,128)(2,1)} %copy-done.2), calls=%async_computation.2 | async-start | bytes 1572864 | tf_op jit(solution)/shard_map/all_to_all | solution.py:250
  189.8 1.5 collective-permute-done.12.refs_4_
  194.7 7.1 %down.2 = bf16[384,2,1536]{2,1,0:T(2,128)(2,1)S(1)} custom-call(bf16[768,2048]{1,0:T(8,128)(2,1)S(1)} %copy-done.1, bf16[256,1536]{1,0:T(8,128)(2,1)} %collective-permute-done.8.refs_0_, bf16[256,1536]{1,0:T(8,128)(2,1)} %collective-permute-done.9.refs_1_, bf16[256,1536]{1,0:T(8,128)(2,1)} %collective-permute-done.10.refs_2_, ...), custom_call_target="tpu_custom_call" | custom-call | flops 4831838208 | bytes 11796480 | tf_op jit(solution)/shard_map/down/pallas_call | solution.py:153
  201.8 1.4 copy-done.3
  203.2 8.7 %all-to-all-done.2.back_ref = bf16[384,2,512]{2,1,0:T(2,128)(2,1)} async-done(((bf16[384,2,512]{2,1,0:T(2,128)(2,1)}), bf16[384,2,512]{2,1,0:T(2,128)(2,1)}, u32[]{:S(2)}, u32[]{:S(2)}) %all-to-all-start.2) | async-done | bytes 786464 | tf_op jit(solution)/shard_map/all_to_all | solution.py:250
  212.0 7.2 %all-to-all-start.1 = ((bf16[384,2,1536]{2,1,0:T(2,128)(2,1)}), bf16[384,2,1536]{2,1,0:T(2,128)(2,1)S(1)}, u32[]{:S(2)}, u32[]{:S(2)}) async-start(bf16[384,2,1536]{2,1,0:T(2,128)(2,1)} %copy-done.3), calls=%async_computation.1 | async-start | bytes 4718592 | tf_op jit(solution)/shard_map/all_to_all | solution.py:250
  219.3 2.6 mix.2.refs_0_
  221.9 50.7 %all-to-all-done.1.back_ref = bf16[384,2,1536]{2,1,0:T(2,128)(2,1)S(1)} async-done(((bf16[384,2,1536]{2,1,0:T(2,128)(2,1)}), bf16[384,2,1536]{2,1,0:T(2,128)(2,1)S(1)}, u32[]{:S(2)}, u32[]{:S(2)}) %all-to-all-start.1) | async-done | bytes 2359328 | tf_op jit(solution)/shard_map/all_to_all | solution.py:250
  272.6 3.3 %mix.3 = bf16[384,2048]{1,0:T(8,128)(2,1)} custom-call(bf16[768,384]{1,0:T(8,128)(2,1)S(1)} %hots.1.hot_ref, bf16[384,2,1536]{2,1,0:T(2,128)(2,1)S(1)} %all-to-all-done.1.back_ref, bf16[384,2048]{1,0:T(8,128)(2,1)} %mix.2.refs_0_), custom_call_target="tpu_custom_call", output_to_operand_aliasing={{}: (2, {})} | custom-call | flops 905969664 | bytes 3538944 | tf_op jit(solution)/shard_map/mix/pallas_call | solution.py:205
  (75 shorter events, 18.3 us)
Async XLA Ops:
  7.4 140.5 %all-to-all-start = ((bf16[384,2,2048]{2,1,0:T(2,128)(2,1)}), bf16[384,2,2048]{2,1,0:T(2,128)(2,1)}, u32[]{:S(2)}, u32[]{:S(2)}) async-start(bf16[384,2,2048]{2,1,0:T(2,128)(2,1)} %get-tuple-element.8), calls=%async_computation | async-start | bytes 6291456 | tf_op jit(solution)/shard_map/all_to_all | solution.py:245
  24.2 83.2 %copy-start.19 = (bf16[2,512,2048]{2,1,0:T(8,128)(2,1)S(1)}, bf16[2,512,2048]{2,1,0:T(8,128)(2,1)}, u32[]{:S(2)}) copy-start(bf16[2,512,2048]{2,1,0:T(8,128)(2,1)} %param.9) | copy-start | bytes 12582916
  26.8 46.3 %collective-permute-start = (bf16[2048,256]{1,0:T(8,128)(2,1)S(1)}, bf16[2048,256]{1,0:T(8,128)(2,1)S(1)}, u32[]{:S(2)}, u32[]{:S(2)}) collective-permute-start(bf16[2048,256]{1,0:T(8,128)(2,1)S(1)} %get-tuple-element.17), channel_id=1, source_target_pairs={{0,0},{1,1},{2,4},{3,5},{4,2},{5,3},{6,6},{7,7},{8,8},{9,9},{10,12... | collective-permute-start | bytes 3145736 | tf_op jit(solution)/shard_map/ppermute | solution.py:231
  31.9 44.1 %collective-permute-start.1 = (bf16[2048,256]{1,0:T(8,128)(2,1)S(1)}, bf16[2048,256]{1,0:T(8,128)(2,1)S(1)}, u32[]{:S(2)}, u32[]{:S(2)}) collective-permute-start(bf16[2048,256]{1,0:T(8,128)(2,1)S(1)} %get-tuple-element.18), channel_id=1, source_target_pairs={{0,1},{1,0},{2,5},{3,4},{4,3},{5,2},{6,7},{7,6},{8,9},{9,8},{10,13... | collective-permute-start | bytes 3145736 | tf_op jit(solution)/shard_map/ppermute | solution.py:231
  32.0 71.4 %collective-permute-start.2 = (bf16[2048,256]{1,0:T(8,128)(2,1)S(1)}, bf16[2048,256]{1,0:T(8,128)(2,1)S(1)}, u32[]{:S(2)}, u32[]{:S(2)}) collective-permute-start(bf16[2048,256]{1,0:T(8,128)(2,1)S(1)} %get-tuple-element.20), channel_id=1, source_target_pairs={{0,4},{1,5},{2,0},{3,1},{4,6},{5,7},{6,2},{7,3},{8,12},{9,13},{10,... | collective-permute-start | bytes 3145736 | tf_op jit(solution)/shard_map/ppermute | solution.py:231
  32.1 74.6 %collective-permute-start.3 = (bf16[2048,256]{1,0:T(8,128)(2,1)S(1)}, bf16[2048,256]{1,0:T(8,128)(2,1)S(1)}, u32[]{:S(2)}, u32[]{:S(2)}) collective-permute-start(bf16[2048,256]{1,0:T(8,128)(2,1)S(1)} %get-tuple-element.19), channel_id=1, source_target_pairs={{0,5},{1,4},{2,1},{3,0},{4,7},{5,6},{6,3},{7,2},{8,13},{9,12},{10,... | collective-permute-start | bytes 3145736 | tf_op jit(solution)/shard_map/ppermute | solution.py:231
  73.2 56.1 %collective-permute-start.4 = (bf16[2048,256]{1,0:T(8,128)(2,1)S(1)}, bf16[2048,256]{1,0:T(8,128)(2,1)S(1)}, u32[]{:S(2)}, u32[]{:S(2)}) collective-permute-start(bf16[2048,256]{1,0:T(8,128)(2,1)S(1)} %collective-permute-done), channel_id=1, source_target_pairs={{0,4},{4,0},{1,5},{5,1},{2,6},{6,2},{3,7},{7,3},{8,12},{12,8},{9,1... | collective-permute-start | bytes 3145736 | tf_op jit(solution)/shard_map/ppermute | solution.py:232
  76.0 60.4 %collective-permute-start.5 = (bf16[2048,256]{1,0:T(8,128)(2,1)S(1)}, bf16[2048,256]{1,0:T(8,128)(2,1)S(1)}, u32[]{:S(2)}, u32[]{:S(2)}) collective-permute-start(bf16[2048,256]{1,0:T(8,128)(2,1)S(1)} %collective-permute-done.1), channel_id=1, source_target_pairs={{0,4},{4,0},{1,5},{5,1},{2,6},{6,2},{3,7},{7,3},{8,12},{12,8},{9,1... | collective-permute-start | bytes 3145736 | tf_op jit(solution)/shard_map/ppermute | solution.py:232
  103.4 34.0 %collective-permute-start.6 = (bf16[2048,256]{1,0:T(8,128)(2,1)S(1)}, bf16[2048,256]{1,0:T(8,128)(2,1)S(1)}, u32[]{:S(2)}, u32[]{:S(2)}) collective-permute-start(bf16[2048,256]{1,0:T(8,128)(2,1)S(1)} %collective-permute-done.2), channel_id=1, source_target_pairs={{0,4},{4,0},{1,5},{5,1},{2,6},{6,2},{3,7},{7,3},{8,12},{12,8},{9,1... | collective-permute-start | bytes 3145736 | tf_op jit(solution)/shard_map/ppermute | solution.py:232
  106.7 30.7 %collective-permute-start.7 = (bf16[2048,256]{1,0:T(8,128)(2,1)S(1)}, bf16[2048,256]{1,0:T(8,128)(2,1)S(1)}, u32[]{:S(2)}, u32[]{:S(2)}) collective-permute-start(bf16[2048,256]{1,0:T(8,128)(2,1)S(1)} %collective-permute-done.3), channel_id=1, source_target_pairs={{0,4},{4,0},{1,5},{5,1},{2,6},{6,2},{3,7},{7,3},{8,12},{12,8},{9,1... | collective-permute-start | bytes 3145736 | tf_op jit(solution)/shard_map/ppermute | solution.py:232
  107.5 9.4 %collective-permute-start.16 = (bf16[256,512]{1,0:T(8,128)(2,1)S(1)}, bf16[256,512]{1,0:T(8,128)(2,1)S(1)}, u32[]{:S(2)}, u32[]{:S(2)}) collective-permute-start(bf16[256,512]{1,0:T(8,128)(2,1)S(1)} %get-tuple-element.11), channel_id=1, source_target_pairs={{0,0},{1,1},{2,4},{3,5},{4,2},{5,3},{6,6},{7,7},{8,8},{9,9},{10,12... | collective-permute-start | bytes 786440 | tf_op jit(solution)/shard_map/ppermute | solution.py:241
  116.8 7.0 %collective-permute-start.17 = (bf16[256,512]{1,0:T(8,128)(2,1)S(1)}, bf16[256,512]{1,0:T(8,128)(2,1)S(1)}, u32[]{:S(2)}, u32[]{:S(2)}) collective-permute-start(bf16[256,512]{1,0:T(8,128)(2,1)S(1)} %get-tuple-element.10), channel_id=1, source_target_pairs={{0,1},{1,0},{2,5},{3,4},{4,3},{5,2},{6,7},{7,6},{8,9},{9,8},{10,13... | collective-permute-start | bytes 786440 | tf_op jit(solution)/shard_map/ppermute | solution.py:241
  123.8 3.3 %collective-permute-start.18 = (bf16[256,512]{1,0:T(8,128)(2,1)S(1)}, bf16[256,512]{1,0:T(8,128)(2,1)S(1)}, u32[]{:S(2)}, u32[]{:S(2)}) collective-permute-start(bf16[256,512]{1,0:T(8,128)(2,1)S(1)} %get-tuple-element.12), channel_id=1, source_target_pairs={{0,4},{1,5},{2,0},{3,1},{4,6},{5,7},{6,2},{7,3},{8,12},{9,13},{10,... | collective-permute-start | bytes 786440 | tf_op jit(solution)/shard_map/ppermute | solution.py:241
  127.2 13.0 %collective-permute-start.19 = (bf16[256,512]{1,0:T(8,128)(2,1)S(1)}, bf16[256,512]{1,0:T(8,128)(2,1)S(1)}, u32[]{:S(2)}, u32[]{:S(2)}) collective-permute-start(bf16[256,512]{1,0:T(8,128)(2,1)S(1)} %get-tuple-element.9), channel_id=1, source_target_pairs={{0,5},{1,4},{2,1},{3,0},{4,7},{5,6},{6,3},{7,2},{8,13},{9,12},{10,... | collective-permute-start | bytes 786440 | tf_op jit(solution)/shard_map/ppermute | solution.py:241
  129.2 59.1 %collective-permute-start.8 = (bf16[256,1536]{1,0:T(8,128)(2,1)}, bf16[256,1536]{1,0:T(8,128)(2,1)}, u32[]{:S(2)}, u32[]{:S(2)}) collective-permute-start(bf16[256,1536]{1,0:T(8,128)(2,1)} %get-tuple-element.16), channel_id=1, source_target_pairs={{0,0},{1,1},{2,4},{3,5},{4,2},{5,3},{6,6},{7,7},{8,8},{9,9},{10,12... | collective-permute-start | bytes 2359304 | tf_op jit(solution)/shard_map/ppermute | solution.py:241
  136.4 3.9 %collective-permute-start.20 = (bf16[256,512]{1,0:T(8,128)(2,1)S(1)}, bf16[256,512]{1,0:T(8,128)(2,1)S(1)}, u32[]{:S(2)}, u32[]{:S(2)}) collective-permute-start(bf16[256,512]{1,0:T(8,128)(2,1)S(1)} %collective-permute-done.16.refs_0_), channel_id=1, source_target_pairs={{0,4},{4,0},{1,5},{5,1},{2,6},{6,2},{3,7},{7,3},{8,12},{12,8},{9,1... | collective-permute-start | bytes 786440 | tf_op jit(solution)/shard_map/ppermute | solution.py:242
  137.3 5.7 %collective-permute-start.21 = (bf16[256,512]{1,0:T(8,128)(2,1)S(1)}, bf16[256,512]{1,0:T(8,128)(2,1)S(1)}, u32[]{:S(2)}, u32[]{:S(2)}) collective-permute-start(bf16[256,512]{1,0:T(8,128)(2,1)S(1)} %collective-permute-done.17.refs_1_), channel_id=1, source_target_pairs={{0,4},{4,0},{1,5},{5,1},{2,6},{6,2},{3,7},{7,3},{8,12},{12,8},{9,1... | collective-permute-start | bytes 786440 | tf_op jit(solution)/shard_map/ppermute | solution.py:242
  137.4 5.9 %collective-permute-start.22 = (bf16[256,512]{1,0:T(8,128)(2,1)S(1)}, bf16[256,512]{1,0:T(8,128)(2,1)S(1)}, u32[]{:S(2)}, u32[]{:S(2)}) collective-permute-start(bf16[256,512]{1,0:T(8,128)(2,1)S(1)} %collective-permute-done.18.refs_2_), channel_id=1, source_target_pairs={{0,4},{4,0},{1,5},{5,1},{2,6},{6,2},{3,7},{7,3},{8,12},{12,8},{9,1... | collective-permute-start | bytes 786440 | tf_op jit(solution)/shard_map/ppermute | solution.py:242
  140.2 20.8 %copy-start.8 = (bf16[256,512]{1,0:T(8,128)(2,1)}, bf16[256,512]{1,0:T(8,128)(2,1)S(1)}, u32[]{:S(2)}) copy-start(bf16[256,512]{1,0:T(8,128)(2,1)S(1)} %collective-permute-done.19.refs_3_) | copy-start | bytes 786436
  140.2 49.0 %collective-permute-start.9 = (bf16[256,1536]{1,0:T(8,128)(2,1)}, bf16[256,1536]{1,0:T(8,128)(2,1)}, u32[]{:S(2)}, u32[]{:S(2)}) collective-permute-start(bf16[256,1536]{1,0:T(8,128)(2,1)} %get-tuple-element.15), channel_id=1, source_target_pairs={{0,1},{1,0},{2,5},{3,4},{4,3},{5,2},{6,7},{7,6},{8,9},{9,8},{10,13... | collective-permute-start | bytes 2359304 | tf_op jit(solution)/shard_map/ppermute | solution.py:241
  140.3 20.7 %copy-start.10 = (bf16[256,512]{1,0:T(8,128)(2,1)}, bf16[256,512]{1,0:T(8,128)(2,1)S(1)}, u32[]{:S(2)}) copy-start(bf16[256,512]{1,0:T(8,128)(2,1)S(1)} %collective-permute-done.20.refs_4_) | copy-start | bytes 786436
  140.3 49.0 %collective-permute-start.10 = (bf16[256,1536]{1,0:T(8,128)(2,1)}, bf16[256,1536]{1,0:T(8,128)(2,1)}, u32[]{:S(2)}, u32[]{:S(2)}) collective-permute-start(bf16[256,1536]{1,0:T(8,128)(2,1)} %get-tuple-element.14), channel_id=1, source_target_pairs={{0,4},{1,5},{2,0},{3,1},{4,6},{5,7},{6,2},{7,3},{8,12},{9,13},{10,... | collective-permute-start | bytes 2359304 | tf_op jit(solution)/shard_map/ppermute | solution.py:241
  143.1 17.9 %copy-start.12 = (bf16[256,512]{1,0:T(8,128)(2,1)}, bf16[256,512]{1,0:T(8,128)(2,1)S(1)}, u32[]{:S(2)}) copy-start(bf16[256,512]{1,0:T(8,128)(2,1)S(1)} %collective-permute-done.21.refs_5_) | copy-start | bytes 786436
  143.1 46.6 %collective-permute-start.11 = (bf16[256,1536]{1,0:T(8,128)(2,1)}, bf16[256,1536]{1,0:T(8,128)(2,1)}, u32[]{:S(2)}, u32[]{:S(2)}) collective-permute-start(bf16[256,1536]{1,0:T(8,128)(2,1)} %get-tuple-element.13), channel_id=1, source_target_pairs={{0,5},{1,4},{2,1},{3,0},{4,7},{5,6},{6,3},{7,2},{8,13},{9,12},{10,... | collective-permute-start | bytes 2359304 | tf_op jit(solution)/shard_map/ppermute | solution.py:241
  143.3 17.6 %collective-permute-start.23 = (bf16[256,512]{1,0:T(8,128)(2,1)S(1)}, bf16[256,512]{1,0:T(8,128)(2,1)S(1)}, u32[]{:S(2)}, u32[]{:S(2)}) collective-permute-start(bf16[256,512]{1,0:T(8,128)(2,1)S(1)} %collective-permute-done.19.refs_3_), channel_id=1, source_target_pairs={{0,4},{4,0},{1,5},{5,1},{2,6},{6,2},{3,7},{7,3},{8,12},{12,8},{9,1... | collective-permute-start | bytes 786440 | tf_op jit(solution)/shard_map/ppermute | solution.py:242
  170.2 24.4 %copy-start.1 = (bf16[768,2048]{1,0:T(8,128)(2,1)S(1)}, bf16[768,2048]{1,0:T(8,128)(2,1)}, u32[]{:S(2)}) copy-start(bf16[768,2048]{1,0:T(8,128)(2,1)} %up.1.hidden_ref) | copy-start | bytes 9437188
  172.9 39.0 %all-to-all-start.2 = ((bf16[384,2,512]{2,1,0:T(2,128)(2,1)}), bf16[384,2,512]{2,1,0:T(2,128)(2,1)}, u32[]{:S(2)}, u32[]{:S(2)}) async-start(bf16[384,2,512]{2,1,0:T(2,128)(2,1)} %copy-done.2), calls=%async_computation.2 | async-start | bytes 1572864 | tf_op jit(solution)/shard_map/all_to_all | solution.py:250
  188.4 2.9 %collective-permute-start.12 = (bf16[256,1536]{1,0:T(8,128)(2,1)}, bf16[256,1536]{1,0:T(8,128)(2,1)S(1)}, u32[]{:S(2)}, u32[]{:S(2)}) collective-permute-start(bf16[256,1536]{1,0:T(8,128)(2,1)} %collective-permute-done.8.refs_0_), channel_id=1, source_target_pairs={{0,4},{4,0},{1,5},{5,1},{2,6},{6,2},{3,7},{7,3},{8,12},{12,8},{9,1... | collective-permute-start | bytes 2359304 | tf_op jit(solution)/shard_map/ppermute | solution.py:242
  189.2 3.2 %collective-permute-start.13 = (bf16[256,1536]{1,0:T(8,128)(2,1)}, bf16[256,1536]{1,0:T(8,128)(2,1)S(1)}, u32[]{:S(2)}, u32[]{:S(2)}) collective-permute-start(bf16[256,1536]{1,0:T(8,128)(2,1)} %collective-permute-done.9.refs_1_), channel_id=1, source_target_pairs={{0,4},{4,0},{1,5},{5,1},{2,6},{6,2},{3,7},{7,3},{8,12},{12,8},{9,1... | collective-permute-start | bytes 2359304 | tf_op jit(solution)/shard_map/ppermute | solution.py:242
  189.3 4.3 %collective-permute-start.14 = (bf16[256,1536]{1,0:T(8,128)(2,1)}, bf16[256,1536]{1,0:T(8,128)(2,1)S(1)}, u32[]{:S(2)}, u32[]{:S(2)}) collective-permute-start(bf16[256,1536]{1,0:T(8,128)(2,1)} %collective-permute-done.10.refs_2_), channel_id=1, source_target_pairs={{0,4},{4,0},{1,5},{5,1},{2,6},{6,2},{3,7},{7,3},{8,12},{12,8},{9,1... | collective-permute-start | bytes 2359304 | tf_op jit(solution)/shard_map/ppermute | solution.py:242
  189.7 5.0 %collective-permute-start.15 = (bf16[256,1536]{1,0:T(8,128)(2,1)}, bf16[256,1536]{1,0:T(8,128)(2,1)S(1)}, u32[]{:S(2)}, u32[]{:S(2)}) collective-permute-start(bf16[256,1536]{1,0:T(8,128)(2,1)} %collective-permute-done.11.refs_3_), channel_id=1, source_target_pairs={{0,4},{4,0},{1,5},{5,1},{2,6},{6,2},{3,7},{7,3},{8,12},{12,8},{9,1... | collective-permute-start | bytes 2359304 | tf_op jit(solution)/shard_map/ppermute | solution.py:242
  212.0 60.7 %all-to-all-start.1 = ((bf16[384,2,1536]{2,1,0:T(2,128)(2,1)}), bf16[384,2,1536]{2,1,0:T(2,128)(2,1)S(1)}, u32[]{:S(2)}, u32[]{:S(2)}) async-start(bf16[384,2,1536]{2,1,0:T(2,128)(2,1)} %copy-done.3), calls=%async_computation.1 | async-start | bytes 4718592 | tf_op jit(solution)/shard_map/all_to_all | solution.py:250
  (15 other events, 71.7 us)

commit v4 on v3

--- a/solution.py
+++ b/solution.py
@@ -10,8 +10,6 @@
 BF = jnp.bfloat16
 F32 = jnp.float32
 CUTS = (0, 512, 2048)
-PACK_VMEM = 59 * 1024 * 1024
-UP_VMEM = 57 * 1024 * 1024
 
 
 def weight_route():
@@ -28,54 +26,47 @@
 
 
 def pack_kernel(slots, ids_ref, table_ref, tok_ref, packed_ref, place_ref):
-    i = pl.program_id(0)
-    pairs, _, width = packed_ref.shape
-    block = 2 * pairs
+    rows, lanes = table_ref.shape
     tok = ids_ref.shape[1]
-
-    @pl.when(i == 0)
-    def _():
-        rows, lanes = table_ref.shape
-        experts = pl.num_programs(0) * block // slots
-        ids = ids_ref[...]
-        low = lax.rem(ids, lanes)
-        high = lax.div(ids, lanes)
-        low_hot = (lax.broadcasted_iota(jnp.int32, (lanes, tok), 0) == low).astype(F32).astype(BF)
-        picked = jnp.dot(table_ref[...].astype(F32).astype(BF), low_hot, preferred_element_type=F32)
-        high_hot = lax.broadcasted_iota(jnp.int32, (rows, tok), 0) == high
-        chosen = jnp.sum(jnp.where(high_hot, picked, 0.0), axis=0, keepdims=True)
-        hot = lax.broadcasted_iota(jnp.int32, (experts, tok), 0).astype(F32) == chosen
-        before = (
-            lax.broadcasted_iota(jnp.int32, (tok, tok), 0) < lax.broadcasted_iota(jnp.int32, (tok, tok), 1)
-        ).astype(F32).astype(BF)
-        earlier = jnp.dot(hot.astype(F32).astype(BF), before, preferred_element_type=F32)
-        rank = jnp.sum(jnp.where(hot, earlier, 0.0), axis=0, keepdims=True)
-        place_ref[...] = jnp.where(rank < slots, chosen * slots + rank, -1.0).astype(jnp.int32)
-
-    at = lax.broadcasted_iota(jnp.int32, (block, tok), 0) + i * block
-    onehot = (at == place_ref[...]).astype(F32).astype(BF)
-    out = jnp.dot(onehot, tok_ref[...], preferred_element_type=F32).astype(BF)
-    packed_ref[...] = out.reshape(pairs, 2, width)
+    pairs = packed_ref.shape[0]
+    experts = 2 * pairs // slots
+    ids = ids_ref[...]
+    low = lax.rem(ids, lanes)
+    high = lax.div(ids, lanes)
+    low_hot = (lax.broadcasted_iota(jnp.int32, (lanes, tok), 0) == low).astype(F32).astype(BF)
+    picked = jnp.dot(table_ref[...].astype(F32).astype(BF), low_hot, preferred_element_type=F32)
+    high_hot = lax.broadcasted_iota(jnp.int32, (rows, tok), 0) == high
+    chosen = jnp.sum(jnp.where(high_hot, picked, 0.0), axis=0, keepdims=True)
+    hot = lax.broadcasted_iota(jnp.int32, (experts, tok), 0).astype(F32) == chosen
+    before = (
+        lax.broadcasted_iota(jnp.int32, (tok, tok), 0) < lax.broadcasted_iota(jnp.int32, (tok, tok), 1)
+    ).astype(F32).astype(BF)
+    earlier = jnp.dot(hot.astype(F32).astype(BF), before, preferred_element_type=F32)
+    rank = jnp.sum(jnp.where(hot, earlier, 0.0), axis=0, keepdims=True)
+    place = jnp.where(rank < slots, chosen * slots + rank, -1.0).astype(jnp.int32)
+    place_ref[...] = place
+    block = 128
+
+    def step(i, _):
+        at = lax.broadcasted_iota(jnp.int32, (block, tok), 0) + i * block
+        onehot = (at == place).astype(F32).astype(BF)
+        out = jnp.dot(onehot, tok_ref[...], preferred_element_type=F32).astype(BF)
+        packed_ref[pl.ds(pl.multiple_of(i * (block // 2), block // 2), block // 2)] = out.reshape(block // 2, 2, out.shape[1])
+        return 0
+
+    lax.fori_loop(0, 2 * pairs // block, step, 0)
 
 
 def pack(token_ids, table, tokens, experts, slots):
     tok, width = tokens.shape
-    block = 64
-    pairs = experts * slots // 2
     return pl.pallas_call(
         functools.partial(pack_kernel, slots),
-        grid=(pairs // block,),
-        in_specs=[pl.BlockSpec(memory_space=pltpu.VMEM)] * 3,
-        out_specs=(
-            pl.BlockSpec((block, 2, width), lambda i: (i, 0, 0)),
-            pl.BlockSpec((1, tok), lambda i: (0, 0)),
-        ),
         out_shape=(
-            jax.ShapeDtypeStruct((pairs, 2, width), BF),
+            jax.ShapeDtypeStruct((experts * slots // 2, 2, width), BF),
             jax.ShapeDtypeStruct((1, tok), jnp.int32),
         ),
-        cost_estimate=pl.CostEstimate(flops=4 * pairs * tok * width, bytes_accessed=6 * 1024 * 1024, transcendentals=0),
-        compiler_params=pltpu.CompilerParams(vmem_limit_bytes=PACK_VMEM),
+        cost_estimate=pl.CostEstimate(flops=2 * experts * slots * tok * width, bytes_accessed=6 * 1024 * 1024, transcendentals=0),
+        compiler_params=pltpu.CompilerParams(vmem_limit_bytes=12 * 1024 * 1024),
         name="pack",
     )(token_ids.reshape(1, tok), table.reshape(-1, 128), tokens)
 
@@ -92,48 +83,38 @@
     lax.fori_loop(0, pairs // block, step, 0)
 
 
-def up_kernel(x_ref, own_ref, other_ref, hidden_ref, rows_ref):
-    j = pl.program_id(0)
-
-    @pl.when(j == 0)
-    def _():
-        flatten_rows(x_ref, rows_ref)
-
-    def run(w_ref):
-        out = jnp.dot(rows_ref[...], w_ref[...], preferred_element_type=F32)
-        hidden_ref[...] = jnp.maximum(out, 0.0).astype(BF)
-
-    half = pl.num_programs(0) // 2
-
-    @pl.when(j < half)
-    def _():
-        run(own_ref)
-
-    @pl.when(j >= half)
-    def _():
-        run(other_ref)
-
-
-def up(arrived, own, other):
+def up_kernel(n, x_ref, *refs):
+    pieces = refs[:n]
+    hidden_ref, rows_ref, w_ref, sems = refs[n:]
+    copies = [pltpu.make_async_copy(pieces[p], w_ref.at[p], sems.at[p]) for p in range(n)]
+    for copy in copies:
+        copy.start()
+    flatten_rows(x_ref, rows_ref)
+    units = w_ref.shape[2]
+    for p in range(n):
+        copies[p].wait()
+        out = jnp.dot(rows_ref[...], w_ref[p], preferred_element_type=F32)
+        hidden_ref[:, p * units:(p + 1) * units] = jnp.maximum(out, 0.0).astype(BF)
+
+
+def up(arrived, pieces):
     pairs, _, width = arrived.shape
-    units = own.shape[1]
-    block = 256
-    half = units // block
-    return pl.pallas_call(
-        up_kernel,
-        grid=(2 * half,),
-        in_specs=[
-            pl.BlockSpec(memory_space=pltpu.VMEM),
-            pl.BlockSpec((width, block), lambda j: (0, jnp.minimum(j, half - 1))),
-            pl.BlockSpec((width, block), lambda j: (0, jnp.maximum(j - half, 0))),
+    n = len(pieces)
+    units = pieces[0].shape[1]
+    return pl.pallas_call(
+        functools.partial(up_kernel, n),
+        in_specs=[pl.BlockSpec(memory_space=pltpu.VMEM)] + [pl.BlockSpec(memory_space=pltpu.HBM)] * n,
+        out_specs=pl.BlockSpec(memory_space=pltpu.VMEM),
+        out_shape=jax.ShapeDtypeStruct((2 * pairs, n * units), BF),
+        scratch_shapes=[
+            pltpu.VMEM((2 * pairs, width), BF),
+            pltpu.VMEM((n, width, units), BF),
+            pltpu.SemaphoreType.DMA((n,)),
         ],
-        out_specs=pl.BlockSpec((2 * pairs, block), lambda j: (0, j)),
-        out_shape=jax.ShapeDtypeStruct((2 * pairs, 2 * units), BF),
-        scratch_shapes=[pltpu.VMEM((2 * pairs, width), BF)],
-        cost_estimate=pl.CostEstimate(flops=8 * pairs * units * width, bytes_accessed=16 * 1024 * 1024, transcendentals=0),
-        compiler_params=pltpu.CompilerParams(vmem_limit_bytes=UP_VMEM),
+        cost_estimate=pl.CostEstimate(flops=4 * pairs * n * units * width, bytes_accessed=16 * 1024 * 1024, transcendentals=0),
+        compiler_params=pltpu.CompilerParams(vmem_limit_bytes=32 * 1024 * 1024),
         name="up",
-    )(arrived, own, other)
+    )(arrived, *pieces)
 
 
 def down_kernel(n, hidden_ref, *refs):
@@ -224,14 +205,12 @@
     y = lax.axis_index("y")
     route = weight_route()
     swap = [(0, 1), (1, 0)]
-    own_in = []
+    own_in, other_in = [], []
     for p in range(4):
         h, k = (y ^ p) >> 1, (y ^ p) & 1
         block = lax.dynamic_slice(w_in, (k, 0, h * half), (1, width, half))[0]
         own_in.append(lax.ppermute(block, ("c", "y"), route[p]))
-    other_in = [lax.ppermute(o, "c", swap) for o in own_in]
-    own_in = jnp.concatenate(own_in, axis=1)
-    other_in = jnp.concatenate(other_in, axis=1)
+        other_in.append(lax.ppermute(own_in[p], "c", swap))
     pieces = []
     for low, high in zip(CUTS[:-1], CUTS[1:]):
         own = []
@@ -243,7 +222,7 @@
 
     packed, place = pack(token_ids, table, tokens, experts, slots)
     arrived = lax.all_to_all(packed, ("g", "y"), split_axis=0, concat_axis=0, tiled=True)
-    hidden = up(arrived, own_in, other_in)
+    hidden = up(arrived, own_in + other_in)
     returned = []
     for j in range(len(CUTS) - 1):
         result = down(hidden, pieces[j])

time: 281 us -> 290 us (1.032)
  local copies, waits for them, and re-layouts: 17.2 us -> 35.2 us
  starting transfers between devices: 76.4 us -> 65.6 us
  waiting for transfers between devices: 143 us -> 148 us
  other arithmetic: 4.58 us -> 0 us
    ppermute x8, waiting for transfers between devices: 10.7 us -> 84.5 us  [on_device(): own.append(lax.ppermute(block, ('c', 'y'), route[p]))]
    ppermute x4, waiting for transfers between devices: 68.3 us -> 0.01 us  [on_device(): own_in.append(lax.ppermute(block, ('c', 'y'), route[p]))]
    unnamed x40 -> x66, local copies, waits for them, and re-layouts: 11.6 us -> 29.9 us
    concatenate x2 -> x0, other arithmetic: 4.58 us -> none  [the longest x1 2.31 us: on_device(): other_in = jnp.concatenate(other_in, axis=1)]
    ppermute x8, starting transfers between devices: 7.35 us -> 3.83 us  [on_device(): pieces.append(own + [lax.ppermute(o, 'c', swap) for o in own])]
    all_to_all x2, starting transfers between devices: 22.7 us -> 19.2 us  [on_device(): lax.all_to_all(result, ('g', 'y'), split_axis=0, concat_axis=0, tiled=True)]
    ppermute x4, starting transfers between devices: 3.97 us -> 1.02 us  [on_device(): other_in.append(lax.ppermute(own_in[p], 'c', swap))]
  transfers between devices with their start and end apart: 27 -> 27, of which waited for: 12 -> 12; matrix products, arithmetic and copies ran while one was open for 3% -> 2% of each run, Pallas kernels for 9% -> 10%
where the time goes in v4:
time: 290 us; the launch traced here: 284 us
  waiting for transfers between devices  148 us (51%)
  starting transfers between devices  65.6 us (23%)
  local copies, waits for them, and re-layouts  35.2 us (12%)
  Pallas kernels  35.2 us (12%)
    ppermute x8, waiting for transfers between devices, on_device(): own.append(lax.ppermute(block, ('c', 'y'), route[p]))  84.5 us
    all_to_all x2, waiting for transfers between devices, on_device(): lax.all_to_all(result, ('g', 'y'), split_axis=0, concat_axis=0, tiled=True)  57.3 us
    unnamed x66, local copies, waits for them, and re-layouts  29.9 us
    all_to_all x2, starting transfers between devices, on_device(): lax.all_to_all(result, ('g', 'y'), split_axis=0, concat_axis=0, tiled=True)  19.2 us
    ppermute x8, starting transfers between devices, on_device(): own.append(lax.ppermute(block, ('c', 'y'), route[p]))  17 us
    all_to_all x1, starting transfers between devices, on_device(): lax.all_to_all(packed, ('g', 'y'), split_axis=0, concat_axis=0, tiled=True)  16.3 us
    pallas_call x1, Pallas kernels, up(): pl.pallas_call(functools.partial(up_kernel, n), in_specs=[pl.BlockSpec(me...  15.3 us
    pallas_call x2, Pallas kernels, down(): pl.pallas_call(functools.partial(down_kernel, n), grid=(cols // block,),...  10.8 us
  transfers between devices with their start and end apart: 27, of which 12 were waited for; matrix products, arithmetic and copies ran while one was open for 2% of the time, Pallas kernels for 10%

profile of v4, /device:TPU:1, one launch (start us, length us, event | category | flops | bytes accessed | tf_op | source)
XLA Modules:
  0.0 284.5 jit_solution(14178184268998613372)
XLA Ops:
  0.7 1.4 copy-done.14
  2.9 3.1 %pack.1 = (bf16[384,2,2048]{2,1,0:T(2,128)(2,1)S(1)}, s32[1,384]{1,0:T(1,128)S(1)}) custom-call(s32[1,384]{1,0:T(1,128)S(1)} %reshape.6.ids_ref, s32[64,128]{1,0:T(8,128)S(1)} %bitcast.25, bf16[384,2048]{1,0:T(8,128)(2,1)S(1)} %copy-done.14), custom_call_target="tpu_custom_call" | custom-call | flops 1207959552 | bytes 6291456 | tf_op jit(solution)/shard_map/pack/pallas_call | solution.py:62
  5.9 1.6 copy-done
  7.6 16.3 %all-to-all-start = ((bf16[384,2,2048]{2,1,0:T(2,128)(2,1)}), bf16[384,2,2048]{2,1,0:T(2,128)(2,1)S(1)}, u32[]{:S(2)}, u32[]{:S(2)}) async-start(bf16[384,2,2048]{2,1,0:T(2,128)(2,1)} %copy-done), calls=%async_computation | async-start | bytes 6291456 | tf_op jit(solution)/shard_map/all_to_all | solution.py:224
  23.9 2.6 dynamic-slice_bitcast_fusion
  26.5 5.1 %collective-permute-start = (bf16[2048,256]{1,0:T(8,128)(2,1)S(1)}, bf16[2048,256]{1,0:T(8,128)(2,1)S(1)}, u32[]{:S(2)}, u32[]{:S(2)}) collective-permute-start(bf16[2048,256]{1,0:T(8,128)(2,1)S(1)} %get-tuple-element.19), channel_id=1, source_target_pairs={{0,0},{1,1},{2,4},{3,5},{4,2},{5,3},{6,6},{7,7},{8,8},{9,9},{10,12... | collective-permute-start | bytes 3145736 | tf_op jit(solution)/shard_map/ppermute | solution.py:212
  31.9 3.0 %collective-permute-start.3 = (bf16[2048,256]{1,0:T(8,128)(2,1)S(1)}, bf16[2048,256]{1,0:T(8,128)(2,1)S(1)}, u32[]{:S(2)}, u32[]{:S(2)}) collective-permute-start(bf16[2048,256]{1,0:T(8,128)(2,1)S(1)} %get-tuple-element.17), channel_id=1, source_target_pairs={{0,5},{1,4},{2,1},{3,0},{4,7},{5,6},{6,3},{7,2},{8,13},{9,12},{10,... | collective-permute-start | bytes 3145736 | tf_op jit(solution)/shard_map/ppermute | solution.py:212
  34.9 1.9 collective-permute-start.16
  36.9 74.8 %collective-permute-done.16.refs_0_ = bf16[256,512]{1,0:T(8,128)(2,1)S(1)} collective-permute-done((bf16[256,512]{1,0:T(8,128)(2,1)S(1)}, bf16[256,512]{1,0:T(8,128)(2,1)S(1)}, u32[]{:S(2)}, u32[]{:S(2)}) %collective-permute-start.16) | collective-permute-done | bytes 262176 | tf_op jit(solution)/shard_map/ppermute | solution.py:220
  111.7 2.2 collective-permute-start.17
  113.9 4.9 %collective-permute-done.17.refs_1_ = bf16[256,512]{1,0:T(8,128)(2,1)S(1)} collective-permute-done((bf16[256,512]{1,0:T(8,128)(2,1)S(1)}, bf16[256,512]{1,0:T(8,128)(2,1)S(1)}, u32[]{:S(2)}, u32[]{:S(2)}) %collective-permute-start.17) | collective-permute-done | bytes 262176 | tf_op jit(solution)/shard_map/ppermute | solution.py:220
  118.7 3.3 %collective-permute-done.18.refs_2_ = bf16[256,512]{1,0:T(8,128)(2,1)S(1)} collective-permute-done((bf16[256,512]{1,0:T(8,128)(2,1)S(1)}, bf16[256,512]{1,0:T(8,128)(2,1)S(1)}, u32[]{:S(2)}, u32[]{:S(2)}) %collective-permute-start.18) | collective-permute-done | bytes 262176 | tf_op jit(solution)/shard_map/ppermute | solution.py:220
  122.0 2.1 collective-permute-start.19
  129.1 1.4 collective-permute-done.19.refs_3_
  136.4 1.8 dynamic-slice_bitcast_fusion.4
  138.9 5.0 %collective-permute-start.8 = (bf16[256,1536]{1,0:T(8,128)(2,1)}, bf16[256,1536]{1,0:T(8,128)(2,1)}, u32[]{:S(2)}, u32[]{:S(2)}) collective-permute-start(bf16[256,1536]{1,0:T(8,128)(2,1)} %get-tuple-element.16), channel_id=1, source_target_pairs={{0,0},{1,1},{2,4},{3,5},{4,2},{5,3},{6,6},{7,7},{8,8},{9,9},{10,12... | collective-permute-start | bytes 2359304 | tf_op jit(solution)/shard_map/ppermute | solution.py:220
  147.0 4.5 %collective-permute-start.10 = (bf16[256,1536]{1,0:T(8,128)(2,1)}, bf16[256,1536]{1,0:T(8,128)(2,1)}, u32[]{:S(2)}, u32[]{:S(2)}) collective-permute-start(bf16[256,1536]{1,0:T(8,128)(2,1)} %get-tuple-element.14), channel_id=1, source_target_pairs={{0,4},{1,5},{2,0},{3,1},{4,6},{5,7},{6,2},{7,3},{8,12},{9,13},{10,... | collective-permute-start | bytes 2359304 | tf_op jit(solution)/shard_map/ppermute | solution.py:220
  154.7 1.2 copy-done.16
  155.9 1.2 copy-done.18
  164.5 15.3 %up.1.hidden_ref = bf16[768,2048]{1,0:T(8,128)(2,1)S(1)} custom-call(bf16[384,2,2048]{2,1,0:T(2,128)(2,1)S(1)} %all-to-all-done.x_ref, bf16[2048,256]{1,0:T(8,128)(2,1)S(1)} %copy-done.16, bf16[2048,256]{1,0:T(8,128)(2,1)S(1)} %copy-done.18, bf16[2048,256]{1,0:T(8,128)(2,1)S(1)} %copy-done.20, bf16[2048,256]{1,0:T(8,128)(2,1)S(1)} %copy-done.22, ...), custom_call_target="tpu_custom_call" | custom-call | flops 6442450944 | bytes 16777216 | tf_op jit(solution)/shard_map/up/pallas_call | solution.py:104
  179.8 3.7 %down.3 = bf16[384,2,512]{2,1,0:T(2,128)(2,1)} custom-call(bf16[768,2048]{1,0:T(8,128)(2,1)S(1)} %up.1.hidden_ref, bf16[256,512]{1,0:T(8,128)(2,1)S(1)} %collective-permute-done.16.refs_0_, bf16[256,512]{1,0:T(8,128)(2,1)S(1)} %copy-done.5, bf16[256,512]{1,0:T(8,128)(2,1)S(1)} %copy-done.7, bf16[256,512]{1,0:T(8,128)(2,1)} %collective-permute-done.19.refs_3_, ...), custom_call_target="tpu_custom_call" | custom-call | flops 1610612736 | bytes 6029312 | tf_op jit(solution)/shard_map/down/pallas_call | solution.py:134
  183.6 1.6 copy-done.1
  185.2 11.7 %all-to-all-start.2 = ((bf16[384,2,512]{2,1,0:T(2,128)(2,1)}), bf16[384,2,512]{2,1,0:T(2,128)(2,1)}, u32[]{:S(2)}, u32[]{:S(2)}) async-start(bf16[384,2,512]{2,1,0:T(2,128)(2,1)} %down.3), calls=%async_computation.2 | async-start | bytes 1572864 | tf_op jit(solution)/shard_map/all_to_all | solution.py:229
  198.4 1.5 collective-permute-done.12.refs_4_
  203.3 1.9 copy-done.2
  205.2 7.1 %down.2 = bf16[384,2,1536]{2,1,0:T(2,128)(2,1)S(1)} custom-call(bf16[768,2048]{1,0:T(8,128)(2,1)S(1)} %copy-done.2, bf16[256,1536]{1,0:T(8,128)(2,1)} %collective-permute-done.8.refs_0_, bf16[256,1536]{1,0:T(8,128)(2,1)} %collective-permute-done.9.refs_1_, bf16[256,1536]{1,0:T(8,128)(2,1)} %collective-permute-done.10.refs_2_, ...), custom_call_target="tpu_custom_call" | custom-call | flops 4831838208 | bytes 11796480 | tf_op jit(solution)/shard_map/down/pallas_call | solution.py:134
  212.3 1.4 copy-done.3
  213.7 6.5 %all-to-all-done.2.back_ref = bf16[384,2,512]{2,1,0:T(2,128)(2,1)} async-done(((bf16[384,2,512]{2,1,0:T(2,128)(2,1)}), bf16[384,2,512]{2,1,0:T(2,128)(2,1)}, u32[]{:S(2)}, u32[]{:S(2)}) %all-to-all-start.2) | async-done | bytes 786464 | tf_op jit(solution)/shard_map/all_to_all | solution.py:229
  220.3 7.5 %all-to-all-start.1 = ((bf16[384,2,1536]{2,1,0:T(2,128)(2,1)}), bf16[384,2,1536]{2,1,0:T(2,128)(2,1)S(1)}, u32[]{:S(2)}, u32[]{:S(2)}) async-start(bf16[384,2,1536]{2,1,0:T(2,128)(2,1)} %copy-done.3), calls=%async_computation.1 | async-start | bytes 4718592 | tf_op jit(solution)/shard_map/all_to_all | solution.py:229
  227.9 2.6 mix.2.refs_0_
  230.4 50.7 %all-to-all-done.1.back_ref = bf16[384,2,1536]{2,1,0:T(2,128)(2,1)S(1)} async-done(((bf16[384,2,1536]{2,1,0:T(2,128)(2,1)}), bf16[384,2,1536]{2,1,0:T(2,128)(2,1)S(1)}, u32[]{:S(2)}, u32[]{:S(2)}) %all-to-all-start.1) | async-done | bytes 2359328 | tf_op jit(solution)/shard_map/all_to_all | solution.py:229
  281.2 3.3 %mix.3 = bf16[384,2048]{1,0:T(8,128)(2,1)} custom-call(bf16[768,384]{1,0:T(8,128)(2,1)S(1)} %hots.1.hot_ref, bf16[384,2,1536]{2,1,0:T(2,128)(2,1)S(1)} %all-to-all-done.1.back_ref, bf16[384,2048]{1,0:T(8,128)(2,1)} %mix.2.refs_0_), custom_call_target="tpu_custom_call", output_to_operand_aliasing={{}: (2, {})} | custom-call | flops 905969664 | bytes 3538944 | tf_op jit(solution)/shard_map/mix/pallas_call | solution.py:186
  (99 shorter events, 31.9 us)
Async XLA Ops:
  7.6 147.1 %all-to-all-start = ((bf16[384,2,2048]{2,1,0:T(2,128)(2,1)}), bf16[384,2,2048]{2,1,0:T(2,128)(2,1)S(1)}, u32[]{:S(2)}, u32[]{:S(2)}) async-start(bf16[384,2,2048]{2,1,0:T(2,128)(2,1)} %copy-done), calls=%async_computation | async-start | bytes 6291456 | tf_op jit(solution)/shard_map/all_to_all | solution.py:224
  26.5 97.6 %collective-permute-start = (bf16[2048,256]{1,0:T(8,128)(2,1)S(1)}, bf16[2048,256]{1,0:T(8,128)(2,1)S(1)}, u32[]{:S(2)}, u32[]{:S(2)}) collective-permute-start(bf16[2048,256]{1,0:T(8,128)(2,1)S(1)} %get-tuple-element.19), channel_id=1, source_target_pairs={{0,0},{1,1},{2,4},{3,5},{4,2},{5,3},{6,6},{7,7},{8,8},{9,9},{10,12... | collective-permute-start | bytes 3145736 | tf_op jit(solution)/shard_map/ppermute | solution.py:212
  31.7 93.4 %collective-permute-start.1 = (bf16[2048,256]{1,0:T(8,128)(2,1)S(1)}, bf16[2048,256]{1,0:T(8,128)(2,1)S(1)}, u32[]{:S(2)}, u32[]{:S(2)}) collective-permute-start(bf16[2048,256]{1,0:T(8,128)(2,1)S(1)} %get-tuple-element.18), channel_id=1, source_target_pairs={{0,1},{1,0},{2,5},{3,4},{4,3},{5,2},{6,7},{7,6},{8,9},{9,8},{10,13... | collective-permute-start | bytes 3145736 | tf_op jit(solution)/shard_map/ppermute | solution.py:212
  31.8 94.8 %collective-permute-start.2 = (bf16[2048,256]{1,0:T(8,128)(2,1)S(1)}, bf16[2048,256]{1,0:T(8,128)(2,1)S(1)}, u32[]{:S(2)}, u32[]{:S(2)}) collective-permute-start(bf16[2048,256]{1,0:T(8,128)(2,1)S(1)} %get-tuple-element.20), channel_id=1, source_target_pairs={{0,4},{1,5},{2,0},{3,1},{4,6},{5,7},{6,2},{7,3},{8,12},{9,13},{10,... | collective-permute-start | bytes 3145736 | tf_op jit(solution)/shard_map/ppermute | solution.py:212
  31.9 95.7 %collective-permute-start.3 = (bf16[2048,256]{1,0:T(8,128)(2,1)S(1)}, bf16[2048,256]{1,0:T(8,128)(2,1)S(1)}, u32[]{:S(2)}, u32[]{:S(2)}) collective-permute-start(bf16[2048,256]{1,0:T(8,128)(2,1)S(1)} %get-tuple-element.17), channel_id=1, source_target_pairs={{0,5},{1,4},{2,1},{3,0},{4,7},{5,6},{6,3},{7,2},{8,13},{9,12},{10,... | collective-permute-start | bytes 3145736 | tf_op jit(solution)/shard_map/ppermute | solution.py:212
  34.9 76.8 %collective-permute-start.16 = (bf16[256,512]{1,0:T(8,128)(2,1)S(1)}, bf16[256,512]{1,0:T(8,128)(2,1)S(1)}, u32[]{:S(2)}, u32[]{:S(2)}) collective-permute-start(bf16[256,512]{1,0:T(8,128)(2,1)S(1)} %get-tuple-element.11), channel_id=1, source_target_pairs={{0,0},{1,1},{2,4},{3,5},{4,2},{5,3},{6,6},{7,7},{8,8},{9,9},{10,12... | collective-permute-start | bytes 786440 | tf_op jit(solution)/shard_map/ppermute | solution.py:220
  111.7 7.0 %collective-permute-start.17 = (bf16[256,512]{1,0:T(8,128)(2,1)S(1)}, bf16[256,512]{1,0:T(8,128)(2,1)S(1)}, u32[]{:S(2)}, u32[]{:S(2)}) collective-permute-start(bf16[256,512]{1,0:T(8,128)(2,1)S(1)} %get-tuple-element.10), channel_id=1, source_target_pairs={{0,1},{1,0},{2,5},{3,4},{4,3},{5,2},{6,7},{7,6},{8,9},{9,8},{10,13... | collective-permute-start | bytes 786440 | tf_op jit(solution)/shard_map/ppermute | solution.py:220
  118.7 3.3 %collective-permute-start.18 = (bf16[256,512]{1,0:T(8,128)(2,1)S(1)}, bf16[256,512]{1,0:T(8,128)(2,1)S(1)}, u32[]{:S(2)}, u32[]{:S(2)}) collective-permute-start(bf16[256,512]{1,0:T(8,128)(2,1)S(1)} %get-tuple-element.12), channel_id=1, source_target_pairs={{0,4},{1,5},{2,0},{3,1},{4,6},{5,7},{6,2},{7,3},{8,12},{9,13},{10,... | collective-permute-start | bytes 786440 | tf_op jit(solution)/shard_map/ppermute | solution.py:220
  122.0 8.5 %collective-permute-start.19 = (bf16[256,512]{1,0:T(8,128)(2,1)S(1)}, bf16[256,512]{1,0:T(8,128)(2,1)}, u32[]{:S(2)}, u32[]{:S(2)}) collective-permute-start(bf16[256,512]{1,0:T(8,128)(2,1)S(1)} %get-tuple-element.9), channel_id=1, source_target_pairs={{0,5},{1,4},{2,1},{3,0},{4,7},{5,6},{6,3},{7,2},{8,13},{9,12},{10,... | collective-permute-start | bytes 786440 | tf_op jit(solution)/shard_map/ppermute | solution.py:220
  124.1 19.8 %collective-permute-start.4 = (bf16[2048,256]{1,0:T(8,128)(2,1)S(1)}, bf16[2048,256]{1,0:T(8,128)(2,1)S(1)}, u32[]{:S(2)}, u32[]{:S(2)}) collective-permute-start(bf16[2048,256]{1,0:T(8,128)(2,1)S(1)} %collective-permute-done.refs_0_), channel_id=1, source_target_pairs={{0,4},{4,0},{1,5},{5,1},{2,6},{6,2},{3,7},{7,3},{8,12},{12,8},{9,1... | collective-permute-start | bytes 3145736 | tf_op jit(solution)/shard_map/ppermute | solution.py:213
  125.1 20.9 %collective-permute-start.5 = (bf16[2048,256]{1,0:T(8,128)(2,1)S(1)}, bf16[2048,256]{1,0:T(8,128)(2,1)S(1)}, u32[]{:S(2)}, u32[]{:S(2)}) collective-permute-start(bf16[2048,256]{1,0:T(8,128)(2,1)S(1)} %collective-permute-done.1.refs_1_), channel_id=1, source_target_pairs={{0,4},{4,0},{1,5},{5,1},{2,6},{6,2},{3,7},{7,3},{8,12},{12,8},{9,1... | collective-permute-start | bytes 3145736 | tf_op jit(solution)/shard_map/ppermute | solution.py:213
  126.6 24.9 %collective-permute-start.6 = (bf16[2048,256]{1,0:T(8,128)(2,1)S(1)}, bf16[2048,256]{1,0:T(8,128)(2,1)S(1)}, u32[]{:S(2)}, u32[]{:S(2)}) collective-permute-start(bf16[2048,256]{1,0:T(8,128)(2,1)S(1)} %collective-permute-done.2.refs_2_), channel_id=1, source_target_pairs={{0,4},{4,0},{1,5},{5,1},{2,6},{6,2},{3,7},{7,3},{8,12},{12,8},{9,1... | collective-permute-start | bytes 3145736 | tf_op jit(solution)/shard_map/ppermute | solution.py:213
  127.6 25.1 %collective-permute-start.7 = (bf16[2048,256]{1,0:T(8,128)(2,1)S(1)}, bf16[2048,256]{1,0:T(8,128)(2,1)S(1)}, u32[]{:S(2)}, u32[]{:S(2)}) collective-permute-start(bf16[2048,256]{1,0:T(8,128)(2,1)S(1)} %collective-permute-done.3.refs_3_), channel_id=1, source_target_pairs={{0,4},{4,0},{1,5},{5,1},{2,6},{6,2},{3,7},{7,3},{8,12},{12,8},{9,1... | collective-permute-start | bytes 3145736 | tf_op jit(solution)/shard_map/ppermute | solution.py:213
  130.5 1.8 collective-permute-start.20
  133.0 1.5 collective-permute-start.21
  135.3 2.9 %collective-permute-start.22 = (bf16[256,512]{1,0:T(8,128)(2,1)S(1)}, bf16[256,512]{1,0:T(8,128)(2,1)S(1)}, u32[]{:S(2)}, u32[]{:S(2)}) collective-permute-start(bf16[256,512]{1,0:T(8,128)(2,1)S(1)} %collective-permute-done.18.refs_2_), channel_id=1, source_target_pairs={{0,4},{4,0},{1,5},{5,1},{2,6},{6,2},{3,7},{7,3},{8,12},{12,8},{9,1... | collective-permute-start | bytes 786440 | tf_op jit(solution)/shard_map/ppermute | solution.py:221
  138.9 58.0 %collective-permute-start.8 = (bf16[256,1536]{1,0:T(8,128)(2,1)}, bf16[256,1536]{1,0:T(8,128)(2,1)}, u32[]{:S(2)}, u32[]{:S(2)}) collective-permute-start(bf16[256,1536]{1,0:T(8,128)(2,1)} %get-tuple-element.16), channel_id=1, source_target_pairs={{0,0},{1,1},{2,4},{3,5},{4,2},{5,3},{6,6},{7,7},{8,8},{9,9},{10,12... | collective-permute-start | bytes 2359304 | tf_op jit(solution)/shard_map/ppermute | solution.py:220
  144.9 52.9 %collective-permute-start.9 = (bf16[256,1536]{1,0:T(8,128)(2,1)}, bf16[256,1536]{1,0:T(8,128)(2,1)}, u32[]{:S(2)}, u32[]{:S(2)}) collective-permute-start(bf16[256,1536]{1,0:T(8,128)(2,1)} %get-tuple-element.15), channel_id=1, source_target_pairs={{0,1},{1,0},{2,5},{3,4},{4,3},{5,2},{6,7},{7,6},{8,9},{9,8},{10,13... | collective-permute-start | bytes 2359304 | tf_op jit(solution)/shard_map/ppermute | solution.py:220
  147.0 50.9 %collective-permute-start.10 = (bf16[256,1536]{1,0:T(8,128)(2,1)}, bf16[256,1536]{1,0:T(8,128)(2,1)}, u32[]{:S(2)}, u32[]{:S(2)}) collective-permute-start(bf16[256,1536]{1,0:T(8,128)(2,1)} %get-tuple-element.14), channel_id=1, source_target_pairs={{0,4},{1,5},{2,0},{3,1},{4,6},{5,7},{6,2},{7,3},{8,12},{9,13},{10,... | collective-permute-start | bytes 2359304 | tf_op jit(solution)/shard_map/ppermute | solution.py:220
  152.5 45.9 %collective-permute-start.11 = (bf16[256,1536]{1,0:T(8,128)(2,1)}, bf16[256,1536]{1,0:T(8,128)(2,1)}, u32[]{:S(2)}, u32[]{:S(2)}) collective-permute-start(bf16[256,1536]{1,0:T(8,128)(2,1)} %get-tuple-element.13), channel_id=1, source_target_pairs={{0,5},{1,4},{2,1},{3,0},{4,7},{5,6},{6,3},{7,2},{8,13},{9,12},{10,... | collective-permute-start | bytes 2359304 | tf_op jit(solution)/shard_map/ppermute | solution.py:220
  153.7 26.1 %collective-permute-start.23 = (bf16[256,512]{1,0:T(8,128)(2,1)}, bf16[256,512]{1,0:T(8,128)(2,1)}, u32[]{:S(2)}, u32[]{:S(2)}) collective-permute-start(bf16[256,512]{1,0:T(8,128)(2,1)} %collective-permute-done.19.refs_3_), channel_id=1, source_target_pairs={{0,4},{4,0},{1,5},{5,1},{2,6},{6,2},{3,7},{7,3},{8,12},{12,8},{9,1... | collective-permute-start | bytes 786440 | tf_op jit(solution)/shard_map/ppermute | solution.py:221
  164.5 15.3 %copy-start.5 = (bf16[256,512]{1,0:T(8,128)(2,1)S(1)}, bf16[256,512]{1,0:T(8,128)(2,1)}, u32[]{:S(2)}) copy-start(bf16[256,512]{1,0:T(8,128)(2,1)} %copy-done.4) | copy-start | bytes 786436
  164.5 15.3 %copy-start.7 = (bf16[256,512]{1,0:T(8,128)(2,1)S(1)}, bf16[256,512]{1,0:T(8,128)(2,1)}, u32[]{:S(2)}) copy-start(bf16[256,512]{1,0:T(8,128)(2,1)} %copy-done.6) | copy-start | bytes 786436
  164.5 15.3 %copy-start.9 = (bf16[256,512]{1,0:T(8,128)(2,1)S(1)}, bf16[256,512]{1,0:T(8,128)(2,1)}, u32[]{:S(2)}) copy-start(bf16[256,512]{1,0:T(8,128)(2,1)} %copy-done.8) | copy-start | bytes 786436
  164.5 15.3 %copy-start.11 = (bf16[256,512]{1,0:T(8,128)(2,1)S(1)}, bf16[256,512]{1,0:T(8,128)(2,1)}, u32[]{:S(2)}) copy-start(bf16[256,512]{1,0:T(8,128)(2,1)} %copy-done.10) | copy-start | bytes 786436
  164.5 15.3 %copy-start.13 = (bf16[256,512]{1,0:T(8,128)(2,1)S(1)}, bf16[256,512]{1,0:T(8,128)(2,1)}, u32[]{:S(2)}) copy-start(bf16[256,512]{1,0:T(8,128)(2,1)} %copy-done.12) | copy-start | bytes 786436
  185.2 35.1 %all-to-all-start.2 = ((bf16[384,2,512]{2,1,0:T(2,128)(2,1)}), bf16[384,2,512]{2,1,0:T(2,128)(2,1)}, u32[]{:S(2)}, u32[]{:S(2)}) async-start(bf16[384,2,512]{2,1,0:T(2,128)(2,1)} %down.3), calls=%async_computation.2 | async-start | bytes 1572864 | tf_op jit(solution)/shard_map/all_to_all | solution.py:229
  196.9 3.0 %collective-permute-start.12 = (bf16[256,1536]{1,0:T(8,128)(2,1)}, bf16[256,1536]{1,0:T(8,128)(2,1)S(1)}, u32[]{:S(2)}, u32[]{:S(2)}) collective-permute-start(bf16[256,1536]{1,0:T(8,128)(2,1)} %collective-permute-done.8.refs_0_), channel_id=1, source_target_pairs={{0,4},{4,0},{1,5},{5,1},{2,6},{6,2},{3,7},{7,3},{8,12},{12,8},{9,1... | collective-permute-start | bytes 2359304 | tf_op jit(solution)/shard_map/ppermute | solution.py:221
  197.8 3.2 %collective-permute-start.13 = (bf16[256,1536]{1,0:T(8,128)(2,1)}, bf16[256,1536]{1,0:T(8,128)(2,1)S(1)}, u32[]{:S(2)}, u32[]{:S(2)}) collective-permute-start(bf16[256,1536]{1,0:T(8,128)(2,1)} %collective-permute-done.9.refs_1_), channel_id=1, source_target_pairs={{0,4},{4,0},{1,5},{5,1},{2,6},{6,2},{3,7},{7,3},{8,12},{12,8},{9,1... | collective-permute-start | bytes 2359304 | tf_op jit(solution)/shard_map/ppermute | solution.py:221
  197.9 4.3 %collective-permute-start.14 = (bf16[256,1536]{1,0:T(8,128)(2,1)}, bf16[256,1536]{1,0:T(8,128)(2,1)S(1)}, u32[]{:S(2)}, u32[]{:S(2)}) collective-permute-start(bf16[256,1536]{1,0:T(8,128)(2,1)} %collective-permute-done.10.refs_2_), channel_id=1, source_target_pairs={{0,4},{4,0},{1,5},{5,1},{2,6},{6,2},{3,7},{7,3},{8,12},{12,8},{9,1... | collective-permute-start | bytes 2359304 | tf_op jit(solution)/shard_map/ppermute | solution.py:221
  198.3 5.0 %collective-permute-start.15 = (bf16[256,1536]{1,0:T(8,128)(2,1)}, bf16[256,1536]{1,0:T(8,128)(2,1)S(1)}, u32[]{:S(2)}, u32[]{:S(2)}) collective-permute-start(bf16[256,1536]{1,0:T(8,128)(2,1)} %collective-permute-done.11.refs_3_), channel_id=1, source_target_pairs={{0,4},{4,0},{1,5},{5,1},{2,6},{6,2},{3,7},{7,3},{8,12},{12,8},{9,1... | collective-permute-start | bytes 2359304 | tf_op jit(solution)/shard_map/ppermute | solution.py:221
  220.3 60.9 %all-to-all-start.1 = ((bf16[384,2,1536]{2,1,0:T(2,128)(2,1)}), bf16[384,2,1536]{2,1,0:T(2,128)(2,1)S(1)}, u32[]{:S(2)}, u32[]{:S(2)}) async-start(bf16[384,2,1536]{2,1,0:T(2,128)(2,1)} %copy-done.3), calls=%async_computation.1 | async-start | bytes 4718592 | tf_op jit(solution)/shard_map/all_to_all | solution.py:229
  (28 other events, 40.9 us)

commit v5 on v4

--- a/solution.py
+++ b/solution.py
@@ -10,6 +10,7 @@
 BF = jnp.bfloat16
 F32 = jnp.float32
 CUTS = (0, 512, 2048)
+UP_VMEM = 46 * 1024 * 1024
 
 
 def weight_route():
@@ -83,38 +84,48 @@
     lax.fori_loop(0, pairs // block, step, 0)
 
 
-def up_kernel(n, x_ref, *refs):
-    pieces = refs[:n]
-    hidden_ref, rows_ref, w_ref, sems = refs[n:]
-    copies = [pltpu.make_async_copy(pieces[p], w_ref.at[p], sems.at[p]) for p in range(n)]
-    for copy in copies:
-        copy.start()
-    flatten_rows(x_ref, rows_ref)
-    units = w_ref.shape[2]
-    for p in range(n):
-        copies[p].wait()
-        out = jnp.dot(rows_ref[...], w_ref[p], preferred_element_type=F32)
-        hidden_ref[:, p * units:(p + 1) * units] = jnp.maximum(out, 0.0).astype(BF)
-
-
-def up(arrived, pieces):
+def up_kernel(x_ref, own_ref, other_ref, hidden_ref, rows_ref):
+    j = pl.program_id(0)
+
+    @pl.when(j == 0)
+    def _():
+        flatten_rows(x_ref, rows_ref)
+
+    def run(w_ref):
+        out = jnp.dot(rows_ref[...], w_ref[...], preferred_element_type=F32)
+        hidden_ref[...] = jnp.maximum(out, 0.0).astype(BF)
+
+    half = pl.num_programs(0) // 2
+
+    @pl.when(j < half)
+    def _():
+        run(own_ref)
+
+    @pl.when(j >= half)
+    def _():
+        run(other_ref)
+
+
+def up(arrived, own, other):
     pairs, _, width = arrived.shape
-    n = len(pieces)
-    units = pieces[0].shape[1]
-    return pl.pallas_call(
-        functools.partial(up_kernel, n),
-        in_specs=[pl.BlockSpec(memory_space=pltpu.VMEM)] + [pl.BlockSpec(memory_space=pltpu.HBM)] * n,
-        out_specs=pl.BlockSpec(memory_space=pltpu.VMEM),
-        out_shape=jax.ShapeDtypeStruct((2 * pairs, n * units), BF),
-        scratch_shapes=[
-            pltpu.VMEM((2 * pairs, width), BF),
-            pltpu.VMEM((n, width, units), BF),
-            pltpu.SemaphoreType.DMA((n,)),
+    units = own.shape[1]
+    block = 256
+    half = units // block
+    return pl.pallas_call(
+        up_kernel,
+        grid=(2 * half,),
+        in_specs=[
+            pl.BlockSpec(memory_space=pltpu.VMEM),
+            pl.BlockSpec((width, block), lambda j: (0, jnp.minimum(j, half - 1))),
+            pl.BlockSpec((width, block), lambda j: (0, jnp.maximum(j - half, 0))),
         ],
-        cost_estimate=pl.CostEstimate(flops=4 * pairs * n * units * width, bytes_accessed=16 * 1024 * 1024, transcendentals=0),
-        compiler_params=pltpu.CompilerParams(vmem_limit_bytes=32 * 1024 * 1024),
+        out_specs=pl.BlockSpec((2 * pairs, block), lambda j: (0, j)),
+        out_shape=jax.ShapeDtypeStruct((2 * pairs, 2 * units), BF),
+        scratch_shapes=[pltpu.VMEM((2 * pairs, width), BF)],
+        cost_estimate=pl.CostEstimate(flops=8 * pairs * units * width, bytes_accessed=16 * 1024 * 1024, transcendentals=0),
+        compiler_params=pltpu.CompilerParams(vmem_limit_bytes=UP_VMEM),
         name="up",
-    )(arrived, *pieces)
+    )(arrived, own, other)
 
 
 def down_kernel(n, hidden_ref, *refs):
@@ -205,12 +216,14 @@
     y = lax.axis_index("y")
     route = weight_route()
     swap = [(0, 1), (1, 0)]
-    own_in, other_in = [], []
+    own_in = []
     for p in range(4):
         h, k = (y ^ p) >> 1, (y ^ p) & 1
         block = lax.dynamic_slice(w_in, (k, 0, h * half), (1, width, half))[0]
         own_in.append(lax.ppermute(block, ("c", "y"), route[p]))
-        other_in.append(lax.ppermute(own_in[p], "c", swap))
+    other_in = [lax.ppermute(o, "c", swap) for o in own_in]
+    own_in = jnp.concatenate(own_in, axis=1)
+    other_in = jnp.concatenate(other_in, axis=1)
     pieces = []
     for low, high in zip(CUTS[:-1], CUTS[1:]):
         own = []
@@ -222,7 +235,7 @@
 
     packed, place = pack(token_ids, table, tokens, experts, slots)
     arrived = lax.all_to_all(packed, ("g", "y"), split_axis=0, concat_axis=0, tiled=True)
-    hidden = up(arrived, own_in + other_in)
+    hidden = up(arrived, own_in, other_in)
     returned = []
     for j in range(len(CUTS) - 1):
         result = down(hidden, pieces[j])

time: 290 us -> 274 us (0.945)
  local copies, waits for them, and re-layouts: 35.2 us -> 16 us
  starting transfers between devices: 65.6 us -> 75.8 us
  waiting for transfers between devices: 148 us -> 141 us
  other arithmetic: 0 us -> 4.56 us
  Pallas kernels: 35.2 us -> 31 us
    ppermute x8, waiting for transfers between devices: 84.5 us -> 10.8 us  [on_device(): own.append(lax.ppermute(block, ('c', 'y'), route[p]))]
    ppermute x4, waiting for transfers between devices: 0.01 us -> 68.5 us  [on_device(): own_in.append(lax.ppermute(block, ('c', 'y'), route[p]))]
    unnamed x66 -> x34, local copies, waits for them, and re-layouts: 29.9 us -> 10.8 us
    concatenate x0 -> x2, other arithmetic: none -> 4.56 us  [the longest x1 2.31 us: on_device(): other_in = jnp.concatenate(other_in, axis=1)]
    pallas_call x1, Pallas kernels: 15.3 us -> 11.1 us  [up(): pl.pallas_call(up_kernel, grid=(2 * half,), in_specs=[pl.BlockSpec(memory...]
    ppermute x8, starting transfers between devices: 3.83 us -> 7.4 us  [on_device(): pieces.append(own + [lax.ppermute(o, 'c', swap) for o in own])]
    all_to_all x2, starting transfers between devices: 19.2 us -> 22.6 us  [on_device(): lax.all_to_all(result, ('g', 'y'), split_axis=0, concat_axis=0, tiled=True)]
    ppermute x4, starting transfers between devices: 1.02 us -> 3.98 us  [on_device(): other_in = [lax.ppermute(o, 'c', swap) for o in own_in]]
  transfers between devices with their start and end apart: 27 -> 27, of which waited for: 12 -> 12; matrix products, arithmetic and copies ran while one was open for 2% -> 3% of each run, Pallas kernels for 10% -> 9%
where the time goes in v5:
time: 274 us; the launch traced here: 269 us
  waiting for transfers between devices  141 us (51%)
  starting transfers between devices  75.8 us (28%)
  Pallas kernels  31 us (11%)
  local copies, waits for them, and re-layouts  16 us (6%)
  other arithmetic  4.56 us (2%)
    ppermute x4, waiting for transfers between devices, on_device(): own_in.append(lax.ppermute(block, ('c', 'y'), route[p]))  68.5 us
    all_to_all x2, waiting for transfers between devices, on_device(): lax.all_to_all(result, ('g', 'y'), split_axis=0, concat_axis=0, tiled=True)  57.3 us
    all_to_all x2, starting transfers between devices, on_device(): lax.all_to_all(result, ('g', 'y'), split_axis=0, concat_axis=0, tiled=True)  22.6 us
    ppermute x8, starting transfers between devices, on_device(): own.append(lax.ppermute(block, ('c', 'y'), route[p]))  17.2 us
    all_to_all x1, starting transfers between devices, on_device(): lax.all_to_all(packed, ('g', 'y'), split_axis=0, concat_axis=0, tiled=True)  16.3 us
    pallas_call x1, Pallas kernels, up(): pl.pallas_call(up_kernel, grid=(2 * half,), in_specs=[pl.BlockSpec(memory...  11.1 us
    pallas_call x2, Pallas kernels, down(): pl.pallas_call(functools.partial(down_kernel, n), grid=(cols // block,),...  10.9 us
    unnamed x34, local copies, waits for them, and re-layouts  10.8 us
  transfers between devices with their start and end apart: 27, of which 12 were waited for; matrix products, arithmetic and copies ran while one was open for 3% of the time, Pallas kernels for 9%

profile of v5, /device:TPU:1, one launch (start us, length us, event | category | flops | bytes accessed | tf_op | source)
XLA Modules:
  0.0 269.1 jit_solution(7254626269590666257)
XLA Ops:
  2.9 3.1 %pack.1 = (bf16[384,2,2048]{2,1,0:T(2,128)(2,1)S(1)}, s32[1,384]{1,0:T(1,128)S(1)}) custom-call(s32[1,384]{1,0:T(1,128)S(1)} %reshape.6.ids_ref, s32[64,128]{1,0:T(8,128)S(1)} %bitcast.25, bf16[384,2048]{1,0:T(8,128)(2,1)S(1)} %copy-done.14), custom_call_target="tpu_custom_call" | custom-call | flops 1207959552 | bytes 6291456 | tf_op jit(solution)/shard_map/pack/pallas_call | solution.py:63
  5.9 1.6 copy-done
  7.6 16.3 %all-to-all-start = ((bf16[384,2,2048]{2,1,0:T(2,128)(2,1)}), bf16[384,2,2048]{2,1,0:T(2,128)(2,1)S(1)}, u32[]{:S(2)}, u32[]{:S(2)}) async-start(bf16[384,2,2048]{2,1,0:T(2,128)(2,1)} %copy-done), calls=%async_computation | async-start | bytes 6291456 | tf_op jit(solution)/shard_map/all_to_all | solution.py:237
  23.9 2.6 dynamic-slice_bitcast_fusion.3
  26.5 5.1 %collective-permute-start = (bf16[2048,256]{1,0:T(8,128)(2,1)S(1)}, bf16[2048,256]{1,0:T(8,128)(2,1)S(1)}, u32[]{:S(2)}, u32[]{:S(2)}) collective-permute-start(bf16[2048,256]{1,0:T(8,128)(2,1)S(1)} %get-tuple-element.17), channel_id=1, source_target_pairs={{0,0},{1,1},{2,4},{3,5},{4,2},{5,3},{6,6},{7,7},{8,8},{9,9},{10,12... | collective-permute-start | bytes 3145736 | tf_op jit(solution)/shard_map/ppermute | solution.py:223
  31.9 3.0 %collective-permute-start.3 = (bf16[2048,256]{1,0:T(8,128)(2,1)S(1)}, bf16[2048,256]{1,0:T(8,128)(2,1)S(1)}, u32[]{:S(2)}, u32[]{:S(2)}) collective-permute-start(bf16[2048,256]{1,0:T(8,128)(2,1)S(1)} %get-tuple-element.19), channel_id=1, source_target_pairs={{0,5},{1,4},{2,1},{3,0},{4,7},{5,6},{6,3},{7,2},{8,13},{9,12},{10,... | collective-permute-start | bytes 3145736 | tf_op jit(solution)/shard_map/ppermute | solution.py:223
  34.8 38.3 %collective-permute-done = bf16[2048,256]{1,0:T(8,128)(2,1)S(1)} collective-permute-done((bf16[2048,256]{1,0:T(8,128)(2,1)S(1)}, bf16[2048,256]{1,0:T(8,128)(2,1)S(1)}, u32[]{:S(2)}, u32[]{:S(2)}) %collective-permute-start) | collective-permute-done | bytes 1048608 | tf_op jit(solution)/shard_map/ppermute | solution.py:223
  73.1 2.1 collective-permute-done.1
  75.2 28.2 %collective-permute-done.2 = bf16[2048,256]{1,0:T(8,128)(2,1)S(1)} collective-permute-done((bf16[2048,256]{1,0:T(8,128)(2,1)S(1)}, bf16[2048,256]{1,0:T(8,128)(2,1)S(1)}, u32[]{:S(2)}, u32[]{:S(2)}) %collective-permute-start.2) | collective-permute-done | bytes 1048608 | tf_op jit(solution)/shard_map/ppermute | solution.py:223
  103.3 3.5 %collective-permute-start.6 = (bf16[2048,256]{1,0:T(8,128)(2,1)S(1)}, bf16[2048,256]{1,0:T(8,128)(2,1)S(1)}, u32[]{:S(2)}, u32[]{:S(2)}) collective-permute-start(bf16[2048,256]{1,0:T(8,128)(2,1)S(1)} %collective-permute-done.2), channel_id=1, source_target_pairs={{0,4},{4,0},{1,5},{5,1},{2,6},{6,2},{3,7},{7,3},{8,12},{12,8},{9,1... | collective-permute-start | bytes 3145736 | tf_op jit(solution)/shard_map/ppermute | solution.py:224
  107.4 2.2 collective-permute-start.16
  109.6 7.2 %collective-permute-done.16.refs_0_ = bf16[256,512]{1,0:T(8,128)(2,1)S(1)} collective-permute-done((bf16[256,512]{1,0:T(8,128)(2,1)S(1)}, bf16[256,512]{1,0:T(8,128)(2,1)S(1)}, u32[]{:S(2)}, u32[]{:S(2)}) %collective-permute-start.16) | collective-permute-done | bytes 262176 | tf_op jit(solution)/shard_map/ppermute | solution.py:233
  116.8 2.8 %collective-permute-start.17 = (bf16[256,512]{1,0:T(8,128)(2,1)S(1)}, bf16[256,512]{1,0:T(8,128)(2,1)S(1)}, u32[]{:S(2)}, u32[]{:S(2)}) collective-permute-start(bf16[256,512]{1,0:T(8,128)(2,1)S(1)} %get-tuple-element.10), channel_id=1, source_target_pairs={{0,1},{1,0},{2,5},{3,4},{4,3},{5,2},{6,7},{7,6},{8,9},{9,8},{10,13... | collective-permute-start | bytes 786440 | tf_op jit(solution)/shard_map/ppermute | solution.py:233
  119.7 1.7 dynamic-slice_bitcast_fusion.4
  121.4 2.5 collective-permute-done.17.refs_1_
  123.9 2.2 pad_maximum_fusion.own_ref
  127.2 2.0 collective-permute-start.19
  129.2 7.1 %collective-permute-start.8 = (bf16[256,1536]{1,0:T(8,128)(2,1)}, bf16[256,1536]{1,0:T(8,128)(2,1)}, u32[]{:S(2)}, u32[]{:S(2)}) collective-permute-start(bf16[256,1536]{1,0:T(8,128)(2,1)} %get-tuple-element.16), channel_id=1, source_target_pairs={{0,0},{1,1},{2,4},{3,5},{4,2},{5,3},{6,6},{7,7},{8,8},{9,9},{10,12... | collective-permute-start | bytes 2359304 | tf_op jit(solution)/shard_map/ppermute | solution.py:233
  137.9 2.3 pad_maximum_fusion.1.other_ref
  140.9 2.6 collective-permute-start.10
  145.4 4.4 %collective-permute-start.23 = (bf16[256,512]{1,0:T(8,128)(2,1)}, bf16[256,512]{1,0:T(8,128)(2,1)}, u32[]{:S(2)}, u32[]{:S(2)}) collective-permute-start(bf16[256,512]{1,0:T(8,128)(2,1)} %collective-permute-done.19.refs_3_), channel_id=1, source_target_pairs={{0,4},{4,0},{1,5},{5,1},{2,6},{6,2},{3,7},{7,3},{8,12},{12,8},{9,1... | collective-permute-start | bytes 786440 | tf_op jit(solution)/shard_map/ppermute | solution.py:234
  149.8 11.1 %up.1.hidden_ref = bf16[768,2048]{1,0:T(8,128)(2,1)S(1)} custom-call(bf16[384,2,2048]{2,1,0:T(2,128)(2,1)S(1)} %all-to-all-done.x_ref, bf16[2048,1024]{1,0:T(8,128)(2,1)} %pad_maximum_fusion.own_ref, bf16[2048,1024]{1,0:T(8,128)(2,1)} %pad_maximum_fusion.1.other_ref), custom_call_target="tpu_custom_call" | custom-call | flops 6442450944 | bytes 16777216 | tf_op jit(solution)/shard_map/up/pallas_call | solution.py:114
  161.0 3.7 %down.3 = bf16[384,2,512]{2,1,0:T(2,128)(2,1)} custom-call(bf16[768,2048]{1,0:T(8,128)(2,1)S(1)} %up.1.hidden_ref, bf16[256,512]{1,0:T(8,128)(2,1)S(1)} %collective-permute-done.16.refs_0_, bf16[256,512]{1,0:T(8,128)(2,1)S(1)} %copy-done.5, bf16[256,512]{1,0:T(8,128)(2,1)S(1)} %copy-done.7, bf16[256,512]{1,0:T(8,128)(2,1)} %collective-permute-done.19.refs_3_, ...), custom_call_target="tpu_custom_call" | custom-call | flops 1610612736 | bytes 6029312 | tf_op jit(solution)/shard_map/down/pallas_call | solution.py:145
  164.7 1.6 copy-done.1
  166.4 15.2 %all-to-all-start.2 = ((bf16[384,2,512]{2,1,0:T(2,128)(2,1)}), bf16[384,2,512]{2,1,0:T(2,128)(2,1)}, u32[]{:S(2)}, u32[]{:S(2)}) async-start(bf16[384,2,512]{2,1,0:T(2,128)(2,1)} %down.3), calls=%async_computation.2 | async-start | bytes 1572864 | tf_op jit(solution)/shard_map/all_to_all | solution.py:242
  187.9 1.9 copy-done.2
  189.8 7.1 %down.2 = bf16[384,2,1536]{2,1,0:T(2,128)(2,1)S(1)} custom-call(bf16[768,2048]{1,0:T(8,128)(2,1)S(1)} %copy-done.2, bf16[256,1536]{1,0:T(8,128)(2,1)} %collective-permute-done.8.refs_0_, bf16[256,1536]{1,0:T(8,128)(2,1)} %collective-permute-done.9.refs_1_, bf16[256,1536]{1,0:T(8,128)(2,1)} %collective-permute-done.10.refs_2_, ...), custom_call_target="tpu_custom_call" | custom-call | flops 4831838208 | bytes 11796480 | tf_op jit(solution)/shard_map/down/pallas_call | solution.py:145
  198.4 6.6 %all-to-all-done.2.back_ref = bf16[384,2,512]{2,1,0:T(2,128)(2,1)} async-done(((bf16[384,2,512]{2,1,0:T(2,128)(2,1)}), bf16[384,2,512]{2,1,0:T(2,128)(2,1)}, u32[]{:S(2)}, u32[]{:S(2)}) %all-to-all-start.2) | async-done | bytes 786464 | tf_op jit(solution)/shard_map/all_to_all | solution.py:242
  205.0 7.4 %all-to-all-start.1 = ((bf16[384,2,1536]{2,1,0:T(2,128)(2,1)}), bf16[384,2,1536]{2,1,0:T(2,128)(2,1)S(1)}, u32[]{:S(2)}, u32[]{:S(2)}) async-start(bf16[384,2,1536]{2,1,0:T(2,128)(2,1)} %copy-done.3), calls=%async_computation.1 | async-start | bytes 4718592 | tf_op jit(solution)/shard_map/all_to_all | solution.py:242
  212.5 2.6 mix.2.refs_0_
  215.1 50.7 %all-to-all-done.1.back_ref = bf16[384,2,1536]{2,1,0:T(2,128)(2,1)S(1)} async-done(((bf16[384,2,1536]{2,1,0:T(2,128)(2,1)}), bf16[384,2,1536]{2,1,0:T(2,128)(2,1)S(1)}, u32[]{:S(2)}, u32[]{:S(2)}) %all-to-all-start.1) | async-done | bytes 2359328 | tf_op jit(solution)/shard_map/all_to_all | solution.py:242
  265.8 3.3 %mix.3 = bf16[384,2048]{1,0:T(8,128)(2,1)} custom-call(bf16[768,384]{1,0:T(8,128)(2,1)S(1)} %hots.1.hot_ref, bf16[384,2,1536]{2,1,0:T(2,128)(2,1)S(1)} %all-to-all-done.1.back_ref, bf16[384,2048]{1,0:T(8,128)(2,1)} %mix.2.refs_0_), custom_call_target="tpu_custom_call", output_to_operand_aliasing={{}: (2, {})} | custom-call | flops 905969664 | bytes 3538944 | tf_op jit(solution)/shard_map/mix/pallas_call | solution.py:197
  (69 shorter events, 16.8 us)
Async XLA Ops:
  7.6 142.2 %all-to-all-start = ((bf16[384,2,2048]{2,1,0:T(2,128)(2,1)}), bf16[384,2,2048]{2,1,0:T(2,128)(2,1)S(1)}, u32[]{:S(2)}, u32[]{:S(2)}) async-start(bf16[384,2,2048]{2,1,0:T(2,128)(2,1)} %copy-done), calls=%async_computation | async-start | bytes 6291456 | tf_op jit(solution)/shard_map/all_to_all | solution.py:237
  23.9 83.4 %copy-start.16 = (bf16[2,512,2048]{2,1,0:T(8,128)(2,1)S(1)}, bf16[2,512,2048]{2,1,0:T(8,128)(2,1)}, u32[]{:S(2)}) copy-start(bf16[2,512,2048]{2,1,0:T(8,128)(2,1)} %param.9) | copy-start | bytes 12582916
  26.5 46.6 %collective-permute-start = (bf16[2048,256]{1,0:T(8,128)(2,1)S(1)}, bf16[2048,256]{1,0:T(8,128)(2,1)S(1)}, u32[]{:S(2)}, u32[]{:S(2)}) collective-permute-start(bf16[2048,256]{1,0:T(8,128)(2,1)S(1)} %get-tuple-element.17), channel_id=1, source_target_pairs={{0,0},{1,1},{2,4},{3,5},{4,2},{5,3},{6,6},{7,7},{8,8},{9,9},{10,12... | collective-permute-start | bytes 3145736 | tf_op jit(solution)/shard_map/ppermute | solution.py:223
  31.7 43.5 %collective-permute-start.1 = (bf16[2048,256]{1,0:T(8,128)(2,1)S(1)}, bf16[2048,256]{1,0:T(8,128)(2,1)S(1)}, u32[]{:S(2)}, u32[]{:S(2)}) collective-permute-start(bf16[2048,256]{1,0:T(8,128)(2,1)S(1)} %get-tuple-element.18), channel_id=1, source_target_pairs={{0,1},{1,0},{2,5},{3,4},{4,3},{5,2},{6,7},{7,6},{8,9},{9,8},{10,13... | collective-permute-start | bytes 3145736 | tf_op jit(solution)/shard_map/ppermute | solution.py:223
  31.8 71.5 %collective-permute-start.2 = (bf16[2048,256]{1,0:T(8,128)(2,1)S(1)}, bf16[2048,256]{1,0:T(8,128)(2,1)S(1)}, u32[]{:S(2)}, u32[]{:S(2)}) collective-permute-start(bf16[2048,256]{1,0:T(8,128)(2,1)S(1)} %get-tuple-element.20), channel_id=1, source_target_pairs={{0,4},{1,5},{2,0},{3,1},{4,6},{5,7},{6,2},{7,3},{8,12},{9,13},{10,... | collective-permute-start | bytes 3145736 | tf_op jit(solution)/shard_map/ppermute | solution.py:223
  31.9 74.9 %collective-permute-start.3 = (bf16[2048,256]{1,0:T(8,128)(2,1)S(1)}, bf16[2048,256]{1,0:T(8,128)(2,1)S(1)}, u32[]{:S(2)}, u32[]{:S(2)}) collective-permute-start(bf16[2048,256]{1,0:T(8,128)(2,1)S(1)} %get-tuple-element.19), channel_id=1, source_target_pairs={{0,5},{1,4},{2,1},{3,0},{4,7},{5,6},{6,3},{7,2},{8,13},{9,12},{10,... | collective-permute-start | bytes 3145736 | tf_op jit(solution)/shard_map/ppermute | solution.py:223
  73.1 56.1 %collective-permute-start.4 = (bf16[2048,256]{1,0:T(8,128)(2,1)S(1)}, bf16[2048,256]{1,0:T(8,128)(2,1)S(1)}, u32[]{:S(2)}, u32[]{:S(2)}) collective-permute-start(bf16[2048,256]{1,0:T(8,128)(2,1)S(1)} %collective-permute-done), channel_id=1, source_target_pairs={{0,4},{4,0},{1,5},{5,1},{2,6},{6,2},{3,7},{7,3},{8,12},{12,8},{9,1... | collective-permute-start | bytes 3145736 | tf_op jit(solution)/shard_map/ppermute | solution.py:224
  75.2 61.2 %collective-permute-start.5 = (bf16[2048,256]{1,0:T(8,128)(2,1)S(1)}, bf16[2048,256]{1,0:T(8,128)(2,1)S(1)}, u32[]{:S(2)}, u32[]{:S(2)}) collective-permute-start(bf16[2048,256]{1,0:T(8,128)(2,1)S(1)} %collective-permute-done.1), channel_id=1, source_target_pairs={{0,4},{4,0},{1,5},{5,1},{2,6},{6,2},{3,7},{7,3},{8,12},{12,8},{9,1... | collective-permute-start | bytes 3145736 | tf_op jit(solution)/shard_map/ppermute | solution.py:224
  103.3 34.0 %collective-permute-start.6 = (bf16[2048,256]{1,0:T(8,128)(2,1)S(1)}, bf16[2048,256]{1,0:T(8,128)(2,1)S(1)}, u32[]{:S(2)}, u32[]{:S(2)}) collective-permute-start(bf16[2048,256]{1,0:T(8,128)(2,1)S(1)} %collective-permute-done.2), channel_id=1, source_target_pairs={{0,4},{4,0},{1,5},{5,1},{2,6},{6,2},{3,7},{7,3},{8,12},{12,8},{9,1... | collective-permute-start | bytes 3145736 | tf_op jit(solution)/shard_map/ppermute | solution.py:224
  106.8 30.7 %collective-permute-start.7 = (bf16[2048,256]{1,0:T(8,128)(2,1)S(1)}, bf16[2048,256]{1,0:T(8,128)(2,1)S(1)}, u32[]{:S(2)}, u32[]{:S(2)}) collective-permute-start(bf16[2048,256]{1,0:T(8,128)(2,1)S(1)} %collective-permute-done.3), channel_id=1, source_target_pairs={{0,4},{4,0},{1,5},{5,1},{2,6},{6,2},{3,7},{7,3},{8,12},{12,8},{9,1... | collective-permute-start | bytes 3145736 | tf_op jit(solution)/shard_map/ppermute | solution.py:224
  107.4 9.4 %collective-permute-start.16 = (bf16[256,512]{1,0:T(8,128)(2,1)S(1)}, bf16[256,512]{1,0:T(8,128)(2,1)S(1)}, u32[]{:S(2)}, u32[]{:S(2)}) collective-permute-start(bf16[256,512]{1,0:T(8,128)(2,1)S(1)} %get-tuple-element.11), channel_id=1, source_target_pairs={{0,0},{1,1},{2,4},{3,5},{4,2},{5,3},{6,6},{7,7},{8,8},{9,9},{10,12... | collective-permute-start | bytes 786440 | tf_op jit(solution)/shard_map/ppermute | solution.py:233
  116.8 7.0 %collective-permute-start.17 = (bf16[256,512]{1,0:T(8,128)(2,1)S(1)}, bf16[256,512]{1,0:T(8,128)(2,1)S(1)}, u32[]{:S(2)}, u32[]{:S(2)}) collective-permute-start(bf16[256,512]{1,0:T(8,128)(2,1)S(1)} %get-tuple-element.10), channel_id=1, source_target_pairs={{0,1},{1,0},{2,5},{3,4},{4,3},{5,2},{6,7},{7,6},{8,9},{9,8},{10,13... | collective-permute-start | bytes 786440 | tf_op jit(solution)/shard_map/ppermute | solution.py:233
  123.9 13.5 %copy-start.4 = (bf16[256,512]{1,0:T(8,128)(2,1)}, bf16[256,512]{1,0:T(8,128)(2,1)S(1)}, u32[]{:S(2)}) copy-start(bf16[256,512]{1,0:T(8,128)(2,1)S(1)} %collective-permute-done.17.refs_1_) | copy-start | bytes 786436
  123.9 3.3 %collective-permute-start.18 = (bf16[256,512]{1,0:T(8,128)(2,1)S(1)}, bf16[256,512]{1,0:T(8,128)(2,1)S(1)}, u32[]{:S(2)}, u32[]{:S(2)}) collective-permute-start(bf16[256,512]{1,0:T(8,128)(2,1)S(1)} %get-tuple-element.12), channel_id=1, source_target_pairs={{0,4},{1,5},{2,0},{3,1},{4,6},{5,7},{6,2},{7,3},{8,12},{9,13},{10,... | collective-permute-start | bytes 786440 | tf_op jit(solution)/shard_map/ppermute | solution.py:233
  127.2 13.0 %copy-start.6 = (bf16[256,512]{1,0:T(8,128)(2,1)}, bf16[256,512]{1,0:T(8,128)(2,1)S(1)}, u32[]{:S(2)}) copy-start(bf16[256,512]{1,0:T(8,128)(2,1)S(1)} %collective-permute-done.18.refs_2_) | copy-start | bytes 786436
  127.2 13.0 %collective-permute-start.19 = (bf16[256,512]{1,0:T(8,128)(2,1)S(1)}, bf16[256,512]{1,0:T(8,128)(2,1)}, u32[]{:S(2)}, u32[]{:S(2)}) collective-permute-start(bf16[256,512]{1,0:T(8,128)(2,1)S(1)} %get-tuple-element.9), channel_id=1, source_target_pairs={{0,5},{1,4},{2,1},{3,0},{4,7},{5,6},{6,3},{7,2},{8,13},{9,12},{10,... | collective-permute-start | bytes 786440 | tf_op jit(solution)/shard_map/ppermute | solution.py:233
  129.2 52.3 %collective-permute-start.8 = (bf16[256,1536]{1,0:T(8,128)(2,1)}, bf16[256,1536]{1,0:T(8,128)(2,1)}, u32[]{:S(2)}, u32[]{:S(2)}) collective-permute-start(bf16[256,1536]{1,0:T(8,128)(2,1)} %get-tuple-element.16), channel_id=1, source_target_pairs={{0,0},{1,1},{2,4},{3,5},{4,2},{5,3},{6,6},{7,7},{8,8},{9,9},{10,12... | collective-permute-start | bytes 2359304 | tf_op jit(solution)/shard_map/ppermute | solution.py:233
  136.3 3.9 %collective-permute-start.20 = (bf16[256,512]{1,0:T(8,128)(2,1)S(1)}, bf16[256,512]{1,0:T(8,128)(2,1)S(1)}, u32[]{:S(2)}, u32[]{:S(2)}) collective-permute-start(bf16[256,512]{1,0:T(8,128)(2,1)S(1)} %collective-permute-done.16.refs_0_), channel_id=1, source_target_pairs={{0,4},{4,0},{1,5},{5,1},{2,6},{6,2},{3,7},{7,3},{8,12},{12,8},{9,1... | collective-permute-start | bytes 786440 | tf_op jit(solution)/shard_map/ppermute | solution.py:234
  137.4 6.2 %collective-permute-start.21 = (bf16[256,512]{1,0:T(8,128)(2,1)S(1)}, bf16[256,512]{1,0:T(8,128)(2,1)S(1)}, u32[]{:S(2)}, u32[]{:S(2)}) collective-permute-start(bf16[256,512]{1,0:T(8,128)(2,1)S(1)} %collective-permute-done.17.refs_1_), channel_id=1, source_target_pairs={{0,4},{4,0},{1,5},{5,1},{2,6},{6,2},{3,7},{7,3},{8,12},{12,8},{9,1... | collective-permute-start | bytes 786440 | tf_op jit(solution)/shard_map/ppermute | solution.py:234
  137.5 7.2 %collective-permute-start.22 = (bf16[256,512]{1,0:T(8,128)(2,1)S(1)}, bf16[256,512]{1,0:T(8,128)(2,1)S(1)}, u32[]{:S(2)}, u32[]{:S(2)}) collective-permute-start(bf16[256,512]{1,0:T(8,128)(2,1)S(1)} %collective-permute-done.18.refs_2_), channel_id=1, source_target_pairs={{0,4},{4,0},{1,5},{5,1},{2,6},{6,2},{3,7},{7,3},{8,12},{12,8},{9,1... | collective-permute-start | bytes 786440 | tf_op jit(solution)/shard_map/ppermute | solution.py:234
  140.2 42.2 %collective-permute-start.9 = (bf16[256,1536]{1,0:T(8,128)(2,1)}, bf16[256,1536]{1,0:T(8,128)(2,1)}, u32[]{:S(2)}, u32[]{:S(2)}) collective-permute-start(bf16[256,1536]{1,0:T(8,128)(2,1)} %get-tuple-element.15), channel_id=1, source_target_pairs={{0,1},{1,0},{2,5},{3,4},{4,3},{5,2},{6,7},{7,6},{8,9},{9,8},{10,13... | collective-permute-start | bytes 2359304 | tf_op jit(solution)/shard_map/ppermute | solution.py:233
  140.9 41.6 %collective-permute-start.10 = (bf16[256,1536]{1,0:T(8,128)(2,1)}, bf16[256,1536]{1,0:T(8,128)(2,1)}, u32[]{:S(2)}, u32[]{:S(2)}) collective-permute-start(bf16[256,1536]{1,0:T(8,128)(2,1)} %get-tuple-element.14), channel_id=1, source_target_pairs={{0,4},{1,5},{2,0},{3,1},{4,6},{5,7},{6,2},{7,3},{8,12},{9,13},{10,... | collective-permute-start | bytes 2359304 | tf_op jit(solution)/shard_map/ppermute | solution.py:233
  144.2 38.7 %collective-permute-start.11 = (bf16[256,1536]{1,0:T(8,128)(2,1)}, bf16[256,1536]{1,0:T(8,128)(2,1)}, u32[]{:S(2)}, u32[]{:S(2)}) collective-permute-start(bf16[256,1536]{1,0:T(8,128)(2,1)} %get-tuple-element.13), channel_id=1, source_target_pairs={{0,5},{1,4},{2,1},{3,0},{4,7},{5,6},{6,3},{7,2},{8,13},{9,12},{10,... | collective-permute-start | bytes 2359304 | tf_op jit(solution)/shard_map/ppermute | solution.py:233
  145.4 15.6 %collective-permute-start.23 = (bf16[256,512]{1,0:T(8,128)(2,1)}, bf16[256,512]{1,0:T(8,128)(2,1)}, u32[]{:S(2)}, u32[]{:S(2)}) collective-permute-start(bf16[256,512]{1,0:T(8,128)(2,1)} %collective-permute-done.19.refs_3_), channel_id=1, source_target_pairs={{0,4},{4,0},{1,5},{5,1},{2,6},{6,2},{3,7},{7,3},{8,12},{12,8},{9,1... | collective-permute-start | bytes 786440 | tf_op jit(solution)/shard_map/ppermute | solution.py:234
  149.8 11.2 %copy-start.11 = (bf16[256,512]{1,0:T(8,128)(2,1)S(1)}, bf16[256,512]{1,0:T(8,128)(2,1)}, u32[]{:S(2)}) copy-start(bf16[256,512]{1,0:T(8,128)(2,1)} %copy-done.10) | copy-start | bytes 786436
  149.8 11.2 %copy-start.13 = (bf16[256,512]{1,0:T(8,128)(2,1)S(1)}, bf16[256,512]{1,0:T(8,128)(2,1)}, u32[]{:S(2)}) copy-start(bf16[256,512]{1,0:T(8,128)(2,1)} %copy-done.12) | copy-start | bytes 786436
  166.4 38.6 %all-to-all-start.2 = ((bf16[384,2,512]{2,1,0:T(2,128)(2,1)}), bf16[384,2,512]{2,1,0:T(2,128)(2,1)}, u32[]{:S(2)}, u32[]{:S(2)}) async-start(bf16[384,2,512]{2,1,0:T(2,128)(2,1)} %down.3), calls=%async_computation.2 | async-start | bytes 1572864 | tf_op jit(solution)/shard_map/all_to_all | solution.py:242
  181.6 3.0 %collective-permute-start.12 = (bf16[256,1536]{1,0:T(8,128)(2,1)}, bf16[256,1536]{1,0:T(8,128)(2,1)S(1)}, u32[]{:S(2)}, u32[]{:S(2)}) collective-permute-start(bf16[256,1536]{1,0:T(8,128)(2,1)} %collective-permute-done.8.refs_0_), channel_id=1, source_target_pairs={{0,4},{4,0},{1,5},{5,1},{2,6},{6,2},{3,7},{7,3},{8,12},{12,8},{9,1... | collective-permute-start | bytes 2359304 | tf_op jit(solution)/shard_map/ppermute | solution.py:234
  182.4 3.2 %collective-permute-start.13 = (bf16[256,1536]{1,0:T(8,128)(2,1)}, bf16[256,1536]{1,0:T(8,128)(2,1)S(1)}, u32[]{:S(2)}, u32[]{:S(2)}) collective-permute-start(bf16[256,1536]{1,0:T(8,128)(2,1)} %collective-permute-done.9.refs_1_), channel_id=1, source_target_pairs={{0,4},{4,0},{1,5},{5,1},{2,6},{6,2},{3,7},{7,3},{8,12},{12,8},{9,1... | collective-permute-start | bytes 2359304 | tf_op jit(solution)/shard_map/ppermute | solution.py:234
  182.5 4.3 %collective-permute-start.14 = (bf16[256,1536]{1,0:T(8,128)(2,1)}, bf16[256,1536]{1,0:T(8,128)(2,1)S(1)}, u32[]{:S(2)}, u32[]{:S(2)}) collective-permute-start(bf16[256,1536]{1,0:T(8,128)(2,1)} %collective-permute-done.10.refs_2_), channel_id=1, source_target_pairs={{0,4},{4,0},{1,5},{5,1},{2,6},{6,2},{3,7},{7,3},{8,12},{12,8},{9,1... | collective-permute-start | bytes 2359304 | tf_op jit(solution)/shard_map/ppermute | solution.py:234
  183.0 5.0 %collective-permute-start.15 = (bf16[256,1536]{1,0:T(8,128)(2,1)}, bf16[256,1536]{1,0:T(8,128)(2,1)S(1)}, u32[]{:S(2)}, u32[]{:S(2)}) collective-permute-start(bf16[256,1536]{1,0:T(8,128)(2,1)} %collective-permute-done.11.refs_3_), channel_id=1, source_target_pairs={{0,4},{4,0},{1,5},{5,1},{2,6},{6,2},{3,7},{7,3},{8,12},{12,8},{9,1... | collective-permute-start | bytes 2359304 | tf_op jit(solution)/shard_map/ppermute | solution.py:234
  205.0 60.9 %all-to-all-start.1 = ((bf16[384,2,1536]{2,1,0:T(2,128)(2,1)}), bf16[384,2,1536]{2,1,0:T(2,128)(2,1)S(1)}, u32[]{:S(2)}, u32[]{:S(2)}) async-start(bf16[384,2,1536]{2,1,0:T(2,128)(2,1)} %copy-done.3), calls=%async_computation.1 | async-start | bytes 4718592 | tf_op jit(solution)/shard_map/all_to_all | solution.py:242
  (12 other events, 44.4 us)

commit v6 on v5

--- a/solution.py
+++ b/solution.py
@@ -14,16 +14,10 @@
 
 
 def weight_route():
-    rounds = []
-    for p in range(4):
-        pairs = []
-        for c in range(2):
-            for y in range(4):
-                bits = y ^ p
-                h, k = bits >> 1, bits & 1
-                pairs.append((c * 4 + y, h * 4 + 2 * c + k))
-        rounds.append(pairs)
-    return rounds
+    return [
+        [(c * 4 + y, (y >> 1) * 4 + 2 * c + ((y ^ p) & 1)) for c in range(2) for y in range(4)]
+        for p in range(2)
+    ]
 
 
 def pack_kernel(slots, ids_ref, table_ref, tok_ref, packed_ref, place_ref):
@@ -212,14 +206,13 @@
     experts = lax.axis_size("g") * lax.axis_size("y")
     tok_rows, width = tokens.shape
     slots = 2 * tok_rows // experts
-    half = w_out.shape[1] // 2
+    quarter = w_out.shape[1]
     y = lax.axis_index("y")
     route = weight_route()
     swap = [(0, 1), (1, 0)]
     own_in = []
-    for p in range(4):
-        h, k = (y ^ p) >> 1, (y ^ p) & 1
-        block = lax.dynamic_slice(w_in, (k, 0, h * half), (1, width, half))[0]
+    for p in range(2):
+        block = lax.dynamic_slice(w_in, ((y ^ p) & 1, 0, 0), (1, width, quarter))[0]
         own_in.append(lax.ppermute(block, ("c", "y"), route[p]))
     other_in = [lax.ppermute(o, "c", swap) for o in own_in]
     own_in = jnp.concatenate(own_in, axis=1)
@@ -227,9 +220,8 @@
     pieces = []
     for low, high in zip(CUTS[:-1], CUTS[1:]):
         own = []
-        for p in range(4):
-            h, k = (y ^ p) >> 1, (y ^ p) & 1
-            block = lax.dynamic_slice(w_out, (k, h * half, low), (1, half, high - low))[0]
+        for p in range(2):
+            block = lax.dynamic_slice(w_out, ((y ^ p) & 1, 0, low), (1, quarter, high - low))[0]
             own.append(lax.ppermute(block, ("c", "y"), route[p]))
         pieces.append(own + [lax.ppermute(o, "c", swap) for o in own])
 

time: 274 us -> 293 us (1.069)
  waiting for transfers between devices: 141 us -> 186 us
  starting transfers between devices: 75.8 us -> 52.7 us
  local copies, waits for them, and re-layouts: 16 us -> 12.5 us
    ppermute x8 -> x4, waiting for transfers between devices: 10.8 us -> 47.9 us  [on_device(): own.append(lax.ppermute(block, ('c', 'y'), route[p]))]
    ppermute x8 -> x4, starting transfers between devices: 17.2 us -> 10.7 us  [on_device(): own.append(lax.ppermute(block, ('c', 'y'), route[p]))]
    ppermute x8 -> x4, starting transfers between devices: 7.4 us -> 1.02 us  [on_device(): pieces.append(own + [lax.ppermute(o, 'c', swap) for o in own])]
    ppermute x4 -> x2, waiting for transfers between devices: 68.5 us -> 74.8 us  [on_device(): own_in.append(lax.ppermute(block, ('c', 'y'), route[p]))]
    all_to_all x2, waiting for transfers between devices: 57.3 us -> 63.6 us  [on_device(): lax.all_to_all(result, ('g', 'y'), split_axis=0, concat_axis=0, tiled=True)]
    ppermute x8 -> x4, waiting for transfers between devices: 4.88 us -> 0.01 us  [on_device(): pieces.append(own + [lax.ppermute(o, 'c', swap) for o in own])]
    ppermute x4 -> x2, starting transfers between devices: 3.98 us -> 0.01 us  [on_device(): other_in = [lax.ppermute(o, 'c', swap) for o in own_in]]
    all_to_all x2, starting transfers between devices: 22.6 us -> 19.4 us  [on_device(): lax.all_to_all(result, ('g', 'y'), split_axis=0, concat_axis=0, tiled=True)]
  transfers between devices with their start and end apart: 27 -> 15, of which waited for: 12 -> 6; matrix products, arithmetic and copies ran while one was open for 3% -> 3% of each run, Pallas kernels for 9% -> 9%
where the time goes in v6:
time: 293 us; the launch traced here: 288 us
  waiting for transfers between devices  186 us (63%)
  starting transfers between devices  52.7 us (18%)
  Pallas kernels  31.6 us (11%)
  local copies, waits for them, and re-layouts  12.5 us (4%)
  other arithmetic  5.04 us (2%)
    ppermute x2, waiting for transfers between devices, on_device(): own_in.append(lax.ppermute(block, ('c', 'y'), route[p]))  74.8 us
    all_to_all x2, waiting for transfers between devices, on_device(): lax.all_to_all(result, ('g', 'y'), split_axis=0, concat_axis=0, tiled=True)  63.6 us
    ppermute x4, waiting for transfers between devices, on_device(): own.append(lax.ppermute(block, ('c', 'y'), route[p]))  47.9 us
    all_to_all x2, starting transfers between devices, on_device(): lax.all_to_all(result, ('g', 'y'), split_axis=0, concat_axis=0, tiled=True)  19.4 us
    all_to_all x1, starting transfers between devices, on_device(): lax.all_to_all(packed, ('g', 'y'), split_axis=0, concat_axis=0, tiled=True)  16.3 us
    pallas_call x2, Pallas kernels, down(): pl.pallas_call(functools.partial(down_kernel, n), grid=(cols // block,),...  11.6 us
    pallas_call x1, Pallas kernels, up(): pl.pallas_call(up_kernel, grid=(2 * half,), in_specs=[pl.BlockSpec(memory...  11 us
    ppermute x4, starting transfers between devices, on_device(): own.append(lax.ppermute(block, ('c', 'y'), route[p]))  10.7 us
  transfers between devices with their start and end apart: 15, of which 6 were waited for; matrix products, arithmetic and copies ran while one was open for 3% of the time, Pallas kernels for 9%

profile of v6, /device:TPU:1, one launch (start us, length us, event | category | flops | bytes accessed | tf_op | source)
XLA Modules:
  0.0 288.4 jit_solution(10663687325698364266)
XLA Ops:
  0.0 0.7 reshape.6.ids_ref
  0.7 1.4 copy-done.4
  2.1 0.8 copy-done.5
  2.9 3.1 %pack.1 = (bf16[384,2,2048]{2,1,0:T(2,128)(2,1)S(1)}, s32[1,384]{1,0:T(1,128)S(1)}) custom-call(s32[1,384]{1,0:T(1,128)S(1)} %reshape.6.ids_ref, s32[64,128]{1,0:T(8,128)S(1)} %bitcast.13, bf16[384,2048]{1,0:T(8,128)(2,1)S(1)} %copy-done.4), custom_call_target="tpu_custom_call" | custom-call | flops 1207959552 | bytes 6291456 | tf_op jit(solution)/shard_map/pack/pallas_call | solution.py:57
  5.9 1.7 copy-done
  7.6 16.3 %all-to-all-start = ((bf16[384,2,2048]{2,1,0:T(2,128)(2,1)}), bf16[384,2,2048]{2,1,0:T(2,128)(2,1)S(1)}, u32[]{:S(2)}, u32[]{:S(2)}) async-start(bf16[384,2,2048]{2,1,0:T(2,128)(2,1)} %copy-done), calls=%async_computation | async-start | bytes 6291456 | tf_op jit(solution)/shard_map/all_to_all | solution.py:229
  24.0 2.7 dynamic-slice_bitcast_fusion.1
  26.6 5.1 %collective-permute-start = (bf16[2048,512]{1,0:T(8,128)(2,1)S(1)}, bf16[2048,512]{1,0:T(8,128)(2,1)S(1)}, u32[]{:S(2)}, u32[]{:S(2)}) collective-permute-start(bf16[2048,512]{1,0:T(8,128)(2,1)S(1)} %get-tuple-element.13), channel_id=1, source_target_pairs={{0,0},{1,1},{2,4},{3,5},{4,2},{5,3},{6,6},{7,7},{8,8},{9,9},{10,12... | collective-permute-start | bytes 6291464 | tf_op jit(solution)/shard_map/ppermute | solution.py:216
  31.9 74.3 %collective-permute-done = bf16[2048,512]{1,0:T(8,128)(2,1)S(1)} collective-permute-done((bf16[2048,512]{1,0:T(8,128)(2,1)S(1)}, bf16[2048,512]{1,0:T(8,128)(2,1)S(1)}, u32[]{:S(2)}, u32[]{:S(2)}) %collective-permute-start) | collective-permute-done | bytes 2097184 | tf_op jit(solution)/shard_map/ppermute | solution.py:216
  106.2 0.5 collective-permute-done.1
  107.0 3.1 %collective-permute-start.4 = (bf16[512,1536]{1,0:T(8,128)(2,1)S(1)}, bf16[512,1536]{1,0:T(8,128)(2,1)}, u32[]{:S(2)}, u32[]{:S(2)}) collective-permute-start(bf16[512,1536]{1,0:T(8,128)(2,1)S(1)} %get-tuple-element.12), channel_id=1, source_target_pairs={{0,0},{1,1},{2,4},{3,5},{4,2},{5,3},{6,6},{7,7},{8,8},{9,9},{10,12... | collective-permute-start | bytes 4718600 | tf_op jit(solution)/shard_map/ppermute | solution.py:225
  110.1 2.1 collective-permute-start.5
  112.3 3.5 %collective-permute-start.8 = (bf16[512,512]{1,0:T(8,128)(2,1)S(1)}, bf16[512,512]{1,0:T(8,128)(2,1)}, u32[]{:S(2)}, u32[]{:S(2)}) collective-permute-start(bf16[512,512]{1,0:T(8,128)(2,1)S(1)} %get-tuple-element.10), channel_id=1, source_target_pairs={{0,0},{1,1},{2,4},{3,5},{4,2},{5,3},{6,6},{7,7},{8,8},{9,9},{10,12... | collective-permute-start | bytes 1572872 | tf_op jit(solution)/shard_map/ppermute | solution.py:225
  115.8 42.4 %collective-permute-done.8.refs_0_ = bf16[512,512]{1,0:T(8,128)(2,1)} collective-permute-done((bf16[512,512]{1,0:T(8,128)(2,1)S(1)}, bf16[512,512]{1,0:T(8,128)(2,1)}, u32[]{:S(2)}, u32[]{:S(2)}) %collective-permute-start.8) | collective-permute-done | bytes 524320 | tf_op jit(solution)/shard_map/ppermute | solution.py:225
  158.3 2.0 collective-permute-start.9
  160.3 2.5 pad_maximum_fusion.own_ref
  162.8 5.4 %collective-permute-done.9.refs_1_ = bf16[512,512]{1,0:T(8,128)(2,1)} collective-permute-done((bf16[512,512]{1,0:T(8,128)(2,1)S(1)}, bf16[512,512]{1,0:T(8,128)(2,1)}, u32[]{:S(2)}, u32[]{:S(2)}) %collective-permute-start.9) | collective-permute-done | bytes 524320 | tf_op jit(solution)/shard_map/ppermute | solution.py:225
  168.2 0.5 collective-permute-start.11
  168.8 0.4 collective-permute-start.7
  169.2 2.6 pad_maximum_fusion.1.other_ref
  171.8 11.0 %up.1.hidden_ref = bf16[768,2048]{1,0:T(8,128)(2,1)S(1)} custom-call(bf16[384,2,2048]{2,1,0:T(2,128)(2,1)S(1)} %all-to-all-done.x_ref, bf16[2048,1024]{1,0:T(8,128)(2,1)} %pad_maximum_fusion.own_ref, bf16[2048,1024]{1,0:T(8,128)(2,1)} %pad_maximum_fusion.1.other_ref), custom_call_target="tpu_custom_call" | custom-call | flops 6442450944 | bytes 16777216 | tf_op jit(solution)/shard_map/up/pallas_call | solution.py:108
  182.8 4.2 %down.3 = bf16[384,2,512]{2,1,0:T(2,128)(2,1)} custom-call(bf16[768,2048]{1,0:T(8,128)(2,1)S(1)} %up.1.hidden_ref, bf16[512,512]{1,0:T(8,128)(2,1)} %collective-permute-done.8.refs_0_, bf16[512,512]{1,0:T(8,128)(2,1)} %collective-permute-done.9.refs_1_, bf16[512,512]{1,0:T(8,128)(2,1)} %collective-permute-done.10.refs_2_, ...), custom_call_target="tpu_custom_call" | custom-call | flops 1610612736 | bytes 6029312 | tf_op jit(solution)/shard_map/down/pallas_call | solution.py:139
  187.0 1.6 copy-done.1
  188.6 12.2 %all-to-all-start.2 = ((bf16[384,2,512]{2,1,0:T(2,128)(2,1)}), bf16[384,2,512]{2,1,0:T(2,128)(2,1)}, u32[]{:S(2)}, u32[]{:S(2)}) async-start(bf16[384,2,512]{2,1,0:T(2,128)(2,1)} %down.3), calls=%async_computation.2 | async-start | bytes 1572864 | tf_op jit(solution)/shard_map/all_to_all | solution.py:234
  200.9 1.9 copy-done.2
  202.7 7.4 %down.2 = bf16[384,2,1536]{2,1,0:T(2,128)(2,1)S(1)} custom-call(bf16[768,2048]{1,0:T(8,128)(2,1)S(1)} %copy-done.2, bf16[512,1536]{1,0:T(8,128)(2,1)} %collective-permute-done.4.refs_0_, bf16[512,1536]{1,0:T(8,128)(2,1)} %collective-permute-done.5.refs_1_, bf16[512,1536]{1,0:T(8,128)(2,1)} %collective-permute-done.6.refs_2_, ...), custom_call_target="tpu_custom_call" | custom-call | flops 4831838208 | bytes 11796480 | tf_op jit(solution)/shard_map/down/pallas_call | solution.py:139
  210.2 1.4 copy-done.3
  211.6 12.8 %all-to-all-done.2.back_ref = bf16[384,2,512]{2,1,0:T(2,128)(2,1)} async-done(((bf16[384,2,512]{2,1,0:T(2,128)(2,1)}), bf16[384,2,512]{2,1,0:T(2,128)(2,1)}, u32[]{:S(2)}, u32[]{:S(2)}) %all-to-all-start.2) | async-done | bytes 786464 | tf_op jit(solution)/shard_map/all_to_all | solution.py:234
  224.4 7.2 %all-to-all-start.1 = ((bf16[384,2,1536]{2,1,0:T(2,128)(2,1)}), bf16[384,2,1536]{2,1,0:T(2,128)(2,1)S(1)}, u32[]{:S(2)}, u32[]{:S(2)}) async-start(bf16[384,2,1536]{2,1,0:T(2,128)(2,1)} %copy-done.3), calls=%async_computation.1 | async-start | bytes 4718592 | tf_op jit(solution)/shard_map/all_to_all | solution.py:234
  231.8 2.6 mix.2.refs_0_
  234.4 50.7 %all-to-all-done.1.back_ref = bf16[384,2,1536]{2,1,0:T(2,128)(2,1)S(1)} async-done(((bf16[384,2,1536]{2,1,0:T(2,128)(2,1)}), bf16[384,2,1536]{2,1,0:T(2,128)(2,1)S(1)}, u32[]{:S(2)}, u32[]{:S(2)}) %all-to-all-start.1) | async-done | bytes 2359328 | tf_op jit(solution)/shard_map/all_to_all | solution.py:234
  285.1 3.3 %mix.3 = bf16[384,2048]{1,0:T(8,128)(2,1)} custom-call(bf16[768,384]{1,0:T(8,128)(2,1)S(1)} %hots.1.hot_ref, bf16[384,2,1536]{2,1,0:T(2,128)(2,1)S(1)} %all-to-all-done.1.back_ref, bf16[384,2048]{1,0:T(8,128)(2,1)} %mix.2.refs_0_), custom_call_target="tpu_custom_call", output_to_operand_aliasing={{}: (2, {})} | custom-call | flops 905969664 | bytes 3538944 | tf_op jit(solution)/shard_map/mix/pallas_call | solution.py:191
  (25 shorter events, 0.8 us)
Async XLA Ops:
  0.7 1.4 copy-start.4
  2.1 0.8 copy-start.5
  5.9 1.7 copy-start
  7.6 164.2 %all-to-all-start = ((bf16[384,2,2048]{2,1,0:T(2,128)(2,1)}), bf16[384,2,2048]{2,1,0:T(2,128)(2,1)S(1)}, u32[]{:S(2)}, u32[]{:S(2)}) async-start(bf16[384,2,2048]{2,1,0:T(2,128)(2,1)} %copy-done), calls=%async_computation | async-start | bytes 6291456 | tf_op jit(solution)/shard_map/all_to_all | solution.py:229
  24.0 82.7 %copy-start.6 = (bf16[2,512,2048]{2,1,0:T(8,128)(2,1)S(1)}, bf16[2,512,2048]{2,1,0:T(8,128)(2,1)}, u32[]{:S(2)}) copy-start(bf16[2,512,2048]{2,1,0:T(8,128)(2,1)} %param.9) | copy-start | bytes 12582916
  26.6 79.5 %collective-permute-start = (bf16[2048,512]{1,0:T(8,128)(2,1)S(1)}, bf16[2048,512]{1,0:T(8,128)(2,1)S(1)}, u32[]{:S(2)}, u32[]{:S(2)}) collective-permute-start(bf16[2048,512]{1,0:T(8,128)(2,1)S(1)} %get-tuple-element.13), channel_id=1, source_target_pairs={{0,0},{1,1},{2,4},{3,5},{4,2},{5,3},{6,6},{7,7},{8,8},{9,9},{10,12... | collective-permute-start | bytes 6291464 | tf_op jit(solution)/shard_map/ppermute | solution.py:216
  31.8 74.9 %collective-permute-start.1 = (bf16[2048,512]{1,0:T(8,128)(2,1)S(1)}, bf16[2048,512]{1,0:T(8,128)(2,1)S(1)}, u32[]{:S(2)}, u32[]{:S(2)}) collective-permute-start(bf16[2048,512]{1,0:T(8,128)(2,1)S(1)} %get-tuple-element.14), channel_id=1, source_target_pairs={{0,1},{1,0},{2,5},{3,4},{4,3},{5,2},{6,7},{7,6},{8,9},{9,8},{10,13... | collective-permute-start | bytes 6291464 | tf_op jit(solution)/shard_map/ppermute | solution.py:216
  106.2 62.6 %collective-permute-start.2 = (bf16[2048,512]{1,0:T(8,128)(2,1)S(1)}, bf16[2048,512]{1,0:T(8,128)(2,1)S(1)}, u32[]{:S(2)}, u32[]{:S(2)}) collective-permute-start(bf16[2048,512]{1,0:T(8,128)(2,1)S(1)} %collective-permute-done), channel_id=1, source_target_pairs={{0,4},{4,0},{1,5},{5,1},{2,6},{6,2},{3,7},{7,3},{8,12},{12,8},{9,1... | collective-permute-start | bytes 6291464 | tf_op jit(solution)/shard_map/ppermute | solution.py:217
  106.7 62.5 %collective-permute-start.3 = (bf16[2048,512]{1,0:T(8,128)(2,1)S(1)}, bf16[2048,512]{1,0:T(8,128)(2,1)S(1)}, u32[]{:S(2)}, u32[]{:S(2)}) collective-permute-start(bf16[2048,512]{1,0:T(8,128)(2,1)S(1)} %collective-permute-done.1), channel_id=1, source_target_pairs={{0,4},{4,0},{1,5},{5,1},{2,6},{6,2},{3,7},{7,3},{8,12},{12,8},{9,1... | collective-permute-start | bytes 6291464 | tf_op jit(solution)/shard_map/ppermute | solution.py:217
  107.0 61.2 %collective-permute-start.4 = (bf16[512,1536]{1,0:T(8,128)(2,1)S(1)}, bf16[512,1536]{1,0:T(8,128)(2,1)}, u32[]{:S(2)}, u32[]{:S(2)}) collective-permute-start(bf16[512,1536]{1,0:T(8,128)(2,1)S(1)} %get-tuple-element.12), channel_id=1, source_target_pairs={{0,0},{1,1},{2,4},{3,5},{4,2},{5,3},{6,6},{7,7},{8,8},{9,9},{10,12... | collective-permute-start | bytes 4718600 | tf_op jit(solution)/shard_map/ppermute | solution.py:225
  110.1 58.6 %collective-permute-start.5 = (bf16[512,1536]{1,0:T(8,128)(2,1)S(1)}, bf16[512,1536]{1,0:T(8,128)(2,1)}, u32[]{:S(2)}, u32[]{:S(2)}) collective-permute-start(bf16[512,1536]{1,0:T(8,128)(2,1)S(1)} %get-tuple-element.11), channel_id=1, source_target_pairs={{0,1},{1,0},{2,5},{3,4},{4,3},{5,2},{6,7},{7,6},{8,9},{9,8},{10,13... | collective-permute-start | bytes 4718600 | tf_op jit(solution)/shard_map/ppermute | solution.py:225
  112.3 45.9 %collective-permute-start.8 = (bf16[512,512]{1,0:T(8,128)(2,1)S(1)}, bf16[512,512]{1,0:T(8,128)(2,1)}, u32[]{:S(2)}, u32[]{:S(2)}) collective-permute-start(bf16[512,512]{1,0:T(8,128)(2,1)S(1)} %get-tuple-element.10), channel_id=1, source_target_pairs={{0,0},{1,1},{2,4},{3,5},{4,2},{5,3},{6,6},{7,7},{8,8},{9,9},{10,12... | collective-permute-start | bytes 1572872 | tf_op jit(solution)/shard_map/ppermute | solution.py:225
  158.3 9.9 %collective-permute-start.9 = (bf16[512,512]{1,0:T(8,128)(2,1)S(1)}, bf16[512,512]{1,0:T(8,128)(2,1)}, u32[]{:S(2)}, u32[]{:S(2)}) collective-permute-start(bf16[512,512]{1,0:T(8,128)(2,1)S(1)} %get-tuple-element.9), channel_id=1, source_target_pairs={{0,1},{1,0},{2,5},{3,4},{4,3},{5,2},{6,7},{7,6},{8,9},{9,8},{10,13... | collective-permute-start | bytes 1572872 | tf_op jit(solution)/shard_map/ppermute | solution.py:225
  168.2 14.6 %collective-permute-start.10 = (bf16[512,512]{1,0:T(8,128)(2,1)}, bf16[512,512]{1,0:T(8,128)(2,1)}, u32[]{:S(2)}, u32[]{:S(2)}) collective-permute-start(bf16[512,512]{1,0:T(8,128)(2,1)} %collective-permute-done.8.refs_0_), channel_id=1, source_target_pairs={{0,4},{4,0},{1,5},{5,1},{2,6},{6,2},{3,7},{7,3},{8,12},{12,8},{9,1... | collective-permute-start | bytes 1572872 | tf_op jit(solution)/shard_map/ppermute | solution.py:226
  168.2 14.6 %collective-permute-start.11 = (bf16[512,512]{1,0:T(8,128)(2,1)}, bf16[512,512]{1,0:T(8,128)(2,1)}, u32[]{:S(2)}, u32[]{:S(2)}) collective-permute-start(bf16[512,512]{1,0:T(8,128)(2,1)} %collective-permute-done.9.refs_1_), channel_id=1, source_target_pairs={{0,4},{4,0},{1,5},{5,1},{2,6},{6,2},{3,7},{7,3},{8,12},{12,8},{9,1... | collective-permute-start | bytes 1572872 | tf_op jit(solution)/shard_map/ppermute | solution.py:226
  168.7 32.1 %collective-permute-start.6 = (bf16[512,1536]{1,0:T(8,128)(2,1)}, bf16[512,1536]{1,0:T(8,128)(2,1)}, u32[]{:S(2)}, u32[]{:S(2)}) collective-permute-start(bf16[512,1536]{1,0:T(8,128)(2,1)} %collective-permute-done.4.refs_0_), channel_id=1, source_target_pairs={{0,4},{4,0},{1,5},{5,1},{2,6},{6,2},{3,7},{7,3},{8,12},{12,8},{9,1... | collective-permute-start | bytes 4718600 | tf_op jit(solution)/shard_map/ppermute | solution.py:226
  168.8 32.1 %collective-permute-start.7 = (bf16[512,1536]{1,0:T(8,128)(2,1)}, bf16[512,1536]{1,0:T(8,128)(2,1)}, u32[]{:S(2)}, u32[]{:S(2)}) collective-permute-start(bf16[512,1536]{1,0:T(8,128)(2,1)} %collective-permute-done.5.refs_1_), channel_id=1, source_target_pairs={{0,4},{4,0},{1,5},{5,1},{2,6},{6,2},{3,7},{7,3},{8,12},{12,8},{9,1... | collective-permute-start | bytes 4718600 | tf_op jit(solution)/shard_map/ppermute | solution.py:226
  187.0 1.6 copy-start.1
  188.6 35.8 %all-to-all-start.2 = ((bf16[384,2,512]{2,1,0:T(2,128)(2,1)}), bf16[384,2,512]{2,1,0:T(2,128)(2,1)}, u32[]{:S(2)}, u32[]{:S(2)}) async-start(bf16[384,2,512]{2,1,0:T(2,128)(2,1)} %down.3), calls=%async_computation.2 | async-start | bytes 1572864 | tf_op jit(solution)/shard_map/all_to_all | solution.py:234
  200.9 1.9 copy-start.2
  210.1 1.4 copy-start.3
  224.4 60.7 %all-to-all-start.1 = ((bf16[384,2,1536]{2,1,0:T(2,128)(2,1)}), bf16[384,2,1536]{2,1,0:T(2,128)(2,1)S(1)}, u32[]{:S(2)}, u32[]{:S(2)}) async-start(bf16[384,2,1536]{2,1,0:T(2,128)(2,1)} %copy-done.3), calls=%async_computation.1 | async-start | bytes 4718592 | tf_op jit(solution)/shard_map/all_to_all | solution.py:234
